TPU v7x, 768 devices: a whole 4x8x12 slice. The times are simulated.
768 devices in a mesh: ep: 32 (over y, x), dp: 2 (over core), tp: 12 (over z).
Axes of the slice: x: 4, y: 8, z: 12, core: 2. Of those that a mesh axis runs over, the one named last changes fastest.
Arguments:
- tokens: bfloat16 [1536, 7168], P(('ep', 'dp')), may hold values from -6 to 6
- expert_ids: int32 [1536, 8], P(('ep', 'dp')), may hold values from 0 to 31, all different within a row; in each aligned block of 24 rows (0 to 23, 24 to 47, ...) at most 8 rows name the same one
- route_weight: float32 [1536, 8], P(('ep', 'dp')), may hold values from 0.1 to 0.6
- gate_weight: bfloat16 [32, 7168, 1536], P('ep', None, 'tp'), may hold values from -0.0625 to 0.0625
- up_weight: bfloat16 [32, 7168, 1536], P('ep', None, 'tp'), may hold values from -0.0625 to 0.0625
- down_weight: bfloat16 [32, 1536, 7168], P('ep', 'tp'), may hold values from -0.15625 to 0.15625
Outputs:
- moe_out: bfloat16 [1536, 7168], P(('ep', 'dp', 'tp'))
Inputs may be any that keep to these rules, and one draw needn't show every extreme that they name: `expert_ids`: each row names 8 different experts. In every aligned block of 24 rows no expert is named by more than 8 rows, a bound that some block reaches.
All inputs are finite; a program needn't handle non-finite values.
Results may differ from a plain program's by a relative error of at most 0.0049.
Values may be sent and summed in bfloat16 or wider, within the bound.
No kernel may reach another device: no remote copies, remote signals or barrier semaphores. Data moves between devices by JAX's collectives and lax.ppermute only.
A program may use at most 64 MiB of HBM per device.

v0:
```python
from functools import partial

import jax
import jax.numpy as jnp
from jax import lax
from jax.sharding import PartitionSpec as P

TOP = 8
EXPERTS = 32
MOST = 8


def in_blocks(array, dim, devices):
    lengths = array.shape
    pieces = array.reshape(*lengths[:dim], devices, lengths[dim] // devices, *lengths[dim + 1 :])
    return jnp.moveaxis(pieces, dim, 0)


def sum_at_owner(array, axis, dim):
    pieces = in_blocks(array, dim, lax.axis_size(axis))
    arrived = lax.all_to_all(pieces, axis, split_axis=0, concat_axis=0, tiled=True)
    return arrived.sum(axis=0)


def expert_block(received, gate_weight, up_weight, down_weight):
    ep_size = lax.axis_size("ep")
    local_count = gate_weight.shape[0]
    slot_count = received.shape[1]
    width = received.shape[2]
    shaped = received.reshape(ep_size, local_count, slot_count, width)
    gate_proj = jnp.einsum(
        "sxmd,xdf->sxmf", shaped, gate_weight, preferred_element_type=jnp.float32
    )
    up_proj = jnp.einsum("sxmd,xdf->sxmf", shaped, up_weight, preferred_element_type=jnp.float32)
    hidden = (jax.nn.silu(gate_proj) * up_proj).astype(jnp.bfloat16)
    partial_rows = jnp.einsum(
        "sxmf,xfd->sxmd", hidden, down_weight, preferred_element_type=jnp.float32
    )
    partial_rows = partial_rows.reshape(ep_size * local_count, slot_count, width)
    return lax.all_to_all(partial_rows, "ep", split_axis=0, concat_axis=0, tiled=True)


def build_rows(source, per_token):
    width = source.shape[1]
    dispatch = jnp.any(per_token, 1).astype(jnp.bfloat16)
    outgoing = jnp.einsum("tp,td->pd", dispatch, source, preferred_element_type=jnp.float32).astype(
        jnp.bfloat16
    )
    return outgoing.reshape(EXPERTS, MOST, width)


def combine_rows(returned, per_token, route_weight):
    weight_table = jnp.sum(per_token.astype(jnp.float32) * route_weight[:, :, None], 1)
    combined = jnp.dot(weight_table, returned, precision=lax.Precision.HIGHEST)
    return combined


def per_device(tokens, expert_ids, route_weight, gate_weight, up_weight, down_weight):
    rows_here = tokens.shape[0]
    width = tokens.shape[1]
    capacity = EXPERTS * MOST
    chosen = expert_ids.reshape(-1)
    onehot = (chosen[:, None] == jnp.arange(EXPERTS, dtype=jnp.int32)[None, :]).astype(jnp.int32)
    earlier = jnp.cumsum(onehot, 0) - onehot
    slot_index = jnp.sum(earlier * onehot, 1)
    position = chosen * MOST + slot_index
    matches = position[:, None] == jnp.arange(capacity, dtype=jnp.int32)[None, :]
    per_token = matches.reshape(rows_here, TOP, capacity)
    outgoing = build_rows(tokens, per_token)
    worker = partial(
        expert_block, gate_weight=gate_weight, up_weight=up_weight, down_weight=down_weight
    )
    returned = worker(lax.all_to_all(outgoing, "ep", split_axis=0, concat_axis=0, tiled=True))
    returned = returned.reshape(capacity, width)
    combined = combine_rows(returned, per_token, route_weight)
    summed = sum_at_owner(combined, "tp", 0)
    return summed.astype(jnp.bfloat16)


def solution(mesh):
    in_specs = (
        P(("ep", "dp"), None),
        P(("ep", "dp"), None),
        P(("ep", "dp"), None),
        P("ep", None, "tp"),
        P("ep", None, "tp"),
        P("ep", "tp", None),
    )
    out_specs = P(("ep", "dp", "tp"), None)
    return jax.shard_map(
        per_device, mesh=mesh, in_specs=in_specs, out_specs=out_specs, check_vma=False
    )
```

profile of v0, /device:TPU:30, one launch (start us, length us, event | category | flops | bytes accessed | tf_op | source)
XLA Modules:
  0.0 335.0 jit_solution(15363505203994296649)
XLA Ops:
  0.0 0.0 copy-start
  0.0 0.9 copy.22
  0.9 0.1 eq.36
  1.0 0.6 reduce-window.6
  1.6 0.2 slice_reduce_fusion
  1.8 0.1 bitcast_bitcast_fusion
  1.9 0.1 reduce_sum.30
  2.1 0.1 fusion.26
  2.2 2.1 fusion
  4.3 0.0 copy-start.2
  4.4 91.5 %all_to_all.15 = bf16[32,8,7168]{2,1,0:T(8,128)(2,1)S(1)} all-to-all(bf16[32,8,7168]{2,1,0:T(8,128)(2,1)S(1)} %fusion), channel_id=1, replica_groups=mesh['ep'=32,'dp'=2,'tp'=12] {'ep'}, dimensions={0} | all-to-all | bytes 7340032 | tf_op jit(solution)/shard_map/all_to_all | solution.py:73
  95.9 0.0 copy-start.1
  95.9 1.9 copy-done.1
  97.8 0.0 copy-done.2
  97.8 1.1 fusion.9
  98.9 0.0 copy-done
  98.9 9.6 %fusion.3 = f32[32,8,7168]{2,1,0:T(8,128)} fusion(bf16[1,128,7168]{2,1,0:T(8,128)(2,1)S(1)} %copy-done, bf16[32,8,7168]{2,1,0:T(8,128)(2,1)} %copy-done.1, bf16[1,7168,128]{2,1,0:T(8,128)(2,1)} %param.10, f32[32,1,8,128]{3,2,0,1:T(8,128)S(1)} %fusion.9), kind=kOutput, calls=%fused_computation.4 | convolution fusion | flops 939720704 | bytes 14811136 | tf_op jit(solution)/shard_map/sxmf,xfd->sxmd/dot_general | solution.py:36
  108.4 0.0 copy-start.3
  108.4 8.7 %all-to-all-start.1 = ((f32[32,8,7168]{2,1,0:T(8,128)}), f32[32,8,7168]{2,1,0:T(8,128)}, u32[]{:S(2)}, u32[]{:S(2)}) async-start(f32[32,8,7168]{2,1,0:T(8,128)} %fusion.3), calls=%async_computation.1 | async-start | bytes 14680064 | tf_op jit(solution)/shard_map/all_to_all | solution.py:40
  117.2 0.0 copy-done.3
  117.2 0.1 copy.26
  117.2 0.1 select_reduce_fusion
  117.4 157.2 %all-to-all-done.1 = f32[32,8,7168]{2,1,0:T(8,128)} async-done(((f32[32,8,7168]{2,1,0:T(8,128)}), f32[32,8,7168]{2,1,0:T(8,128)}, u32[]{:S(2)}, u32[]{:S(2)}) %all-to-all-start.1) | async-done | bytes 7340064 | tf_op jit(solution)/shard_map/all_to_all | solution.py:40
  274.6 6.4 %fusion.1 = f32[12,2,7168]{2,0,1:T(8,128)S(1)} fusion(f32[32,8,7168]{2,1,0:T(8,128)} %all-to-all-done.1, f32[12,2,256]{2,1,0:T(2,128)S(1)} %dot_general.25), kind=kOutput, calls=%fused_computation.2 | convolution fusion | flops 528482304 | bytes 8052736 | tf_op jit(solution)/shard_map/dot_general | solution.py:54
  281.1 0.5 copy.28
  281.6 52.6 %all_to_all.16 = f32[12,2,7168]{2,1,0:T(2,128)S(1)} all-to-all(f32[12,2,7168]{2,1,0:T(2,128)S(1)} %copy.28), channel_id=1, replica_groups=mesh['ep'=32,'dp'=2,'tp'=12] {'tp'}, dimensions={0} | all-to-all | bytes 1376256 | tf_op jit(solution)/shard_map/all_to_all | solution.py:21
  334.2 0.8 reduce_sum.32
  (7 shorter events, 0.1 us)
Async XLA Ops:
  0.0 98.9 %copy-start = (bf16[1,128,7168]{2,1,0:T(8,128)(2,1)S(1)}, bf16[1,128,7168]{2,1,0:T(8,128)(2,1)}, u32[]{:S(2)}) copy-start(bf16[1,128,7168]{2,1,0:T(8,128)(2,1)} %param.11) | copy-start | bytes 5505028
  4.3 93.4 %copy-start.2 = (bf16[1,7168,128]{2,1,0:T(8,128)(2,1)S(1)}, bf16[1,7168,128]{2,1,0:T(8,128)(2,1)}, u32[]{:S(2)}) copy-start(bf16[1,7168,128]{2,1,0:T(8,128)(2,1)} %param.9) | copy-start | bytes 5505028
  95.9 1.9 copy-start.1
  108.4 8.7 %copy-start.3 = (f32[24,8]{0,1:T(8,128)S(1)}, f32[24,8]{0,1:T(8,128)}, u32[]{:S(2)}) copy-start(f32[24,8]{0,1:T(8,128)} %param.8) | copy-start | bytes 2308
  108.4 166.2 %all-to-all-start.1 = ((f32[32,8,7168]{2,1,0:T(8,128)}), f32[32,8,7168]{2,1,0:T(8,128)}, u32[]{:S(2)}, u32[]{:S(2)}) async-start(f32[32,8,7168]{2,1,0:T(8,128)} %fusion.3), calls=%async_computation.1 | async-start | bytes 14680064 | tf_op jit(solution)/shard_map/all_to_all | solution.py:40
where the time goes:
time: 335 us
  waiting for transfers between devices  157 us (47%)
  blocking collectives  144 us (43%)
  matrix products  19.2 us (6%)
  starting transfers between devices  8.7 us (3%)
  local copies, waits for them, and re-layouts  3.79 us (1%)
    all_to_all x1, waiting for transfers between devices, expert_block(): lax.all_to_all(partial_rows, 'ep', split_axis=0, concat_axis=0, tiled=True)  157 us
    all_to_all x1, blocking collectives, per_device(): lax.all_to_all(outgoing, 'ep', split_axis=0, concat_axis=0, tiled=True)  91.5 us
    all_to_all x1, blocking collectives, sum_at_owner(): lax.all_to_all(pieces, axis, split_axis=0, concat_axis=0, tiled=True)  52.6 us
    dot_general x1, matrix products, expert_block(): jnp.einsum('sxmf,xfd->sxmd', hidden, down_weight, preferred_element_type=...  9.56 us
    all_to_all x1, starting transfers between devices, expert_block(): lax.all_to_all(partial_rows, 'ep', split_axis=0, concat_axis=0, tiled=True)  8.7 us
  transfers between devices with their start and end apart: 1, of which 1 were waited for; matrix products, arithmetic and copies ran while one was open for 0% of the time, Pallas kernels for 0%

commit v1 on v0

v1 whole, which is shorter than its diff:
```python
import jax
import jax.numpy as jnp
from jax import lax
from jax.sharding import PartitionSpec as P

TOP = 8
EXPERTS = 32
MOST = 8
LANES = 128
PARTS = 3


def ring(step):
    size = lax.axis_size("tp")
    return [(i, (i + step) % size) for i in range(size)]


def piece_width(width):
    tiles = -(-width // LANES)
    return -(-tiles // PARTS) * LANES


def piece_start(index, width):
    piece = piece_width(width)
    return jnp.minimum(lax.rem(index, PARTS) * piece, width - piece)


def positions(expert_ids):
    chosen = expert_ids.reshape(-1)
    onehot = (chosen[:, None] == jnp.arange(EXPERTS, dtype=jnp.int32)[None, :]).astype(jnp.int32)
    earlier = jnp.cumsum(onehot, 0) - onehot
    slot_index = jnp.sum(earlier * onehot, 1)
    position = chosen * MOST + slot_index
    return position.reshape(expert_ids.shape)


def gate_up_piece(gate_weight, up_weight, index):
    width = gate_weight.shape[1]
    start, piece = piece_start(index, width), piece_width(width)
    gate = lax.dynamic_slice_in_dim(gate_weight[0], start, piece, 0)
    up = lax.dynamic_slice_in_dim(up_weight[0], start, piece, 0)
    return jnp.concatenate([gate, up], 1)


def down_piece(down_weight, index):
    width = down_weight.shape[2]
    return lax.dynamic_slice_in_dim(
        down_weight[0], piece_start(index, width), piece_width(width), 1
    )


def combine(weight_table, returned):
    high = lax.reduce_precision(weight_table, 8, 7)
    low = weight_table - high
    both = jnp.concatenate([high, low], 0).astype(jnp.bfloat16)
    sums = jnp.dot(both, returned, preferred_element_type=jnp.float32)
    rows = weight_table.shape[0]
    return sums[:rows] + sums[rows:]


def per_device(tokens, expert_ids, route_weight, gate_weight, up_weight, down_weight):
    rows_here, width = tokens.shape
    capacity = EXPERTS * MOST
    piece = piece_width(width)
    tp_size = lax.axis_size("tp")
    here = lax.axis_index("tp")
    right = lax.rem(here + 1, tp_size)
    left = lax.rem(here + tp_size - 1, tp_size)

    gate_up_left = lax.ppermute(gate_up_piece(gate_weight, up_weight, right), "tp", ring(1))
    gate_up_right = lax.ppermute(gate_up_piece(gate_weight, up_weight, left), "tp", ring(-1))
    down_left = lax.ppermute(down_piece(down_weight, right), "tp", ring(1))
    down_right = lax.ppermute(down_piece(down_weight, left), "tp", ring(-1))

    position = positions(expert_ids)
    matches = position[:, :, None] == jnp.arange(capacity, dtype=jnp.int32)[None, None, :]
    dispatch = jnp.any(matches, 1).astype(jnp.bfloat16)
    weight_table = jnp.sum(jnp.where(matches, route_weight[:, :, None], 0.0), 1)

    start = piece_start(here, width)
    source = lax.dynamic_slice_in_dim(tokens, start, piece, 1)
    column = lax.broadcasted_iota(jnp.int32, source.shape, 1) + start
    source = jnp.where(column >= lax.rem(here, PARTS) * piece, source, jnp.zeros_like(source))
    outgoing = jnp.einsum(
        "tp,td->pd", dispatch, source, preferred_element_type=jnp.float32
    ).astype(jnp.bfloat16)
    outgoing = outgoing.reshape(EXPERTS, MOST, piece)
    received = lax.all_to_all(outgoing, "ep", split_axis=0, concat_axis=0, tiled=True)
    received = received.reshape(capacity, piece)

    def product(weights):
        return jnp.dot(received, weights, preferred_element_type=jnp.float32)

    from_right = lax.ppermute(product(gate_up_left), "tp", ring(-1))
    from_left = lax.ppermute(product(gate_up_right), "tp", ring(1))
    gate_up = product(gate_up_piece(gate_weight, up_weight, here)) + from_right + from_left
    units = gate_weight.shape[2]
    hidden = (jax.nn.silu(gate_up[:, :units]) * gate_up[:, units:]).astype(jnp.bfloat16)
    hidden_left = lax.ppermute(hidden, "tp", ring(1))
    hidden_right = lax.ppermute(hidden, "tp", ring(-1))

    partial_rows = jnp.dot(
        jnp.concatenate([hidden_left, hidden, hidden_right], 1),
        jnp.concatenate([down_left, down_piece(down_weight, here), down_right], 0),
        preferred_element_type=jnp.float32,
    ).astype(jnp.bfloat16)
    partial_rows = partial_rows.reshape(EXPERTS, MOST, piece)
    returned = lax.all_to_all(partial_rows, "ep", split_axis=0, concat_axis=0, tiled=True)
    combined = combine(weight_table, returned.reshape(capacity, piece))

    pieces = combined.reshape(tp_size, rows_here // tp_size, piece)
    arrived = lax.all_to_all(pieces, "tp", split_axis=0, concat_axis=0, tiled=True)
    arrived = arrived.reshape(tp_size // PARTS, PARTS, rows_here // tp_size, piece).sum(0)
    skip = PARTS * piece - width
    parts = [arrived[i] for i in range(PARTS)]
    parts[-1] = parts[-1][:, skip:]
    return jnp.concatenate(parts, 1).astype(jnp.bfloat16)


def solution(mesh):
    in_specs = (
        P(("ep", "dp"), None),
        P(("ep", "dp"), None),
        P(("ep", "dp"), None),
        P("ep", None, "tp"),
        P("ep", None, "tp"),
        P("ep", "tp", None),
    )
    out_specs = P(("ep", "dp", "tp"), None)
    return jax.shard_map(
        per_device, mesh=mesh, in_specs=in_specs, out_specs=out_specs, check_vma=False
    )
```

time: 335 us -> 154 us (0.46)
  the two profiles are of different devices: /device:TPU:30 before, /device:TPU:4 now
where the time goes in v1:
time: 154 us
  starting transfers between devices  57.4 us (37%)
  waiting for transfers between devices  57.1 us (37%)
  blocking collectives  19.1 us (12%)
  matrix products  10.5 us (7%)
  local copies, waits for them, and re-layouts  6.78 us (4%)
  other arithmetic  2.2 us (1%)
    all_to_all x1, waiting for transfers between devices, per_device(): lax.all_to_all(partial_rows, 'ep', split_axis=0, concat_axis=0, tiled=True)  29.8 us
    all_to_all x1, blocking collectives, per_device(): lax.all_to_all(pieces, 'tp', split_axis=0, concat_axis=0, tiled=True)  19.1 us
    ppermute x1, waiting for transfers between devices, per_device(): lax.ppermute(gate_up_piece(gate_weight, up_weight, right), 'tp', ring(1))  17.1 us
    all_to_all x1, starting transfers between devices, per_device(): lax.all_to_all(outgoing, 'ep', split_axis=0, concat_axis=0, tiled=True)  13.2 us
    ppermute x1, starting transfers between devices, per_device(): lax.ppermute(gate_up_piece(gate_weight, up_weight, left), 'tp', ring(-1))  11.9 us
    all_to_all x1, starting transfers between devices, per_device(): lax.all_to_all(partial_rows, 'ep', split_axis=0, concat_axis=0, tiled=True)  9.91 us
    ppermute x1, waiting for transfers between devices, per_device(): from_right = lax.ppermute(product(gate_up_left), 'tp', ring(-1))  8.37 us
    ppermute x1, starting transfers between devices, per_device(): hidden_right = lax.ppermute(hidden, 'tp', ring(-1))  5.6 us
  transfers between devices with their start and end apart: 10, of which 5 were waited for; matrix products, arithmetic and copies ran while one was open for 7% of the time, Pallas kernels for 0%

profile of v1, /device:TPU:4, one launch (start us, length us, event | category | flops | bytes accessed | tf_op | source)
XLA Modules:
  0.0 153.5 jit_solution(3338246638370985752)
XLA Ops:
  0.0 0.8 copy.18
  0.8 0.1 eq.35
  0.9 0.6 reduce-window.6
  1.5 0.2 slice_reduce_fusion
  1.7 0.1 bitcast_bitcast_fusion
  1.8 0.1 reduce_sum.30
  1.9 0.1 fusion.23
  2.1 2.5 %fusion = bf16[32,8,2432]{2,1,0:T(8,128)(2,1)} fusion(pred[24,256]{1,0:T(8,128)(4,1)S(1)} %fusion.23, bf16[24,7168]{1,0:T(8,128)(2,1)} %param.6, s32[]{:T(128)S(6)} %select_n.25, pred[2432]{0:T(1024)(128)(4,1)S(1)} %add_compare_fusion), kind=kOutput, calls=%fused_computation.2 | convolution fusion | flops 30565376 | bytes 1370500 | tf_op jit(solution)/shard_map/tp,td->pd/dot_general | solution.py:84
  4.6 13.2 %all-to-all-start = ((bf16[32,8,2432]{2,1,0:T(8,128)(2,1)}), bf16[32,8,2432]{2,1,0:T(8,128)(2,1)S(1)}, u32[]{:S(2)}, u32[]{:S(2)}) async-start(bf16[32,8,2432]{2,1,0:T(8,128)(2,1)} %fusion), calls=%async_computation | async-start | bytes 2490368 | tf_op jit(solution)/shard_map/all_to_all | solution.py:88
  17.9 0.0 copy-done.1
  17.9 3.5 %dynamic-slice_bitcast_fusion.5 = (bf16[2432,128]{1,0:T(8,128)(2,1)S(1)}, bf16[2432,128]{1,0:T(8,128)(2,1)}, bf16[2432,128]{1,0:T(8,128)(2,1)S(1)}, bf16[2432,12...) fusion(bf16[1,7168,128]{2,1,0:T(8,128)(2,1)S(1)} %copy-done.1, s32[]{:T(128)S(6)} %select_n.27, ...), kind=kLoop, calls=%fused_computation.27 | loop fusion | bytes 7471116 | tf_op jit(solution)/shard_map/dynamic_slice | solution.py:41
  21.4 0.1 pad_maximum_fusion
  21.5 1.9 %collective-permute-start = (bf16[2432,256]{1,0:T(8,128)(2,1)S(1)}, bf16[2432,256]{1,0:T(8,128)(2,1)}, u32[]{:S(2)}, u32[]{:S(2)}) collective-permute-start(bf16[2432,256]{1,0:T(8,128)(2,1)S(1)} %pad_maximum_fusion), channel_id=1, source_target_pairs={{0,1},{1,2},{2,3},{3,4},{4,5},{5,6},{6,7},{7,8},{8,9},{9,10},{10,1... | collective-permute-start | bytes 3735560 | tf_op jit(solution)/shard_map/ppermute | solution.py:70
  23.5 0.0 copy-start
  23.5 0.1 pad_maximum_fusion.1
  23.6 11.9 %collective-permute-start.2 = (bf16[2432,256]{1,0:T(8,128)(2,1)S(1)}, bf16[2432,256]{1,0:T(8,128)(2,1)}, u32[]{:S(2)}, u32[]{:S(2)}) collective-permute-start(bf16[2432,256]{1,0:T(8,128)(2,1)S(1)} %pad_maximum_fusion.1), channel_id=1, source_target_pairs={{0,11},{1,0},{2,1},{3,2},{4,3},{5,4},{6,5},{7,6},{8,7},{9,8},{10,9... | collective-permute-start | bytes 3735560 | tf_op jit(solution)/shard_map/ppermute | solution.py:71
  35.5 0.0 copy-done
  35.5 1.9 %dynamic-slice_bitcast_fusion.2 = (bf16[128,2432]{1,0:T(8,128)(2,1)}, bf16[128,2432]{1,0:T(8,128)(2,1)}, bf16[128,2432]{1,0:T(8,128)(2,1)S(1)}) fusion(bf16[1,128,7168]{2,1,0:T(8,128)(2,1)S(1)} %copy-done, s32[]{:T(128)S(6)} %select_n.27, s32[]{:T(128)S(6)} %select_n.28, s32[]{:T(128)S(6)} %select_n.25), kind=kLoop, calls=%fused_computation.24 | loop fusion | bytes 3735564 | tf_op jit(solution)/shard_map/dynamic_slice | solution.py:47
  37.4 1.9 %collective-permute-start.6 = (bf16[128,2432]{1,0:T(8,128)(2,1)}, bf16[128,2432]{1,0:T(8,128)(2,1)}, u32[]{:S(2)}, u32[]{:S(2)}) collective-permute-start(bf16[128,2432]{1,0:T(8,128)(2,1)} %get-tuple-element.11), channel_id=1, source_target_pairs={{0,1},{1,2},{2,3},{3,4},{4,5},{5,6},{6,7},{7,8},{8,9},{9,10},{10,1... | collective-permute-start | bytes 1867784 | tf_op jit(solution)/shard_map/ppermute | solution.py:72
  39.3 5.1 %collective-permute-start.7 = (bf16[128,2432]{1,0:T(8,128)(2,1)}, bf16[128,2432]{1,0:T(8,128)(2,1)}, u32[]{:S(2)}, u32[]{:S(2)}) collective-permute-start(bf16[128,2432]{1,0:T(8,128)(2,1)} %get-tuple-element.12), channel_id=1, source_target_pairs={{0,11},{1,0},{2,1},{3,2},{4,3},{5,4},{6,5},{7,6},{8,7},{9,8},{10,9... | collective-permute-start | bytes 1867784 | tf_op jit(solution)/shard_map/ppermute | solution.py:73
  44.5 17.1 %collective-permute-done = bf16[2432,256]{1,0:T(8,128)(2,1)} collective-permute-done((bf16[2432,256]{1,0:T(8,128)(2,1)S(1)}, bf16[2432,256]{1,0:T(8,128)(2,1)}, u32[]{:S(2)}, u32[]{:S(2)}) %collective-permute-start) | collective-permute-done | bytes 1245216 | tf_op jit(solution)/shard_map/ppermute | solution.py:70
  61.6 0.0 all-to-all-done
  61.6 1.9 %fusion.15 = f32[256,256]{0,1:T(8,128)S(1)} fusion(bf16[2432,256]{1,0:T(8,128)(2,1)} %collective-permute-done, bf16[32,8,2432]{2,1,0:T(8,128)(2,1)S(1)} %all-to-all-done), kind=kOutput, calls=%fused_computation.19 | convolution fusion | flops 318767104 | bytes 2752512 | tf_op jit(solution)/shard_map/dot_general | solution.py:92
  63.5 0.0 copy-start.2
  63.5 4.1 %collective-permute-start.1 = (f32[256,256]{0,1:T(8,128)S(1)}, f32[256,256]{0,1:T(8,128)S(1)}, u32[]{:S(2)}, u32[]{:S(2)}) collective-permute-start(f32[256,256]{0,1:T(8,128)S(1)} %fusion.15), channel_id=1, source_target_pairs={{0,11},{1,0},{2,1},{3,2},{4,3},{5,4},{6,5},{7,6},{8,7},{9,8},{10,9... | collective-permute-start | bytes 786440 | tf_op jit(solution)/shard_map/ppermute | solution.py:94
  67.6 0.0 collective-permute-done.2
  67.6 1.9 %fusion.13 = f32[256,256]{0,1:T(8,128)S(1)} fusion(bf16[2432,256]{1,0:T(8,128)(2,1)} %collective-permute-done.2, bf16[32,8,2432]{2,1,0:T(8,128)(2,1)S(1)} %all-to-all-done), kind=kOutput, calls=%fused_computation.17 | convolution fusion | flops 318767104 | bytes 2752512 | tf_op jit(solution)/shard_map/dot_general | solution.py:92
  69.5 1.9 %collective-permute-start.3 = (f32[256,256]{0,1:T(8,128)S(1)}, f32[256,256]{0,1:T(8,128)S(1)}, u32[]{:S(2)}, u32[]{:S(2)}) collective-permute-start(f32[256,256]{0,1:T(8,128)S(1)} %fusion.13), channel_id=1, source_target_pairs={{0,1},{1,2},{2,3},{3,4},{4,5},{5,6},{6,7},{7,8},{8,9},{9,10},{10,1... | collective-permute-start | bytes 786440 | tf_op jit(solution)/shard_map/ppermute | solution.py:95
  71.5 0.6 fusion.7
  72.1 8.4 %collective-permute-done.1 = f32[256,256]{0,1:T(8,128)S(1)} collective-permute-done((f32[256,256]{0,1:T(8,128)S(1)}, f32[256,256]{0,1:T(8,128)S(1)}, u32[]{:S(2)}, u32[]{:S(2)}) %collective-permute-start.1) | collective-permute-done | bytes 262176 | tf_op jit(solution)/shard_map/ppermute | solution.py:94
  80.5 0.0 collective-permute-done.3
  80.5 0.1 add_add_fusion
  80.6 1.9 %collective-permute-start.4 = (bf16[256,128]{0,1:T(8,128)(2,1)S(1)}, bf16[256,128]{0,1:T(8,128)(2,1)S(1)}, u32[]{:S(2)}, u32[]{:S(2)}) collective-permute-start(bf16[256,128]{0,1:T(8,128)(2,1)S(1)} %fusion.24), channel_id=1, source_target_pairs={{0,1},{1,2},{2,3},{3,4},{4,5},{5,6},{6,7},{7,8},{8,9},{9,10},{10,1... | collective-permute-start | bytes 196616 | tf_op jit(solution)/shard_map/ppermute | solution.py:99
  82.5 5.6 %collective-permute-start.5 = (bf16[256,128]{0,1:T(8,128)(2,1)S(1)}, bf16[256,128]{0,1:T(8,128)(2,1)S(1)}, u32[]{:S(2)}, u32[]{:S(2)}) collective-permute-start(bf16[256,128]{0,1:T(8,128)(2,1)S(1)} %fusion.24), channel_id=1, source_target_pairs={{0,11},{1,0},{2,1},{3,2},{4,3},{5,4},{6,5},{7,6},{8,7},{9,8},{10,9... | collective-permute-start | bytes 196616 | tf_op jit(solution)/shard_map/ppermute | solution.py:100
  88.1 0.0 collective-permute-done.6
  88.2 0.0 collective-permute-done.7
  88.2 0.3 collective-permute-done.4
  88.4 1.6 %collective-permute-done.5 = bf16[256,128]{0,1:T(8,128)(2,1)S(1)} collective-permute-done((bf16[256,128]{0,1:T(8,128)(2,1)S(1)}, bf16[256,128]{0,1:T(8,128)(2,1)S(1)}, u32[]{:S(2)}, u32[]{:S(2)}) %collective-permute-start.5) | collective-permute-done | bytes 65568 | tf_op jit(solution)/shard_map/ppermute | solution.py:100
  90.0 3.2 %fusion.1 = bf16[32,8,2432]{2,1,0:T(8,128)(2,1)} fusion(bf16[128,2432]{1,0:T(8,128)(2,1)} %collective-permute-done.7, bf16[128,2432]{1,0:T(8,128)(2,1)S(1)} %get-tuple-element.13, bf16[128,2432]{1,0:T(8,128)(2,1)} %collective-permute-done.6, bf16[256,128]{0,1:T(8,128)(2,1)S(1)} %collective-permute-done.5, bf16[256,128]{0,1:T(8,128)(2,1)S(1)} %fusion.24, ...), kind=kOutput, calls=%fused_computation.3 | convolution fusion | flops 484966400 | bytes 3309568 | tf_op jit(solution)/shard_map/dot_general | solution.py:102
  93.2 9.9 %all-to-all-start.1 = ((bf16[32,8,2432]{2,1,0:T(8,128)(2,1)}), bf16[32,8,2432]{2,1,0:T(8,128)(2,1)S(1)}, u32[]{:S(2)}, u32[]{:S(2)}) async-start(bf16[32,8,2432]{2,1,0:T(8,128)(2,1)} %fusion.1), calls=%async_computation.1 | async-start | bytes 2490368 | tf_op jit(solution)/shard_map/all_to_all | solution.py:108
  103.1 0.1 copy.22
  103.2 0.1 select_reduce_fusion
  103.4 29.8 %all-to-all-done.1 = bf16[32,8,2432]{2,1,0:T(8,128)(2,1)S(1)} async-done(((bf16[32,8,2432]{2,1,0:T(8,128)(2,1)}), bf16[32,8,2432]{2,1,0:T(8,128)(2,1)S(1)}, u32[]{:S(2)}, u32[]{:S(2)}) %all-to-all-start.1) | async-done | bytes 1245216 | tf_op jit(solution)/shard_map/all_to_all | solution.py:108
  133.1 0.3 fusion.11
  133.5 0.1 reshape.53
  133.6 19.1 %all_to_all.15 = f32[12,2,2432]{2,1,0:T(2,128)S(1)} all-to-all(f32[12,2,2432]{2,1,0:T(2,128)S(1)} %reshape.53), channel_id=1, replica_groups=mesh['ep'=32,'dp'=2,'tp'=12] {'tp'}, dimensions={0} | all-to-all | bytes 466944 | tf_op jit(solution)/shard_map/all_to_all | solution.py:112
  152.7 0.1 reduce_sum.32
  152.9 0.6 pad_maximum_fusion.2
  (18 shorter events, 0.2 us)
Async XLA Ops:
  4.6 13.3 %copy-start.1 = (bf16[1,7168,128]{2,1,0:T(8,128)(2,1)S(1)}, bf16[1,7168,128]{2,1,0:T(8,128)(2,1)}, u32[]{:S(2)}) copy-start(bf16[1,7168,128]{2,1,0:T(8,128)(2,1)} %param.10) | copy-start | bytes 5505028
  4.6 56.9 %all-to-all-start = ((bf16[32,8,2432]{2,1,0:T(8,128)(2,1)}), bf16[32,8,2432]{2,1,0:T(8,128)(2,1)S(1)}, u32[]{:S(2)}, u32[]{:S(2)}) async-start(bf16[32,8,2432]{2,1,0:T(8,128)(2,1)} %fusion), calls=%async_computation | async-start | bytes 2490368 | tf_op jit(solution)/shard_map/all_to_all | solution.py:88
  21.5 40.0 %collective-permute-start = (bf16[2432,256]{1,0:T(8,128)(2,1)S(1)}, bf16[2432,256]{1,0:T(8,128)(2,1)}, u32[]{:S(2)}, u32[]{:S(2)}) collective-permute-start(bf16[2432,256]{1,0:T(8,128)(2,1)S(1)} %pad_maximum_fusion), channel_id=1, source_target_pairs={{0,1},{1,2},{2,3},{3,4},{4,5},{5,6},{6,7},{7,8},{8,9},{9,10},{10,1... | collective-permute-start | bytes 3735560 | tf_op jit(solution)/shard_map/ppermute | solution.py:70
  23.5 12.0 %copy-start = (bf16[1,128,7168]{2,1,0:T(8,128)(2,1)S(1)}, bf16[1,128,7168]{2,1,0:T(8,128)(2,1)}, u32[]{:S(2)}) copy-start(bf16[1,128,7168]{2,1,0:T(8,128)(2,1)} %param.11) | copy-start | bytes 5505028
  23.6 44.0 %collective-permute-start.2 = (bf16[2432,256]{1,0:T(8,128)(2,1)S(1)}, bf16[2432,256]{1,0:T(8,128)(2,1)}, u32[]{:S(2)}, u32[]{:S(2)}) collective-permute-start(bf16[2432,256]{1,0:T(8,128)(2,1)S(1)} %pad_maximum_fusion.1), channel_id=1, source_target_pairs={{0,11},{1,0},{2,1},{3,2},{4,3},{5,4},{6,5},{7,6},{8,7},{9,8},{10,9... | collective-permute-start | bytes 3735560 | tf_op jit(solution)/shard_map/ppermute | solution.py:71
  37.4 50.7 %collective-permute-start.6 = (bf16[128,2432]{1,0:T(8,128)(2,1)}, bf16[128,2432]{1,0:T(8,128)(2,1)}, u32[]{:S(2)}, u32[]{:S(2)}) collective-permute-start(bf16[128,2432]{1,0:T(8,128)(2,1)} %get-tuple-element.11), channel_id=1, source_target_pairs={{0,1},{1,2},{2,3},{3,4},{4,5},{5,6},{6,7},{7,8},{8,9},{9,10},{10,1... | collective-permute-start | bytes 1867784 | tf_op jit(solution)/shard_map/ppermute | solution.py:72
  39.3 48.8 %collective-permute-start.7 = (bf16[128,2432]{1,0:T(8,128)(2,1)}, bf16[128,2432]{1,0:T(8,128)(2,1)}, u32[]{:S(2)}, u32[]{:S(2)}) collective-permute-start(bf16[128,2432]{1,0:T(8,128)(2,1)} %get-tuple-element.12), channel_id=1, source_target_pairs={{0,11},{1,0},{2,1},{3,2},{4,3},{5,4},{6,5},{7,6},{8,7},{9,8},{10,9... | collective-permute-start | bytes 1867784 | tf_op jit(solution)/shard_map/ppermute | solution.py:73
  63.5 7.9 %copy-start.2 = (bf16[2432,128]{1,0:T(8,128)(2,1)S(1)}, bf16[2432,128]{1,0:T(8,128)(2,1)}, u32[]{:S(2)}) copy-start(bf16[2432,128]{1,0:T(8,128)(2,1)} %get-tuple-element.9) | copy-start | bytes 1867780
  63.5 7.9 %copy-start.3 = (bf16[2432,128]{1,0:T(8,128)(2,1)S(1)}, bf16[2432,128]{1,0:T(8,128)(2,1)}, u32[]{:S(2)}) copy-start(bf16[2432,128]{1,0:T(8,128)(2,1)} %get-tuple-element.20) | copy-start | bytes 1867780
  63.5 17.0 %collective-permute-start.1 = (f32[256,256]{0,1:T(8,128)S(1)}, f32[256,256]{0,1:T(8,128)S(1)}, u32[]{:S(2)}, u32[]{:S(2)}) collective-permute-start(f32[256,256]{0,1:T(8,128)S(1)} %fusion.15), channel_id=1, source_target_pairs={{0,11},{1,0},{2,1},{3,2},{4,3},{5,4},{6,5},{7,6},{8,7},{9,8},{10,9... | collective-permute-start | bytes 786440 | tf_op jit(solution)/shard_map/ppermute | solution.py:94
  69.5 11.0 %collective-permute-start.3 = (f32[256,256]{0,1:T(8,128)S(1)}, f32[256,256]{0,1:T(8,128)S(1)}, u32[]{:S(2)}, u32[]{:S(2)}) collective-permute-start(f32[256,256]{0,1:T(8,128)S(1)} %fusion.13), channel_id=1, source_target_pairs={{0,1},{1,2},{2,3},{3,4},{4,5},{5,6},{6,7},{7,8},{8,9},{9,10},{10,1... | collective-permute-start | bytes 786440 | tf_op jit(solution)/shard_map/ppermute | solution.py:95
  80.6 7.8 %collective-permute-start.4 = (bf16[256,128]{0,1:T(8,128)(2,1)S(1)}, bf16[256,128]{0,1:T(8,128)(2,1)S(1)}, u32[]{:S(2)}, u32[]{:S(2)}) collective-permute-start(bf16[256,128]{0,1:T(8,128)(2,1)S(1)} %fusion.24), channel_id=1, source_target_pairs={{0,1},{1,2},{2,3},{3,4},{4,5},{5,6},{6,7},{7,8},{8,9},{9,10},{10,1... | collective-permute-start | bytes 196616 | tf_op jit(solution)/shard_map/ppermute | solution.py:99
  82.5 7.5 %collective-permute-start.5 = (bf16[256,128]{0,1:T(8,128)(2,1)S(1)}, bf16[256,128]{0,1:T(8,128)(2,1)S(1)}, u32[]{:S(2)}, u32[]{:S(2)}) collective-permute-start(bf16[256,128]{0,1:T(8,128)(2,1)S(1)} %fusion.24), channel_id=1, source_target_pairs={{0,11},{1,0},{2,1},{3,2},{4,3},{5,4},{6,5},{7,6},{8,7},{9,8},{10,9... | collective-permute-start | bytes 196616 | tf_op jit(solution)/shard_map/ppermute | solution.py:100
  93.2 9.9 %copy-start.4 = (f32[24,8]{0,1:T(8,128)S(1)}, f32[24,8]{0,1:T(8,128)}, u32[]{:S(2)}) copy-start(f32[24,8]{0,1:T(8,128)} %param.8) | copy-start | bytes 2308
  93.2 39.9 %all-to-all-start.1 = ((bf16[32,8,2432]{2,1,0:T(8,128)(2,1)}), bf16[32,8,2432]{2,1,0:T(8,128)(2,1)S(1)}, u32[]{:S(2)}, u32[]{:S(2)}) async-start(bf16[32,8,2432]{2,1,0:T(8,128)(2,1)} %fusion.1), calls=%async_computation.1 | async-start | bytes 2490368 | tf_op jit(solution)/shard_map/all_to_all | solution.py:108

commit v2 on v1

v2 whole, which is shorter than its diff:
```python
import jax
import jax.numpy as jnp
from jax import lax
from jax.sharding import PartitionSpec as P

TOP = 8
EXPERTS = 32
MOST = 8
LANES = 128
PARTS = 3
CHUNKS = 2


def shift(array, step):
    size = lax.axis_size("tp")
    pairs = [
        (core * size + i, core * size + (i + sign * step) % size)
        for core, sign in ((0, 1), (1, -1))
        for i in range(size)
    ]
    return lax.ppermute(array, ("dp", "tp"), pairs)


def swap(array):
    return lax.ppermute(array, "dp", [(0, 1), (1, 0)])


def piece_width(width):
    tiles = -(-width // LANES)
    return -(-tiles // PARTS) * LANES


def piece_start(index, width):
    piece = piece_width(width)
    return jnp.minimum(lax.rem(index, PARTS) * piece, width - piece)


def positions(expert_ids):
    chosen = expert_ids.reshape(-1)
    onehot = (chosen[:, None] == jnp.arange(EXPERTS, dtype=jnp.int32)[None, :]).astype(jnp.int32)
    earlier = jnp.cumsum(onehot, 0) - onehot
    slot_index = jnp.sum(earlier * onehot, 1)
    slots = MOST // CHUNKS
    chunk = slot_index // slots
    position = chunk * EXPERTS * slots + chosen * slots + slot_index % slots
    return position.reshape(expert_ids.shape)


def gate_up_piece(gate_weight, up_weight, index):
    width = gate_weight.shape[1]
    start, piece = piece_start(index, width), piece_width(width)
    gate = lax.dynamic_slice_in_dim(gate_weight[0], start, piece, 0)
    up = lax.dynamic_slice_in_dim(up_weight[0], start, piece, 0)
    return jnp.concatenate([gate, up], 1)


def down_piece(down_weight, index):
    width = down_weight.shape[2]
    return lax.dynamic_slice_in_dim(
        down_weight[0], piece_start(index, width), piece_width(width), 1
    )


def combine(weight_table, returned):
    high = lax.reduce_precision(weight_table, 8, 7)
    low = weight_table - high
    both = jnp.concatenate([high, low], 0).astype(jnp.bfloat16)
    sums = jnp.dot(both, returned, preferred_element_type=jnp.float32)
    rows = weight_table.shape[0]
    return sums[:rows] + sums[rows:]


def per_device(tokens, expert_ids, route_weight, gate_weight, up_weight, down_weight):
    rows_here, width = tokens.shape
    piece = piece_width(width)
    tp_size = lax.axis_size("tp")
    here = lax.axis_index("tp")
    target = lax.rem(here + jnp.where(lax.axis_index("dp") == 0, 1, tp_size - 1), tp_size)

    gate_up_near = shift(gate_up_piece(gate_weight, up_weight, target), 1)
    gate_up_far = swap(gate_up_near)
    down_near = shift(down_piece(down_weight, target), 1)
    down_far = swap(down_near)
    gate_up_here = gate_up_piece(gate_weight, up_weight, here)
    down_all = jnp.concatenate([down_near, down_piece(down_weight, here), down_far], 0)
    units = gate_weight.shape[2]

    position = positions(expert_ids)
    matches = position[:, :, None] == jnp.arange(EXPERTS * MOST, dtype=jnp.int32)[None, None, :]
    dispatch = jnp.any(matches, 1).astype(jnp.bfloat16)
    weight_table = jnp.sum(jnp.where(matches, route_weight[:, :, None], 0.0), 1)

    start = piece_start(here, width)
    source = lax.dynamic_slice_in_dim(tokens, start, piece, 1)
    column = lax.broadcasted_iota(jnp.int32, source.shape, 1) + start
    source = jnp.where(column >= lax.rem(here, PARTS) * piece, source, jnp.zeros_like(source))

    slots = MOST // CHUNKS
    rows = EXPERTS * slots
    combined = 0.0
    for chunk in range(CHUNKS):
        span = slice(chunk * rows, (chunk + 1) * rows)
        outgoing = jnp.einsum(
            "tp,td->pd", dispatch[:, span], source, preferred_element_type=jnp.float32
        ).astype(jnp.bfloat16)
        outgoing = outgoing.reshape(EXPERTS, slots, piece)
        received = lax.all_to_all(outgoing, "ep", split_axis=0, concat_axis=0, tiled=True)
        received = received.reshape(rows, piece)

        def product(weights):
            return jnp.dot(received, weights, preferred_element_type=jnp.float32)

        from_far = shift(product(gate_up_near), -1)
        from_near = shift(product(gate_up_far), 1)
        gate_up = product(gate_up_here) + from_far + from_near
        hidden = (jax.nn.silu(gate_up[:, :units]) * gate_up[:, units:]).astype(jnp.bfloat16)
        hidden_near, hidden_far = shift(hidden, 1), shift(hidden, -1)
        partial_rows = jnp.dot(
            jnp.concatenate([hidden_near, hidden, hidden_far], 1),
            down_all,
            preferred_element_type=jnp.float32,
        ).astype(jnp.bfloat16)
        partial_rows = partial_rows.reshape(EXPERTS, slots, piece)
        returned = lax.all_to_all(partial_rows, "ep", split_axis=0, concat_axis=0, tiled=True)
        combined += combine(weight_table[:, span], returned.reshape(rows, piece))

    pieces = combined.reshape(tp_size, rows_here // tp_size, piece)
    arrived = lax.all_to_all(pieces, "tp", split_axis=0, concat_axis=0, tiled=True)
    arrived = arrived.reshape(tp_size // PARTS, PARTS, rows_here // tp_size, piece).sum(0)
    skip = PARTS * piece - width
    parts = [arrived[i] for i in range(PARTS)]
    parts[-1] = parts[-1][:, skip:]
    return jnp.concatenate(parts, 1).astype(jnp.bfloat16)


def solution(mesh):
    in_specs = (
        P(("ep", "dp"), None),
        P(("ep", "dp"), None),
        P(("ep", "dp"), None),
        P("ep", None, "tp"),
        P("ep", None, "tp"),
        P("ep", "tp", None),
    )
    out_specs = P(("ep", "dp", "tp"), None)
    return jax.shard_map(
        per_device, mesh=mesh, in_specs=in_specs, out_specs=out_specs, check_vma=False
    )
```

time: 154 us -> 172 us (1.12)
  starting transfers between devices: 57.4 us -> 74 us
  local copies, waits for them, and re-layouts: 6.78 us -> 18.8 us
  waiting for transfers between devices: 57.1 us -> 45.6 us
  matrix products: 10.5 us -> 8.75 us
    all_to_all x1 -> x2, waiting for transfers between devices: 29.8 us -> 12 us  [per_device(): lax.all_to_all(partial_rows, 'ep', split_axis=0, concat_axis=0, tiled=True)]
    reshape x0 -> x8, local copies, waits for them, and re-layouts: none -> 11.1 us  [the longest x2 3.27 us: per_device(): partial_rows = partial_rows.reshape(EXPERTS, slots, piece)]
    all_to_all x1 -> x2, starting transfers between devices: 9.91 us -> 19.6 us  [per_device(): lax.all_to_all(partial_rows, 'ep', split_axis=0, concat_axis=0, tiled=True)]
    all_to_all x1 -> x2, starting transfers between devices: 13.2 us -> 21 us  [per_device(): lax.all_to_all(outgoing, 'ep', split_axis=0, concat_axis=0, tiled=True)]
    ppermute x8 -> x12, waiting for transfers between devices: 27.3 us -> 33.3 us  [the longest x10 33.3 us: shift(): return lax.ppermute(array, ('dp', 'tp'), pairs)]
    dot_general x3 -> x6, matrix products: 4.48 us -> 2.05 us  [product(): return jnp.dot(received, weights, preferred_element_type=jnp.float32)]
    ppermute x8 -> x12, starting transfers between devices: 34.3 us -> 33.5 us  [the longest x10 29.7 us: shift(): return lax.ppermute(array, ('dp', 'tp'), pairs)]
    dot_general x2 -> x4, matrix products: 5.71 us -> 6.25 us  [the longest x2 4.58 us: per_device(): jnp.dot(jnp.concatenate([hidden_near, hidden, hidden_far], 1), down_all,...]
  transfers between devices with their start and end apart: 10 -> 16, of which waited for: 5 -> 10; matrix products, arithmetic and copies ran while one was open for 7% -> 11% of each run, Pallas kernels for 0% -> 0%
where the time goes in v2:
time: 172 us; the launch traced here: 171 us
  starting transfers between devices  74 us (43%)
  waiting for transfers between devices  45.6 us (27%)
  blocking collectives  20.1 us (12%)
  local copies, waits for them, and re-layouts  18.8 us (11%)
  matrix products  8.75 us (5%)
  other arithmetic  3.19 us (2%)
    ppermute x10, waiting for transfers between devices, shift(): return lax.ppermute(array, ('dp', 'tp'), pairs)  33.3 us
    ppermute x10, starting transfers between devices, shift(): return lax.ppermute(array, ('dp', 'tp'), pairs)  29.7 us
    all_to_all x2, starting transfers between devices, per_device(): lax.all_to_all(outgoing, 'ep', split_axis=0, concat_axis=0, tiled=True)  21 us
    all_to_all x1, blocking collectives, per_device(): lax.all_to_all(pieces, 'tp', split_axis=0, concat_axis=0, tiled=True)  20.1 us
    all_to_all x2, starting transfers between devices, per_device(): lax.all_to_all(partial_rows, 'ep', split_axis=0, concat_axis=0, tiled=True)  19.6 us
    all_to_all x2, waiting for transfers between devices, per_device(): lax.all_to_all(partial_rows, 'ep', split_axis=0, concat_axis=0, tiled=True)  12 us
    dot_general x2, matrix products, per_device(): jnp.dot(jnp.concatenate([hidden_near, hidden, hidden_far], 1), down_all,...  4.58 us
    ppermute x2, starting transfers between devices, swap(): return lax.ppermute(array, 'dp', [(0, 1), (1, 0)])  3.82 us
  transfers between devices with their start and end apart: 16, of which 10 were waited for; matrix products, arithmetic and copies ran while one was open for 11% of the time, Pallas kernels for 0%

profile of v2, /device:TPU:4, one launch (start us, length us, event | category | flops | bytes accessed | tf_op | source)
XLA Modules:
  0.0 170.9 jit_solution(14592928979798665206)
XLA Ops:
  0.0 3.3 %dynamic-slice_bitcast_fusion.4 = (bf16[2432,128]{1,0:T(8,128)(2,1)}, bf16[2432,128]{1,0:T(8,128)(2,1)S(1)}, bf16[2432,128]{1,0:T(8,128)(2,1)S(1)}, bf16[2432,128]{1,0:T(8,128)(2,1)}) fusion(bf16[1,7168,128]{2,1,0:T(8,128)(2,1)} %param.10, s32[]{:T(128)S(6)} %select_n.42, s32[]{:T(128)S(6)} %select_n.45, bf16[1,7168,128]{2,1,0:T(8,128)(2,1)} %param.9), kind=kLoop, calls=%fused_computation.13 | loop fusion | bytes 4980744 | tf_op jit(solution)/shard_map/dynamic_slice | solution.py:53
  3.3 1.2 pad_maximum_fusion.2
  4.5 4.3 %collective-permute-start = (bf16[2432,256]{1,0:T(8,128)(2,1)}, bf16[2432,256]{1,0:T(8,128)(2,1)S(1)}, u32[]{:S(2)}, u32[]{:S(2)}) collective-permute-start(bf16[2432,256]{1,0:T(8,128)(2,1)} %pad_maximum_fusion.2), channel_id=1, source_target_pairs={{0,1},{1,2},{2,3},{3,4},{4,5},{5,6},{6,7},{7,8},{8,9},{9,10},{10,1... | collective-permute-start | bytes 3735560 | tf_op jit(solution)/shard_map/ppermute | solution.py:21
  9.0 0.6 reduce-window.6
  10.2 0.4 convolution_convert_fusion
  10.6 1.0 reshape.96
  11.6 10.7 %all-to-all-start.2 = ((bf16[32,4,2432]{2,1,0:T(4,128)(2,1)}), bf16[32,4,2432]{2,1,0:T(4,128)(2,1)S(1)}, u32[]{:S(2)}, u32[]{:S(2)}) async-start(bf16[32,4,2432]{2,1,0:T(4,128)(2,1)} %reshape.96), calls=%async_computation.2 | async-start | bytes 1245184 | tf_op jit(solution)/shard_map/all_to_all | solution.py:107
  22.3 11.9 %collective-permute-done = bf16[2432,256]{1,0:T(8,128)(2,1)S(1)} collective-permute-done((bf16[2432,256]{1,0:T(8,128)(2,1)}, bf16[2432,256]{1,0:T(8,128)(2,1)S(1)}, u32[]{:S(2)}, u32[]{:S(2)}) %collective-permute-start) | collective-permute-done | bytes 1245216 | tf_op jit(solution)/shard_map/ppermute | solution.py:21
  34.2 1.9 %collective-permute-start.2 = (bf16[2432,256]{1,0:T(8,128)(2,1)S(1)}, bf16[2432,256]{1,0:T(8,128)(2,1)S(1)}, u32[]{:S(2)}, u32[]{:S(2)}) collective-permute-start(bf16[2432,256]{1,0:T(8,128)(2,1)S(1)} %collective-permute-done), channel_id=1, source_target_pairs={{0,12},{12,0},{1,13},{13,1},{2,14},{14,2},{3,15},{15,3},{4,16},{16... | collective-permute-start | bytes 3735560 | tf_op jit(solution)/shard_map/ppermute | solution.py:25
  36.1 2.9 %dynamic-slice_bitcast_fusion = (bf16[128,2432]{1,0:T(8,128)(2,1)}, bf16[128,2432]{1,0:T(8,128)(2,1)}) fusion(bf16[1,128,7168]{2,1,0:T(8,128)(2,1)} %param.11, s32[]{:T(128)S(6)} %select_n.42, s32[]{:T(128)S(6)} %select_n.45), kind=kLoop, calls=%fused_computation.9 | loop fusion | bytes 2490376 | tf_op jit(solution)/shard_map/dynamic_slice | solution.py:59
  38.9 1.9 %collective-permute-start.6 = (bf16[128,2432]{1,0:T(8,128)(2,1)}, bf16[128,2432]{1,0:T(8,128)(2,1)}, u32[]{:S(2)}, u32[]{:S(2)}) collective-permute-start(bf16[128,2432]{1,0:T(8,128)(2,1)} %get-tuple-element.10), channel_id=1, source_target_pairs={{0,1},{1,2},{2,3},{3,4},{4,5},{5,6},{6,7},{7,8},{8,9},{9,10},{10,1... | collective-permute-start | bytes 1867784 | tf_op jit(solution)/shard_map/ppermute | solution.py:21
  40.8 1.3 convolution_convert_fusion.1
  42.1 2.3 %reshape.92 = bf16[32,4,2432]{2,1,0:T(4,128)(2,1)} reshape(bf16[128,2432]{1,0:T(8,128)(2,1)} %convolution_convert_fusion.1) | data formatting | bytes 1245184 | tf_op jit(solution)/shard_map/reshape | solution.py:106
  44.4 8.2 %collective-permute-done.6 = bf16[128,2432]{1,0:T(8,128)(2,1)} collective-permute-done((bf16[128,2432]{1,0:T(8,128)(2,1)}, bf16[128,2432]{1,0:T(8,128)(2,1)}, u32[]{:S(2)}, u32[]{:S(2)}) %collective-permute-start.6) | collective-permute-done | bytes 622624 | tf_op jit(solution)/shard_map/ppermute | solution.py:21
  52.6 1.9 %collective-permute-start.7 = (bf16[128,2432]{1,0:T(8,128)(2,1)}, bf16[128,2432]{1,0:T(8,128)(2,1)}, u32[]{:S(2)}, u32[]{:S(2)}) collective-permute-start(bf16[128,2432]{1,0:T(8,128)(2,1)} %collective-permute-done.6), channel_id=1, source_target_pairs={{0,12},{12,0},{1,13},{13,1},{2,14},{14,2},{3,15},{15,3},{4,16},{16... | collective-permute-start | bytes 1867784 | tf_op jit(solution)/shard_map/ppermute | solution.py:25
  54.5 0.8 copy-done
  55.3 10.3 %all-to-all-start = ((bf16[32,4,2432]{2,1,0:T(4,128)(2,1)}), bf16[32,4,2432]{2,1,0:T(4,128)(2,1)}, u32[]{:S(2)}, u32[]{:S(2)}) async-start(bf16[32,4,2432]{2,1,0:T(4,128)(2,1)} %reshape.92), calls=%async_computation | async-start | bytes 1245184 | tf_op jit(solution)/shard_map/all_to_all | solution.py:107
  65.6 1.5 reshape.97
  67.1 0.3 fusion.51
  67.5 3.2 %collective-permute-start.8 = (f32[128,256]{1,0:T(8,128)S(1)}, f32[128,256]{1,0:T(8,128)S(1)}, u32[]{:S(2)}, u32[]{:S(2)}) collective-permute-start(f32[128,256]{1,0:T(8,128)S(1)} %fusion.51), channel_id=1, source_target_pairs={{0,11},{1,0},{2,1},{3,2},{4,3},{5,4},{6,5},{7,6},{8,7},{9,8},{10,9... | collective-permute-start | bytes 393224 | tf_op jit(solution)/shard_map/ppermute | solution.py:21
  70.7 0.3 fusion.52
  71.1 2.6 %collective-permute-start.9 = (f32[128,256]{1,0:T(8,128)S(1)}, f32[128,256]{1,0:T(8,128)S(1)}, u32[]{:S(2)}, u32[]{:S(2)}) collective-permute-start(f32[128,256]{1,0:T(8,128)S(1)} %fusion.52), channel_id=1, source_target_pairs={{0,1},{1,2},{2,3},{3,4},{4,5},{5,6},{6,7},{7,8},{8,9},{9,10},{10,1... | collective-permute-start | bytes 393224 | tf_op jit(solution)/shard_map/ppermute | solution.py:21
  73.7 0.3 fusion
  74.1 0.4 collective-permute-done.8
  74.5 4.6 %collective-permute-done.9 = f32[128,256]{1,0:T(8,128)S(1)} collective-permute-done((f32[128,256]{1,0:T(8,128)S(1)}, f32[128,256]{1,0:T(8,128)S(1)}, u32[]{:S(2)}, u32[]{:S(2)}) %collective-permute-start.9) | collective-permute-done | bytes 131104 | tf_op jit(solution)/shard_map/ppermute | solution.py:21
  79.2 1.9 %collective-permute-start.11 = (bf16[128,128]{1,0:T(8,128)(2,1)S(1)}, bf16[128,128]{1,0:T(8,128)(2,1)S(1)}, u32[]{:S(2)}, u32[]{:S(2)}) collective-permute-start(bf16[128,128]{1,0:T(8,128)(2,1)S(1)} %fusion.14), channel_id=1, source_target_pairs={{0,11},{1,0},{2,1},{3,2},{4,3},{5,4},{6,5},{7,6},{8,7},{9,8},{10,9... | collective-permute-start | bytes 98312 | tf_op jit(solution)/shard_map/ppermute | solution.py:21
  81.1 3.9 %collective-permute-start.10 = (bf16[128,128]{1,0:T(8,128)(2,1)S(1)}, bf16[128,128]{1,0:T(8,128)(2,1)S(1)}, u32[]{:S(2)}, u32[]{:S(2)}) collective-permute-start(bf16[128,128]{1,0:T(8,128)(2,1)S(1)} %fusion.14), channel_id=1, source_target_pairs={{0,1},{1,2},{2,3},{3,4},{4,5},{5,6},{6,7},{7,8},{8,9},{9,10},{10,1... | collective-permute-start | bytes 98312 | tf_op jit(solution)/shard_map/ppermute | solution.py:21
  85.3 1.5 reshape.93
  86.8 1.4 collective-permute-done.10
  88.2 2.8 %convolution_convert_fusion.2 = bf16[128,2432]{1,0:T(8,128)(2,1)} fusion(bf16[128,2432]{1,0:T(8,128)(2,1)} %collective-permute-done.7, bf16[128,2432]{1,0:T(8,128)(2,1)} %get-tuple-element.9, bf16[128,2432]{1,0:T(8,128)(2,1)} %collective-permute-done.6, bf16[128,128]{1,0:T(8,128)(2,1)S(1)} %collective-permute-done.11, bf16[128,128]{1,0:T(8,128)(2,1)S(1)} %fusion.14, ...), kind=kOutput, calls=%fused_computation.2 | convolution fusion | flops 245284864 | bytes 2588672 | tf_op jit(solution)/shard_map/dot_general | solution.py:118
  90.9 2.3 %reshape.98 = bf16[32,4,2432]{2,1,0:T(4,128)(2,1)} reshape(bf16[128,2432]{1,0:T(8,128)(2,1)} %convolution_convert_fusion.2) | data formatting | bytes 1245184 | tf_op jit(solution)/shard_map/reshape | solution.py:123
  93.2 9.8 %all-to-all-start.3 = ((bf16[32,4,2432]{2,1,0:T(4,128)(2,1)}), bf16[32,4,2432]{2,1,0:T(4,128)(2,1)}, u32[]{:S(2)}, u32[]{:S(2)}) async-start(bf16[32,4,2432]{2,1,0:T(4,128)(2,1)} %reshape.98), calls=%async_computation.3 | async-start | bytes 1245184 | tf_op jit(solution)/shard_map/all_to_all | solution.py:124
  103.1 0.3 fusion.49
  103.4 1.9 %collective-permute-start.1 = (f32[128,256]{1,0:T(8,128)S(1)}, f32[128,256]{1,0:T(8,128)S(1)}, u32[]{:S(2)}, u32[]{:S(2)}) collective-permute-start(f32[128,256]{1,0:T(8,128)S(1)} %fusion.49), channel_id=1, source_target_pairs={{0,11},{1,0},{2,1},{3,2},{4,3},{5,4},{6,5},{7,6},{8,7},{9,8},{10,9... | collective-permute-start | bytes 393224 | tf_op jit(solution)/shard_map/ppermute | solution.py:21
  105.4 0.3 fusion.50
  105.7 4.1 %collective-permute-start.3 = (f32[128,256]{1,0:T(8,128)S(1)}, f32[128,256]{1,0:T(8,128)S(1)}, u32[]{:S(2)}, u32[]{:S(2)}) collective-permute-start(f32[128,256]{1,0:T(8,128)S(1)} %fusion.50), channel_id=1, source_target_pairs={{0,1},{1,2},{2,3},{3,4},{4,5},{5,6},{6,7},{7,8},{8,9},{9,10},{10,1... | collective-permute-start | bytes 393224 | tf_op jit(solution)/shard_map/ppermute | solution.py:21
  109.8 0.3 fusion.1
  110.3 3.6 %collective-permute-done.3 = f32[128,256]{1,0:T(8,128)S(1)} collective-permute-done((f32[128,256]{1,0:T(8,128)S(1)}, f32[128,256]{1,0:T(8,128)S(1)}, u32[]{:S(2)}, u32[]{:S(2)}) %collective-permute-start.3) | collective-permute-done | bytes 131104 | tf_op jit(solution)/shard_map/ppermute | solution.py:21
  114.0 1.9 %collective-permute-start.5 = (bf16[128,128]{1,0:T(8,128)(2,1)S(1)}, bf16[128,128]{1,0:T(8,128)(2,1)S(1)}, u32[]{:S(2)}, u32[]{:S(2)}) collective-permute-start(bf16[128,128]{1,0:T(8,128)(2,1)S(1)} %fusion.15), channel_id=1, source_target_pairs={{0,11},{1,0},{2,1},{3,2},{4,3},{5,4},{6,5},{7,6},{8,7},{9,8},{10,9... | collective-permute-start | bytes 98312 | tf_op jit(solution)/shard_map/ppermute | solution.py:21
  115.9 3.9 %collective-permute-start.4 = (bf16[128,128]{1,0:T(8,128)(2,1)S(1)}, bf16[128,128]{1,0:T(8,128)(2,1)S(1)}, u32[]{:S(2)}, u32[]{:S(2)}) collective-permute-start(bf16[128,128]{1,0:T(8,128)(2,1)S(1)} %fusion.15), channel_id=1, source_target_pairs={{0,1},{1,2},{2,3},{3,4},{4,5},{5,6},{6,7},{7,8},{8,9},{9,10},{10,1... | collective-permute-start | bytes 98312 | tf_op jit(solution)/shard_map/ppermute | solution.py:21
  119.9 3.1 %collective-permute-done.4 = bf16[128,128]{1,0:T(8,128)(2,1)S(1)} collective-permute-done((bf16[128,128]{1,0:T(8,128)(2,1)S(1)}, bf16[128,128]{1,0:T(8,128)(2,1)S(1)}, u32[]{:S(2)}, u32[]{:S(2)}) %collective-permute-start.4) | collective-permute-done | bytes 32800 | tf_op jit(solution)/shard_map/ppermute | solution.py:21
  122.9 1.8 %convolution_convert_fusion.3 = bf16[128,2432]{1,0:T(8,128)(2,1)S(1)} fusion(bf16[128,2432]{1,0:T(8,128)(2,1)} %collective-permute-done.7, bf16[128,2432]{1,0:T(8,128)(2,1)S(1)} %copy-done.1, bf16[128,2432]{1,0:T(8,128)(2,1)} %collective-permute-done.6, bf16[128,128]{1,0:T(8,128)(2,1)S(1)} %collective-permute-done.5, bf16[128,128]{1,0:T(8,128)(2,1)S(1)} %fusion.15, ...), kind=kOutput, calls=%fused_computation.3 | convolution fusion | flops 245284864 | bytes 2588672 | tf_op jit(solution)/shard_map/dot_general | solution.py:118
  124.7 1.0 reshape.94
  125.7 9.8 %all-to-all-start.1 = ((bf16[32,4,2432]{2,1,0:T(4,128)(2,1)}), bf16[32,4,2432]{2,1,0:T(4,128)(2,1)S(1)}, u32[]{:S(2)}, u32[]{:S(2)}) async-start(bf16[32,4,2432]{2,1,0:T(4,128)(2,1)} %reshape.94), calls=%async_computation.1 | async-start | bytes 1245184 | tf_op jit(solution)/shard_map/all_to_all | solution.py:124
  135.7 1.5 reshape.99
  137.5 12.0 %all-to-all-done.1 = bf16[32,4,2432]{2,1,0:T(4,128)(2,1)S(1)} async-done(((bf16[32,4,2432]{2,1,0:T(4,128)(2,1)}), bf16[32,4,2432]{2,1,0:T(4,128)(2,1)S(1)}, u32[]{:S(2)}, u32[]{:S(2)}) %all-to-all-start.1) | async-done | bytes 622624 | tf_op jit(solution)/shard_map/all_to_all | solution.py:124
  150.1 20.1 %all_to_all.25 = f32[12,2,2432]{2,1,0:T(2,128)S(1)} all-to-all(f32[12,2,2432]{2,1,0:T(2,128)S(1)} %reshape.100), channel_id=1, replica_groups=mesh['ep'=32,'dp'=2,'tp'=12] {'tp'}, dimensions={0} | all-to-all | bytes 466944 | tf_op jit(solution)/shard_map/all_to_all | solution.py:128
  170.3 0.6 pad_maximum_fusion.7
  (53 shorter events, 2.4 us)
Async XLA Ops:
  3.3 5.5 %copy-start.7 = (s32[24,8]{0,1:T(8,128)S(1)}, s32[24,8]{0,1:T(8,128)}, u32[]{:S(2)}) copy-start(s32[24,8]{0,1:T(8,128)} %param.7) | copy-start | bytes 2308
  3.3 6.9 %copy-start.6 = (bf16[24,7168]{1,0:T(8,128)(2,1)S(1)}, bf16[24,7168]{1,0:T(8,128)(2,1)}, u32[]{:S(2)}) copy-start(bf16[24,7168]{1,0:T(8,128)(2,1)} %param.6) | copy-start | bytes 1032196
  4.5 29.7 %collective-permute-start = (bf16[2432,256]{1,0:T(8,128)(2,1)}, bf16[2432,256]{1,0:T(8,128)(2,1)S(1)}, u32[]{:S(2)}, u32[]{:S(2)}) collective-permute-start(bf16[2432,256]{1,0:T(8,128)(2,1)} %pad_maximum_fusion.2), channel_id=1, source_target_pairs={{0,1},{1,2},{2,3},{3,4},{4,5},{5,6},{6,7},{7,8},{8,9},{9,10},{10,1... | collective-permute-start | bytes 3735560 | tf_op jit(solution)/shard_map/ppermute | solution.py:21
  11.6 42.9 %all-to-all-start.2 = ((bf16[32,4,2432]{2,1,0:T(4,128)(2,1)}), bf16[32,4,2432]{2,1,0:T(4,128)(2,1)S(1)}, u32[]{:S(2)}, u32[]{:S(2)}) async-start(bf16[32,4,2432]{2,1,0:T(4,128)(2,1)} %reshape.96), calls=%async_computation.2 | async-start | bytes 1245184 | tf_op jit(solution)/shard_map/all_to_all | solution.py:107
  34.2 36.5 %collective-permute-start.2 = (bf16[2432,256]{1,0:T(8,128)(2,1)S(1)}, bf16[2432,256]{1,0:T(8,128)(2,1)S(1)}, u32[]{:S(2)}, u32[]{:S(2)}) collective-permute-start(bf16[2432,256]{1,0:T(8,128)(2,1)S(1)} %collective-permute-done), channel_id=1, source_target_pairs={{0,12},{12,0},{1,13},{13,1},{2,14},{14,2},{3,15},{15,3},{4,16},{16... | collective-permute-start | bytes 3735560 | tf_op jit(solution)/shard_map/ppermute | solution.py:25
  38.9 13.6 %collective-permute-start.6 = (bf16[128,2432]{1,0:T(8,128)(2,1)}, bf16[128,2432]{1,0:T(8,128)(2,1)}, u32[]{:S(2)}, u32[]{:S(2)}) collective-permute-start(bf16[128,2432]{1,0:T(8,128)(2,1)} %get-tuple-element.10), channel_id=1, source_target_pairs={{0,1},{1,2},{2,3},{3,4},{4,5},{5,6},{6,7},{7,8},{8,9},{9,10},{10,1... | collective-permute-start | bytes 1867784 | tf_op jit(solution)/shard_map/ppermute | solution.py:21
  52.6 34.2 %collective-permute-start.7 = (bf16[128,2432]{1,0:T(8,128)(2,1)}, bf16[128,2432]{1,0:T(8,128)(2,1)}, u32[]{:S(2)}, u32[]{:S(2)}) collective-permute-start(bf16[128,2432]{1,0:T(8,128)(2,1)} %collective-permute-done.6), channel_id=1, source_target_pairs={{0,12},{12,0},{1,13},{13,1},{2,14},{14,2},{3,15},{15,3},{4,16},{16... | collective-permute-start | bytes 1867784 | tf_op jit(solution)/shard_map/ppermute | solution.py:25
  54.5 0.8 copy-start
  55.3 29.9 %all-to-all-start = ((bf16[32,4,2432]{2,1,0:T(4,128)(2,1)}), bf16[32,4,2432]{2,1,0:T(4,128)(2,1)}, u32[]{:S(2)}, u32[]{:S(2)}) async-start(bf16[32,4,2432]{2,1,0:T(4,128)(2,1)} %reshape.92), calls=%async_computation | async-start | bytes 1245184 | tf_op jit(solution)/shard_map/all_to_all | solution.py:107
  67.1 6.6 %copy-start.2 = (bf16[2432,128]{1,0:T(8,128)(2,1)S(1)}, bf16[2432,128]{1,0:T(8,128)(2,1)}, u32[]{:S(2)}) copy-start(bf16[2432,128]{1,0:T(8,128)(2,1)} %get-tuple-element.7) | copy-start | bytes 1867780
  67.1 6.6 %copy-start.4 = (bf16[2432,128]{1,0:T(8,128)(2,1)S(1)}, bf16[2432,128]{1,0:T(8,128)(2,1)}, u32[]{:S(2)}) copy-start(bf16[2432,128]{1,0:T(8,128)(2,1)} %get-tuple-element.19) | copy-start | bytes 1867780
  67.5 7.0 %collective-permute-start.8 = (f32[128,256]{1,0:T(8,128)S(1)}, f32[128,256]{1,0:T(8,128)S(1)}, u32[]{:S(2)}, u32[]{:S(2)}) collective-permute-start(f32[128,256]{1,0:T(8,128)S(1)} %fusion.51), channel_id=1, source_target_pairs={{0,11},{1,0},{2,1},{3,2},{4,3},{5,4},{6,5},{7,6},{8,7},{9,8},{10,9... | collective-permute-start | bytes 393224 | tf_op jit(solution)/shard_map/ppermute | solution.py:21
  71.1 8.1 %collective-permute-start.9 = (f32[128,256]{1,0:T(8,128)S(1)}, f32[128,256]{1,0:T(8,128)S(1)}, u32[]{:S(2)}, u32[]{:S(2)}) collective-permute-start(f32[128,256]{1,0:T(8,128)S(1)} %fusion.52), channel_id=1, source_target_pairs={{0,1},{1,2},{2,3},{3,4},{4,5},{5,6},{6,7},{7,8},{8,9},{9,10},{10,1... | collective-permute-start | bytes 393224 | tf_op jit(solution)/shard_map/ppermute | solution.py:21
  79.2 7.6 %collective-permute-start.11 = (bf16[128,128]{1,0:T(8,128)(2,1)S(1)}, bf16[128,128]{1,0:T(8,128)(2,1)S(1)}, u32[]{:S(2)}, u32[]{:S(2)}) collective-permute-start(bf16[128,128]{1,0:T(8,128)(2,1)S(1)} %fusion.14), channel_id=1, source_target_pairs={{0,11},{1,0},{2,1},{3,2},{4,3},{5,4},{6,5},{7,6},{8,7},{9,8},{10,9... | collective-permute-start | bytes 98312 | tf_op jit(solution)/shard_map/ppermute | solution.py:21
  81.1 7.0 %collective-permute-start.10 = (bf16[128,128]{1,0:T(8,128)(2,1)S(1)}, bf16[128,128]{1,0:T(8,128)(2,1)S(1)}, u32[]{:S(2)}, u32[]{:S(2)}) collective-permute-start(bf16[128,128]{1,0:T(8,128)(2,1)S(1)} %fusion.14), channel_id=1, source_target_pairs={{0,1},{1,2},{2,3},{3,4},{4,5},{5,6},{6,7},{7,8},{8,9},{9,10},{10,1... | collective-permute-start | bytes 98312 | tf_op jit(solution)/shard_map/ppermute | solution.py:21
  93.2 32.5 %all-to-all-start.3 = ((bf16[32,4,2432]{2,1,0:T(4,128)(2,1)}), bf16[32,4,2432]{2,1,0:T(4,128)(2,1)}, u32[]{:S(2)}, u32[]{:S(2)}) async-start(bf16[32,4,2432]{2,1,0:T(4,128)(2,1)} %reshape.98), calls=%async_computation.3 | async-start | bytes 1245184 | tf_op jit(solution)/shard_map/all_to_all | solution.py:124
  103.1 6.7 %copy-start.3 = (bf16[2432,128]{1,0:T(8,128)(2,1)S(1)}, bf16[2432,128]{1,0:T(8,128)(2,1)}, u32[]{:S(2)}) copy-start(bf16[2432,128]{1,0:T(8,128)(2,1)} %get-tuple-element.7) | copy-start | bytes 1867780
  103.1 6.7 %copy-start.5 = (bf16[2432,128]{1,0:T(8,128)(2,1)S(1)}, bf16[2432,128]{1,0:T(8,128)(2,1)}, u32[]{:S(2)}) copy-start(bf16[2432,128]{1,0:T(8,128)(2,1)} %get-tuple-element.19) | copy-start | bytes 1867780
  103.4 6.9 %collective-permute-start.1 = (f32[128,256]{1,0:T(8,128)S(1)}, f32[128,256]{1,0:T(8,128)S(1)}, u32[]{:S(2)}, u32[]{:S(2)}) collective-permute-start(f32[128,256]{1,0:T(8,128)S(1)} %fusion.49), channel_id=1, source_target_pairs={{0,11},{1,0},{2,1},{3,2},{4,3},{5,4},{6,5},{7,6},{8,7},{9,8},{10,9... | collective-permute-start | bytes 393224 | tf_op jit(solution)/shard_map/ppermute | solution.py:21
  105.7 17.2 %copy-start.1 = (bf16[128,2432]{1,0:T(8,128)(2,1)S(1)}, bf16[128,2432]{1,0:T(8,128)(2,1)}, u32[]{:S(2)}) copy-start(bf16[128,2432]{1,0:T(8,128)(2,1)} %get-tuple-element.9) | copy-start | bytes 1867780
  105.7 8.2 %collective-permute-start.3 = (f32[128,256]{1,0:T(8,128)S(1)}, f32[128,256]{1,0:T(8,128)S(1)}, u32[]{:S(2)}, u32[]{:S(2)}) collective-permute-start(f32[128,256]{1,0:T(8,128)S(1)} %fusion.50), channel_id=1, source_target_pairs={{0,1},{1,2},{2,3},{3,4},{4,5},{5,6},{6,7},{7,8},{8,9},{9,10},{10,1... | collective-permute-start | bytes 393224 | tf_op jit(solution)/shard_map/ppermute | solution.py:21
  114.0 5.9 %collective-permute-start.5 = (bf16[128,128]{1,0:T(8,128)(2,1)S(1)}, bf16[128,128]{1,0:T(8,128)(2,1)S(1)}, u32[]{:S(2)}, u32[]{:S(2)}) collective-permute-start(bf16[128,128]{1,0:T(8,128)(2,1)S(1)} %fusion.15), channel_id=1, source_target_pairs={{0,11},{1,0},{2,1},{3,2},{4,3},{5,4},{6,5},{7,6},{8,7},{9,8},{10,9... | collective-permute-start | bytes 98312 | tf_op jit(solution)/shard_map/ppermute | solution.py:21
  115.9 7.0 %collective-permute-start.4 = (bf16[128,128]{1,0:T(8,128)(2,1)S(1)}, bf16[128,128]{1,0:T(8,128)(2,1)S(1)}, u32[]{:S(2)}, u32[]{:S(2)}) collective-permute-start(bf16[128,128]{1,0:T(8,128)(2,1)S(1)} %fusion.15), channel_id=1, source_target_pairs={{0,1},{1,2},{2,3},{3,4},{4,5},{5,6},{6,7},{7,8},{8,9},{9,10},{10,1... | collective-permute-start | bytes 98312 | tf_op jit(solution)/shard_map/ppermute | solution.py:21
  124.7 10.8 %copy-start.8 = (f32[24,8]{0,1:T(8,128)S(1)}, f32[24,8]{0,1:T(8,128)}, u32[]{:S(2)}) copy-start(f32[24,8]{0,1:T(8,128)} %param.8) | copy-start | bytes 2308
  125.7 23.7 %all-to-all-start.1 = ((bf16[32,4,2432]{2,1,0:T(4,128)(2,1)}), bf16[32,4,2432]{2,1,0:T(4,128)(2,1)S(1)}, u32[]{:S(2)}, u32[]{:S(2)}) async-start(bf16[32,4,2432]{2,1,0:T(4,128)(2,1)} %reshape.94), calls=%async_computation.1 | async-start | bytes 1245184 | tf_op jit(solution)/shard_map/all_to_all | solution.py:124

commit v3 on v1

--- a/solution.py
+++ b/solution.py
@@ -3,16 +3,28 @@
 from jax import lax
 from jax.sharding import PartitionSpec as P
 
-TOP = 8
 EXPERTS = 32
 MOST = 8
 LANES = 128
 PARTS = 3
 
 
-def ring(step):
+def shift(array, step):
     size = lax.axis_size("tp")
-    return [(i, (i + step) % size) for i in range(size)]
+    pairs = [
+        (core * size + i, core * size + (i + sign * step) % size)
+        for core, sign in ((0, 1), (1, -1))
+        for i in range(size)
+    ]
+    return lax.ppermute(array, ("dp", "tp"), pairs)
+
+
+def swap(array):
+    return lax.ppermute(array, "dp", [(0, 1), (1, 0)])
+
+
+def exchange(array, axis):
+    return lax.all_to_all(array, axis, split_axis=0, concat_axis=0, tiled=True)
 
 
 def piece_width(width):
@@ -60,22 +72,21 @@
 
 def per_device(tokens, expert_ids, route_weight, gate_weight, up_weight, down_weight):
     rows_here, width = tokens.shape
+    piece = piece_width(width)
+    units = gate_weight.shape[2]
     capacity = EXPERTS * MOST
-    piece = piece_width(width)
     tp_size = lax.axis_size("tp")
     here = lax.axis_index("tp")
-    right = lax.rem(here + 1, tp_size)
-    left = lax.rem(here + tp_size - 1, tp_size)
+    target = lax.rem(here + jnp.where(lax.axis_index("dp") == 0, 1, tp_size - 1), tp_size)
 
-    gate_up_left = lax.ppermute(gate_up_piece(gate_weight, up_weight, right), "tp", ring(1))
-    gate_up_right = lax.ppermute(gate_up_piece(gate_weight, up_weight, left), "tp", ring(-1))
-    down_left = lax.ppermute(down_piece(down_weight, right), "tp", ring(1))
-    down_right = lax.ppermute(down_piece(down_weight, left), "tp", ring(-1))
+    sent = gate_up_piece(gate_weight, up_weight, target)
+    sent, expert_ids, tokens = lax.optimization_barrier((sent, expert_ids, tokens))
+    gate_up_near = shift(sent, 1)
+    gate_up_far = swap(gate_up_near)
 
     position = positions(expert_ids)
     matches = position[:, :, None] == jnp.arange(capacity, dtype=jnp.int32)[None, None, :]
     dispatch = jnp.any(matches, 1).astype(jnp.bfloat16)
-    weight_table = jnp.sum(jnp.where(matches, route_weight[:, :, None], 0.0), 1)
 
     start = piece_start(here, width)
     source = lax.dynamic_slice_in_dim(tokens, start, piece, 1)
@@ -84,33 +95,37 @@
     outgoing = jnp.einsum(
         "tp,td->pd", dispatch, source, preferred_element_type=jnp.float32
     ).astype(jnp.bfloat16)
-    outgoing = outgoing.reshape(EXPERTS, MOST, piece)
-    received = lax.all_to_all(outgoing, "ep", split_axis=0, concat_axis=0, tiled=True)
+    outgoing, gate_weight, up_weight, down_weight = lax.optimization_barrier(
+        (outgoing, gate_weight, up_weight, down_weight)
+    )
+    received = exchange(outgoing.reshape(EXPERTS, MOST, piece), "ep")
     received = received.reshape(capacity, piece)
+
+    down_near = shift(down_piece(down_weight, target), 1)
+    down_far = swap(down_near)
 
     def product(weights):
         return jnp.dot(received, weights, preferred_element_type=jnp.float32)
 
-    from_right = lax.ppermute(product(gate_up_left), "tp", ring(-1))
-    from_left = lax.ppermute(product(gate_up_right), "tp", ring(1))
-    gate_up = product(gate_up_piece(gate_weight, up_weight, here)) + from_right + from_left
-    units = gate_weight.shape[2]
+    from_far = shift(product(gate_up_near).astype(jnp.bfloat16), -1)
+    from_near = shift(product(gate_up_far).astype(jnp.bfloat16), 1)
+    gate_up = product(gate_up_piece(gate_weight, up_weight, here))
+    gate_up = gate_up + from_far.astype(jnp.float32) + from_near.astype(jnp.float32)
     hidden = (jax.nn.silu(gate_up[:, :units]) * gate_up[:, units:]).astype(jnp.bfloat16)
-    hidden_left = lax.ppermute(hidden, "tp", ring(1))
-    hidden_right = lax.ppermute(hidden, "tp", ring(-1))
-
+    hidden_near, hidden_far = shift(hidden, 1), shift(hidden, -1)
     partial_rows = jnp.dot(
-        jnp.concatenate([hidden_left, hidden, hidden_right], 1),
-        jnp.concatenate([down_left, down_piece(down_weight, here), down_right], 0),
+        jnp.concatenate([hidden_near, hidden, hidden_far], 1),
+        jnp.concatenate([down_near, down_piece(down_weight, here), down_far], 0),
         preferred_element_type=jnp.float32,
     ).astype(jnp.bfloat16)
-    partial_rows = partial_rows.reshape(EXPERTS, MOST, piece)
-    returned = lax.all_to_all(partial_rows, "ep", split_axis=0, concat_axis=0, tiled=True)
-    combined = combine(weight_table, returned.reshape(capacity, piece))
+    returned = exchange(partial_rows.reshape(EXPERTS, MOST, piece), "ep")
+    weight_table = jnp.sum(jnp.where(matches, route_weight[:, :, None], 0.0), 1)
+    combined = combine(weight_table, returned.reshape(capacity, piece)).astype(jnp.bfloat16)
 
     pieces = combined.reshape(tp_size, rows_here // tp_size, piece)
-    arrived = lax.all_to_all(pieces, "tp", split_axis=0, concat_axis=0, tiled=True)
-    arrived = arrived.reshape(tp_size // PARTS, PARTS, rows_here // tp_size, piece).sum(0)
+    arrived = exchange(pieces, "tp")
+    arrived = arrived.reshape(tp_size // PARTS, PARTS, rows_here // tp_size, piece)
+    arrived = sum(arrived[i].astype(jnp.float32) for i in range(tp_size // PARTS))
     skip = PARTS * piece - width
     parts = [arrived[i] for i in range(PARTS)]
     parts[-1] = parts[-1][:, skip:]

time: 154 us -> 153 us (level)
  the two profiles are of different devices: /device:TPU:4 before, /device:TPU:2 now
where the time goes in v3:
time: 153 us; the launch traced here: 152 us
  waiting for transfers between devices  70.3 us (46%)
  starting transfers between devices  43.7 us (29%)
  blocking collectives  17.3 us (11%)
  matrix products  9.23 us (6%)
  local copies, waits for them, and re-layouts  8.16 us (5%)
  other arithmetic  3.08 us (2%)
    ppermute x6, waiting for transfers between devices, shift(): return lax.ppermute(array, ('dp', 'tp'), pairs)  38.9 us
    all_to_all x2, waiting for transfers between devices, exchange(): return lax.all_to_all(array, axis, split_axis=0, concat_axis=0, tiled=True)  31.4 us
    all_to_all x2, starting transfers between devices, exchange(): return lax.all_to_all(array, axis, split_axis=0, concat_axis=0, tiled=True)  23 us
    all_to_all x1, blocking collectives, exchange(): return lax.all_to_all(array, axis, split_axis=0, concat_axis=0, tiled=True)  17.3 us
    ppermute x6, starting transfers between devices, shift(): return lax.ppermute(array, ('dp', 'tp'), pairs)  16.9 us
    ppermute x2, starting transfers between devices, swap(): return lax.ppermute(array, 'dp', [(0, 1), (1, 0)])  3.82 us
    dynamic_slice x2, local copies, waits for them, and re-layouts, gate_up_piece(): up = lax.dynamic_slice_in_dim(up_weight[0], start, piece, 0)  3.68 us
    dot_general x3, matrix products, product(): return jnp.dot(received, weights, preferred_element_type=jnp.float32)  3.18 us
  transfers between devices with their start and end apart: 10, of which 6 were waited for; matrix products, arithmetic and copies ran while one was open for 6% of the time, Pallas kernels for 0%

profile of v3, /device:TPU:2, one launch (start us, length us, event | category | flops | bytes accessed | tf_op | source)
XLA Modules:
  0.0 152.0 jit_solution(5770664436948668802)
XLA Ops:
  0.0 1.6 %dynamic-slice_bitcast_fusion.4 = (bf16[2432,128]{1,0:T(8,128)(2,1)S(1)}, bf16[2432,128]{1,0:T(8,128)(2,1)S(1)}) fusion(bf16[1,7168,128]{2,1,0:T(8,128)(2,1)} %param.10, s32[]{:T(128)S(6)} %select_n.24, bf16[1,7168,128]{2,1,0:T(8,128)(2,1)} %param.9), kind=kLoop, calls=%fused_computation.26 | loop fusion | bytes 2490372 | tf_op jit(solution)/shard_map/dynamic_slice | solution.py:53
  1.6 0.0 copy-start.2
  1.6 1.2 pad_maximum_fusion
  2.8 0.0 copy-done.2
  2.8 0.1 copy.18
  2.9 0.1 eq.39
  3.0 0.6 reduce-window.6
  3.6 0.2 slice_reduce_fusion
  3.8 0.1 bitcast_bitcast_fusion
  3.9 0.1 reduce_sum.21
  4.1 0.1 fusion.29
  4.2 2.5 %convolution_convert_fusion.1 = bf16[256,2432]{1,0:T(8,128)(2,1)} fusion(pred[24,256]{1,0:T(8,128)(4,1)S(1)} %fusion.29, bf16[24,7168]{1,0:T(8,128)(2,1)} %param.6, s32[]{:T(128)S(6)} %select_n.26, pred[2432]{0:T(1024)(128)(4,1)S(1)} %add_compare_fusion), kind=kOutput, calls=%fused_computation.1 | convolution fusion | flops 30565376 | bytes 1370500 | tf_op jit(solution)/shard_map/tp,td->pd/dot_general | solution.py:95
  6.8 13.1 %all-to-all-start = ((bf16[32,8,2432]{2,1,0:T(8,128)(2,1)}), bf16[32,8,2432]{2,1,0:T(8,128)(2,1)S(1)}, u32[]{:S(2)}, u32[]{:S(2)}) async-start(bf16[32,8,2432]{2,1,0:T(8,128)(2,1)} %bitcast.3), calls=%async_computation | async-start | bytes 2490368 | tf_op jit(solution)/shard_map/all_to_all | solution.py:27
  19.9 1.9 %collective-permute-start = (bf16[2432,256]{1,0:T(8,128)(2,1)}, bf16[2432,256]{1,0:T(8,128)(2,1)S(1)}, u32[]{:S(2)}, u32[]{:S(2)}) collective-permute-start(bf16[2432,256]{1,0:T(8,128)(2,1)} %pad_maximum_fusion), channel_id=1, source_target_pairs={{0,1},{1,2},{2,3},{3,4},{4,5},{5,6},{6,7},{7,8},{8,9},{9,10},{10,1... | collective-permute-start | bytes 3735560 | tf_op jit(solution)/shard_map/ppermute | solution.py:19
  21.8 24.9 %collective-permute-done = bf16[2432,256]{1,0:T(8,128)(2,1)S(1)} collective-permute-done((bf16[2432,256]{1,0:T(8,128)(2,1)}, bf16[2432,256]{1,0:T(8,128)(2,1)S(1)}, u32[]{:S(2)}, u32[]{:S(2)}) %collective-permute-start) | collective-permute-done | bytes 1245216 | tf_op jit(solution)/shard_map/ppermute | solution.py:19
  46.7 1.9 %collective-permute-start.2 = (bf16[2432,256]{1,0:T(8,128)(2,1)S(1)}, bf16[2432,256]{1,0:T(8,128)(2,1)}, u32[]{:S(2)}, u32[]{:S(2)}) collective-permute-start(bf16[2432,256]{1,0:T(8,128)(2,1)S(1)} %collective-permute-done), channel_id=1, source_target_pairs={{0,12},{12,0},{1,13},{13,1},{2,14},{14,2},{3,15},{15,3},{4,16},{16... | collective-permute-start | bytes 3735560 | tf_op jit(solution)/shard_map/ppermute | solution.py:23
  48.6 1.8 %dynamic-slice_bitcast_fusion = (bf16[128,2432]{1,0:T(8,128)(2,1)S(1)}, bf16[128,2432]{1,0:T(8,128)(2,1)S(1)}) fusion(bf16[1,128,7168]{2,1,0:T(8,128)(2,1)} %param.11, s32[]{:T(128)S(6)} %select_n.26, s32[]{:T(128)S(6)} %select_n.24), kind=kLoop, calls=%fused_computation.22 | loop fusion | bytes 2490376 | tf_op jit(solution)/shard_map/dynamic_slice | solution.py:59
  50.4 1.9 %collective-permute-start.6 = (bf16[128,2432]{1,0:T(8,128)(2,1)S(1)}, bf16[128,2432]{1,0:T(8,128)(2,1)}, u32[]{:S(2)}, u32[]{:S(2)}) collective-permute-start(bf16[128,2432]{1,0:T(8,128)(2,1)S(1)} %get-tuple-element.20), channel_id=1, source_target_pairs={{0,1},{1,2},{2,3},{3,4},{4,5},{5,6},{6,7},{7,8},{8,9},{9,10},{10,1... | collective-permute-start | bytes 1867784 | tf_op jit(solution)/shard_map/ppermute | solution.py:19
  52.3 2.1 %dynamic-slice_bitcast_fusion.2 = bf16[2432,128]{1,0:T(8,128)(2,1)} fusion(bf16[1,7168,128]{2,1,0:T(8,128)(2,1)} %param.10, s32[]{:T(128)S(6)} %select_n.26), kind=kLoop, calls=%fused_computation.24 | loop fusion | bytes 1245188 | tf_op jit(solution)/shard_map/dynamic_slice | solution.py:53
  54.4 2.1 %dynamic-slice_bitcast_fusion.3 = bf16[2432,128]{1,0:T(8,128)(2,1)} fusion(bf16[1,7168,128]{2,1,0:T(8,128)(2,1)} %param.9, s32[]{:T(128)S(6)} %select_n.26), kind=kLoop, calls=%fused_computation.25 | loop fusion | bytes 1245188 | tf_op jit(solution)/shard_map/dynamic_slice | solution.py:52
  56.5 7.4 %collective-permute-done.6 = bf16[128,2432]{1,0:T(8,128)(2,1)} collective-permute-done((bf16[128,2432]{1,0:T(8,128)(2,1)S(1)}, bf16[128,2432]{1,0:T(8,128)(2,1)}, u32[]{:S(2)}, u32[]{:S(2)}) %collective-permute-start.6) | collective-permute-done | bytes 622624 | tf_op jit(solution)/shard_map/ppermute | solution.py:19
  63.9 1.9 %collective-permute-start.7 = (bf16[128,2432]{1,0:T(8,128)(2,1)}, bf16[128,2432]{1,0:T(8,128)(2,1)}, u32[]{:S(2)}, u32[]{:S(2)}) collective-permute-start(bf16[128,2432]{1,0:T(8,128)(2,1)} %collective-permute-done.6), channel_id=1, source_target_pairs={{0,12},{12,0},{1,13},{13,1},{2,14},{14,2},{3,15},{15,3},{4,16},{16... | collective-permute-start | bytes 1867784 | tf_op jit(solution)/shard_map/ppermute | solution.py:23
  65.8 0.0 all-to-all-done
  65.8 0.6 fusion.17
  66.4 0.0 copy-start
  66.4 3.3 %collective-permute-start.1 = (bf16[256,256]{0,1:T(8,128)(2,1)S(1)}, bf16[256,256]{0,1:T(8,128)(2,1)S(1)}, u32[]{:S(2)}, u32[]{:S(2)}) collective-permute-start(bf16[256,256]{0,1:T(8,128)(2,1)S(1)} %fusion.17), channel_id=1, source_target_pairs={{0,11},{1,0},{2,1},{3,2},{4,3},{5,4},{6,5},{7,6},{8,7},{9,8},{10,9... | collective-permute-start | bytes 393224 | tf_op jit(solution)/shard_map/ppermute | solution.py:19
  69.8 0.0 collective-permute-done.2
  69.8 1.9 %fusion.20 = bf16[256,256]{0,1:T(8,128)(2,1)S(1)} fusion(bf16[2432,256]{1,0:T(8,128)(2,1)} %collective-permute-done.2, bf16[32,8,2432]{2,1,0:T(8,128)(2,1)S(1)} %all-to-all-done), kind=kOutput, calls=%fused_computation.21 | convolution fusion | flops 318832640 | bytes 2621440 | tf_op jit(solution)/shard_map/dot_general | solution.py:108
  71.7 2.6 %collective-permute-start.3 = (bf16[256,256]{0,1:T(8,128)(2,1)S(1)}, bf16[256,256]{0,1:T(8,128)(2,1)S(1)}, u32[]{:S(2)}, u32[]{:S(2)}) collective-permute-start(bf16[256,256]{0,1:T(8,128)(2,1)S(1)} %fusion.20), channel_id=1, source_target_pairs={{0,1},{1,2},{2,3},{3,4},{4,5},{5,6},{6,7},{7,8},{8,9},{9,10},{10,1... | collective-permute-start | bytes 393224 | tf_op jit(solution)/shard_map/ppermute | solution.py:19
  74.4 0.0 copy-done
  74.4 0.0 copy-done.1
  74.4 0.6 fusion.6
  75.0 0.0 collective-permute-done.1
  75.0 4.8 %collective-permute-done.3 = bf16[256,256]{0,1:T(8,128)(2,1)S(1)} collective-permute-done((bf16[256,256]{0,1:T(8,128)(2,1)S(1)}, bf16[256,256]{0,1:T(8,128)(2,1)S(1)}, u32[]{:S(2)}, u32[]{:S(2)}) %collective-permute-start.3) | collective-permute-done | bytes 131104 | tf_op jit(solution)/shard_map/ppermute | solution.py:19
  79.9 1.9 %collective-permute-start.4 = (bf16[256,128]{0,1:T(8,128)(2,1)S(1)}, bf16[256,128]{0,1:T(8,128)(2,1)S(1)}, u32[]{:S(2)}, u32[]{:S(2)}) collective-permute-start(bf16[256,128]{0,1:T(8,128)(2,1)S(1)} %fusion.30), channel_id=1, source_target_pairs={{0,1},{1,2},{2,3},{3,4},{4,5},{5,6},{6,7},{7,8},{8,9},{9,10},{10,1... | collective-permute-start | bytes 196616 | tf_op jit(solution)/shard_map/ppermute | solution.py:19
  81.8 5.1 %collective-permute-start.5 = (bf16[256,128]{0,1:T(8,128)(2,1)S(1)}, bf16[256,128]{0,1:T(8,128)(2,1)S(1)}, u32[]{:S(2)}, u32[]{:S(2)}) collective-permute-start(bf16[256,128]{0,1:T(8,128)(2,1)S(1)} %fusion.30), channel_id=1, source_target_pairs={{0,11},{1,0},{2,1},{3,2},{4,3},{5,4},{6,5},{7,6},{8,7},{9,8},{10,9... | collective-permute-start | bytes 196616 | tf_op jit(solution)/shard_map/ppermute | solution.py:19
  87.0 0.0 collective-permute-done.7
  87.0 0.3 collective-permute-done.4
  87.3 1.6 %collective-permute-done.5 = bf16[256,128]{0,1:T(8,128)(2,1)S(1)} collective-permute-done((bf16[256,128]{0,1:T(8,128)(2,1)S(1)}, bf16[256,128]{0,1:T(8,128)(2,1)S(1)}, u32[]{:S(2)}, u32[]{:S(2)}) %collective-permute-start.5) | collective-permute-done | bytes 65568 | tf_op jit(solution)/shard_map/ppermute | solution.py:19
  88.8 3.2 %fusion = bf16[32,8,2432]{2,1,0:T(8,128)(2,1)} fusion(bf16[128,2432]{1,0:T(8,128)(2,1)} %collective-permute-done.7, bf16[128,2432]{1,0:T(8,128)(2,1)S(1)} %get-tuple-element.19, bf16[128,2432]{1,0:T(8,128)(2,1)} %collective-permute-done.6, bf16[256,128]{0,1:T(8,128)(2,1)S(1)} %collective-permute-done.5, bf16[256,128]{0,1:T(8,128)(2,1)S(1)} %fusion.30, ...), kind=kOutput, calls=%fused_computation.2 | convolution fusion | flops 484966400 | bytes 3309568 | tf_op jit(solution)/shard_map/dot_general | solution.py:116
  92.0 9.9 %all-to-all-start.1 = ((bf16[32,8,2432]{2,1,0:T(8,128)(2,1)}), bf16[32,8,2432]{2,1,0:T(8,128)(2,1)S(1)}, u32[]{:S(2)}, u32[]{:S(2)}) async-start(bf16[32,8,2432]{2,1,0:T(8,128)(2,1)} %fusion), calls=%async_computation.1 | async-start | bytes 2490368 | tf_op jit(solution)/shard_map/all_to_all | solution.py:27
  101.9 0.1 copy.22
  102.0 0.1 select_reduce_fusion
  102.2 31.4 %all-to-all-done.1 = bf16[32,8,2432]{2,1,0:T(8,128)(2,1)S(1)} async-done(((bf16[32,8,2432]{2,1,0:T(8,128)(2,1)}), bf16[32,8,2432]{2,1,0:T(8,128)(2,1)S(1)}, u32[]{:S(2)}, u32[]{:S(2)}) %all-to-all-start.1) | async-done | bytes 1245216 | tf_op jit(solution)/shard_map/all_to_all | solution.py:27
  133.6 0.3 fusion.10
  134.0 17.3 %all_to_all.15 = bf16[12,2,2432]{2,1,0:T(2,128)(2,1)S(1)} all-to-all(bf16[12,2,2432]{2,1,0:T(2,128)(2,1)S(1)} %reshape.56), channel_id=1, replica_groups=mesh['ep'=32,'dp'=2,'tp'=12] {'tp'}, dimensions={0} | all-to-all | bytes 233472 | tf_op jit(solution)/shard_map/all_to_all | solution.py:27
  151.2 0.1 add_convert_fusion
  151.4 0.6 pad_maximum_fusion.1
  (17 shorter events, 0.3 us)
Async XLA Ops:
  1.6 1.2 copy-start.2
  6.8 59.0 %all-to-all-start = ((bf16[32,8,2432]{2,1,0:T(8,128)(2,1)}), bf16[32,8,2432]{2,1,0:T(8,128)(2,1)S(1)}, u32[]{:S(2)}, u32[]{:S(2)}) async-start(bf16[32,8,2432]{2,1,0:T(8,128)(2,1)} %bitcast.3), calls=%async_computation | async-start | bytes 2490368 | tf_op jit(solution)/shard_map/all_to_all | solution.py:27
  19.9 26.8 %collective-permute-start = (bf16[2432,256]{1,0:T(8,128)(2,1)}, bf16[2432,256]{1,0:T(8,128)(2,1)S(1)}, u32[]{:S(2)}, u32[]{:S(2)}) collective-permute-start(bf16[2432,256]{1,0:T(8,128)(2,1)} %pad_maximum_fusion), channel_id=1, source_target_pairs={{0,1},{1,2},{2,3},{3,4},{4,5},{5,6},{6,7},{7,8},{8,9},{9,10},{10,1... | collective-permute-start | bytes 3735560 | tf_op jit(solution)/shard_map/ppermute | solution.py:19
  46.7 23.1 %collective-permute-start.2 = (bf16[2432,256]{1,0:T(8,128)(2,1)S(1)}, bf16[2432,256]{1,0:T(8,128)(2,1)}, u32[]{:S(2)}, u32[]{:S(2)}) collective-permute-start(bf16[2432,256]{1,0:T(8,128)(2,1)S(1)} %collective-permute-done), channel_id=1, source_target_pairs={{0,12},{12,0},{1,13},{13,1},{2,14},{14,2},{3,15},{15,3},{4,16},{16... | collective-permute-start | bytes 3735560 | tf_op jit(solution)/shard_map/ppermute | solution.py:23
  50.4 13.4 %collective-permute-start.6 = (bf16[128,2432]{1,0:T(8,128)(2,1)S(1)}, bf16[128,2432]{1,0:T(8,128)(2,1)}, u32[]{:S(2)}, u32[]{:S(2)}) collective-permute-start(bf16[128,2432]{1,0:T(8,128)(2,1)S(1)} %get-tuple-element.20), channel_id=1, source_target_pairs={{0,1},{1,2},{2,3},{3,4},{4,5},{5,6},{6,7},{7,8},{8,9},{9,10},{10,1... | collective-permute-start | bytes 1867784 | tf_op jit(solution)/shard_map/ppermute | solution.py:19
  63.9 23.1 %collective-permute-start.7 = (bf16[128,2432]{1,0:T(8,128)(2,1)}, bf16[128,2432]{1,0:T(8,128)(2,1)}, u32[]{:S(2)}, u32[]{:S(2)}) collective-permute-start(bf16[128,2432]{1,0:T(8,128)(2,1)} %collective-permute-done.6), channel_id=1, source_target_pairs={{0,12},{12,0},{1,13},{13,1},{2,14},{14,2},{3,15},{15,3},{4,16},{16... | collective-permute-start | bytes 1867784 | tf_op jit(solution)/shard_map/ppermute | solution.py:23
  66.4 7.9 %copy-start = (bf16[2432,128]{1,0:T(8,128)(2,1)S(1)}, bf16[2432,128]{1,0:T(8,128)(2,1)}, u32[]{:S(2)}) copy-start(bf16[2432,128]{1,0:T(8,128)(2,1)} %dynamic-slice_bitcast_fusion.2) | copy-start | bytes 1867780
  66.4 7.9 %copy-start.1 = (bf16[2432,128]{1,0:T(8,128)(2,1)S(1)}, bf16[2432,128]{1,0:T(8,128)(2,1)}, u32[]{:S(2)}) copy-start(bf16[2432,128]{1,0:T(8,128)(2,1)} %dynamic-slice_bitcast_fusion.3) | copy-start | bytes 1867780
  66.4 8.6 %collective-permute-start.1 = (bf16[256,256]{0,1:T(8,128)(2,1)S(1)}, bf16[256,256]{0,1:T(8,128)(2,1)S(1)}, u32[]{:S(2)}, u32[]{:S(2)}) collective-permute-start(bf16[256,256]{0,1:T(8,128)(2,1)S(1)} %fusion.17), channel_id=1, source_target_pairs={{0,11},{1,0},{2,1},{3,2},{4,3},{5,4},{6,5},{7,6},{8,7},{9,8},{10,9... | collective-permute-start | bytes 393224 | tf_op jit(solution)/shard_map/ppermute | solution.py:19
  71.7 8.1 %collective-permute-start.3 = (bf16[256,256]{0,1:T(8,128)(2,1)S(1)}, bf16[256,256]{0,1:T(8,128)(2,1)S(1)}, u32[]{:S(2)}, u32[]{:S(2)}) collective-permute-start(bf16[256,256]{0,1:T(8,128)(2,1)S(1)} %fusion.20), channel_id=1, source_target_pairs={{0,1},{1,2},{2,3},{3,4},{4,5},{5,6},{6,7},{7,8},{8,9},{9,10},{10,1... | collective-permute-start | bytes 393224 | tf_op jit(solution)/shard_map/ppermute | solution.py:19
  79.9 7.4 %collective-permute-start.4 = (bf16[256,128]{0,1:T(8,128)(2,1)S(1)}, bf16[256,128]{0,1:T(8,128)(2,1)S(1)}, u32[]{:S(2)}, u32[]{:S(2)}) collective-permute-start(bf16[256,128]{0,1:T(8,128)(2,1)S(1)} %fusion.30), channel_id=1, source_target_pairs={{0,1},{1,2},{2,3},{3,4},{4,5},{5,6},{6,7},{7,8},{8,9},{9,10},{10,1... | collective-permute-start | bytes 196616 | tf_op jit(solution)/shard_map/ppermute | solution.py:19
  81.8 7.0 %collective-permute-start.5 = (bf16[256,128]{0,1:T(8,128)(2,1)S(1)}, bf16[256,128]{0,1:T(8,128)(2,1)S(1)}, u32[]{:S(2)}, u32[]{:S(2)}) collective-permute-start(bf16[256,128]{0,1:T(8,128)(2,1)S(1)} %fusion.30), channel_id=1, source_target_pairs={{0,11},{1,0},{2,1},{3,2},{4,3},{5,4},{6,5},{7,6},{8,7},{9,8},{10,9... | collective-permute-start | bytes 196616 | tf_op jit(solution)/shard_map/ppermute | solution.py:19
  92.0 9.9 %copy-start.3 = (f32[24,8]{0,1:T(8,128)S(1)}, f32[24,8]{0,1:T(8,128)}, u32[]{:S(2)}) copy-start(f32[24,8]{0,1:T(8,128)} %param.8) | copy-start | bytes 2308
  92.0 41.5 %all-to-all-start.1 = ((bf16[32,8,2432]{2,1,0:T(8,128)(2,1)}), bf16[32,8,2432]{2,1,0:T(8,128)(2,1)S(1)}, u32[]{:S(2)}, u32[]{:S(2)}) async-start(bf16[32,8,2432]{2,1,0:T(8,128)(2,1)} %fusion), calls=%async_computation.1 | async-start | bytes 2490368 | tf_op jit(solution)/shard_map/all_to_all | solution.py:27

commit v4 on v3

v4 whole, which is shorter than its diff:
```python
import jax
import jax.numpy as jnp
from jax import lax
from jax.experimental import pallas as pl
from jax.experimental.pallas import tpu as pltpu
from jax.sharding import PartitionSpec as P

TOP = 8
EXPERTS = 32
MOST = 8
LANES = 128
PARTS = 3


def shift(array, step):
    size = lax.axis_size("tp")
    pairs = [
        (core * size + i, core * size + (i + sign * step) % size)
        for core, sign in ((0, 1), (1, -1))
        for i in range(size)
    ]
    return lax.ppermute(array, ("dp", "tp"), pairs)


def swap(array):
    return lax.ppermute(array, "dp", [(0, 1), (1, 0)])


def exchange(array, axis):
    return lax.all_to_all(array, axis, split_axis=0, concat_axis=0, tiled=True)


def piece_width(width):
    tiles = -(-width // LANES)
    return -(-tiles // PARTS) * LANES


def piece_start(index, width):
    piece = piece_width(width)
    return jnp.minimum(lax.rem(index, PARTS) * piece, width - piece)


def cut_gate_up(start_ref, gate_ref, up_ref, out_ref, sem):
    piece, units = out_ref.shape[0], gate_ref.shape[2]
    rows = pl.ds(pl.multiple_of(start_ref[0], LANES), piece)
    copies = [
        pltpu.make_async_copy(
            ref.at[0, rows, :], out_ref.at[:, pl.ds(i * units, units)], sem.at[i]
        )
        for i, ref in enumerate((gate_ref, up_ref))
    ]
    for copy in copies:
        copy.start()
    for copy in copies:
        copy.wait()


def cut_down(start_ref, down_ref, out_ref, sem):
    columns = pl.ds(pl.multiple_of(start_ref[0], LANES), out_ref.shape[1])
    copy = pltpu.make_async_copy(down_ref.at[0, :, columns], out_ref, sem.at[0])
    copy.start()
    copy.wait()


def cut(kernel, start, arrays, shape):
    size = shape[0] * shape[1]
    return pl.pallas_call(
        kernel,
        out_shape=jax.ShapeDtypeStruct(shape, jnp.bfloat16),
        in_specs=[pl.BlockSpec(memory_space=pltpu.SMEM)]
        + [pl.BlockSpec(memory_space=pl.ANY)] * len(arrays),
        out_specs=pl.BlockSpec(memory_space=pltpu.VMEM),
        scratch_shapes=[pltpu.SemaphoreType.DMA((2,))],
        cost_estimate=pl.CostEstimate(
            flops=500 * size, bytes_accessed=4 * size, transcendentals=0
        ),
    )(start.reshape(1), *arrays)


def gate_up_piece(gate_weight, up_weight, index):
    width, units = gate_weight.shape[1:]
    shape = (piece_width(width), 2 * units)
    return cut(cut_gate_up, piece_start(index, width), (gate_weight, up_weight), shape)


def down_piece(down_weight, index):
    units, width = down_weight.shape[1:]
    shape = (units, piece_width(width))
    return cut(cut_down, piece_start(index, width), (down_weight,), shape)


def dispatch_kernel(where_ref, ids_ref, route_ref, tokens_ref, rows_ref, weights_ref, held, sem):
    tokens, piece = held.shape
    capacity = rows_ref.shape[0]
    start = pl.multiple_of(where_ref[0], LANES)
    copy = pltpu.make_async_copy(tokens_ref.at[:, pl.ds(start, piece)], held, sem.at[0])
    copy.start()
    lane = lax.broadcasted_iota(jnp.int32, (tokens, capacity), 1)
    expert, slot = lane // MOST, lane % MOST
    member = jnp.zeros((tokens, capacity), jnp.float32)
    weight = jnp.zeros((tokens, capacity), jnp.float32)
    for k in range(TOP):
        same = ids_ref[:, k : k + 1] == expert
        member = jnp.where(same, 1.0, member)
        weight = jnp.where(same, route_ref[:, k : k + 1], weight)
    row = lax.broadcasted_iota(jnp.int32, (tokens, tokens), 0)
    column = lax.broadcasted_iota(jnp.int32, (tokens, tokens), 1)
    above = jnp.where(column < row, 1.0, 0.0).astype(jnp.bfloat16)
    earlier = jnp.dot(above, member.astype(jnp.bfloat16), preferred_element_type=jnp.float32)
    here = earlier == slot.astype(jnp.float32)
    chosen = jnp.where(here, member, 0.0).astype(jnp.bfloat16)
    weight = jnp.where(here, weight, 0.0)
    high = weight.astype(jnp.bfloat16)
    weights_ref[0] = high
    weights_ref[1] = (weight - high.astype(jnp.float32)).astype(jnp.bfloat16)
    copy.wait()
    wide = lax.broadcasted_iota(jnp.int32, (tokens, piece), 1)
    source = jnp.where(wide >= where_ref[1], held[...].astype(jnp.float32), 0.0)
    rows_ref[...] = lax.dot_general(
        chosen,
        source.astype(jnp.bfloat16),
        (((0,), (0,)), ((), ())),
        preferred_element_type=jnp.float32,
    ).astype(jnp.bfloat16)


def dispatch(tokens, expert_ids, route_weight, index):
    count, width = tokens.shape
    piece, capacity = piece_width(width), EXPERTS * MOST
    start = piece_start(index, width)
    where = jnp.stack([start, lax.rem(index, PARTS) * piece - start])
    return pl.pallas_call(
        dispatch_kernel,
        out_shape=(
            jax.ShapeDtypeStruct((capacity, piece), jnp.bfloat16),
            jax.ShapeDtypeStruct((2, count, capacity), jnp.bfloat16),
        ),
        in_specs=[pl.BlockSpec(memory_space=pltpu.SMEM)]
        + [pl.BlockSpec(memory_space=pltpu.VMEM)] * 2
        + [pl.BlockSpec(memory_space=pl.ANY)],
        out_specs=(pl.BlockSpec(memory_space=pltpu.VMEM),) * 2,
        scratch_shapes=[pltpu.VMEM((count, piece), jnp.bfloat16), pltpu.SemaphoreType.DMA((1,))],
        cost_estimate=pl.CostEstimate(
            flops=2 * count * piece * capacity, bytes_accessed=2**21, transcendentals=0
        ),
        name="dispatch",
    )(where, expert_ids, route_weight, tokens)


def combine(weights, returned):
    parts, rows, capacity = weights.shape
    both = weights.reshape(parts * rows, capacity)
    sums = jnp.dot(both, returned, preferred_element_type=jnp.float32)
    return sums[:rows] + sums[rows:]


def per_device(tokens, expert_ids, route_weight, gate_weight, up_weight, down_weight):
    rows_here, width = tokens.shape
    piece = piece_width(width)
    units = gate_weight.shape[2]
    capacity = EXPERTS * MOST
    tp_size = lax.axis_size("tp")
    here = lax.axis_index("tp")
    target = lax.rem(here + jnp.where(lax.axis_index("dp") == 0, 1, tp_size - 1), tp_size)

    outgoing, weights = dispatch(tokens, expert_ids, route_weight, here)
    outgoing, gate_weight, up_weight, down_weight = lax.optimization_barrier(
        (outgoing, gate_weight, up_weight, down_weight)
    )
    received = exchange(outgoing.reshape(EXPERTS, MOST, piece), "ep")
    received = received.reshape(capacity, piece)

    gate_up_near = shift(gate_up_piece(gate_weight, up_weight, target), 1)
    gate_up_far = swap(gate_up_near)
    down_near = shift(down_piece(down_weight, target), 1)
    down_far = swap(down_near)
    gate_weight, up_weight, down_weight, _ = lax.optimization_barrier(
        (gate_weight, up_weight, down_weight, gate_up_near)
    )
    gate_up_here = gate_up_piece(gate_weight, up_weight, here)
    down_here = down_piece(down_weight, here)

    def product(weights):
        return jnp.dot(received, weights, preferred_element_type=jnp.float32)

    from_far = shift(product(gate_up_near).astype(jnp.bfloat16), -1)
    from_near = shift(product(gate_up_far).astype(jnp.bfloat16), 1)
    gate_up = product(gate_up_here)
    gate_up = gate_up + from_far.astype(jnp.float32) + from_near.astype(jnp.float32)
    hidden = (jax.nn.silu(gate_up[:, :units]) * gate_up[:, units:]).astype(jnp.bfloat16)
    hidden_near, hidden_far = shift(hidden, 1), shift(hidden, -1)
    partial_rows = jnp.dot(
        jnp.concatenate([hidden_near, hidden, hidden_far], 1),
        jnp.concatenate([down_near, down_here, down_far], 0),
        preferred_element_type=jnp.float32,
    ).astype(jnp.bfloat16)
    returned = exchange(partial_rows.reshape(EXPERTS, MOST, piece), "ep")
    combined = combine(weights, returned.reshape(capacity, piece)).astype(jnp.bfloat16)

    pieces = combined.reshape(tp_size, rows_here // tp_size, piece)
    arrived = exchange(pieces, "tp")
    arrived = arrived.reshape(tp_size // PARTS, PARTS, rows_here // tp_size, piece)
    arrived = sum(arrived[i].astype(jnp.float32) for i in range(tp_size // PARTS))
    skip = PARTS * piece - width
    parts = [arrived[i] for i in range(PARTS)]
    parts[-1] = parts[-1][:, skip:]
    return jnp.concatenate(parts, 1).astype(jnp.bfloat16)


def solution(mesh):
    in_specs = (
        P(("ep", "dp"), None),
        P(("ep", "dp"), None),
        P(("ep", "dp"), None),
        P("ep", None, "tp"),
        P("ep", None, "tp"),
        P("ep", "tp", None),
    )
    out_specs = P(("ep", "dp", "tp"), None)
    return jax.shard_map(
        per_device, mesh=mesh, in_specs=in_specs, out_specs=out_specs, check_vma=False
    )
```

time: 153 us -> 145 us (0.948)
  the two profiles are of different devices: /device:TPU:2 before, /device:TPU:8 now
where the time goes in v4:
time: 145 us; the launch traced here: 144 us
  blocking collectives  56.8 us (39%)
  starting transfers between devices  37.9 us (26%)
  waiting for transfers between devices  26.8 us (18%)
  Pallas kernels  11.7 us (8%)
  matrix products  6.71 us (5%)
  local copies, waits for them, and re-layouts  2.79 us (2%)
    all_to_all x2, blocking collectives, exchange(): return lax.all_to_all(array, axis, split_axis=0, concat_axis=0, tiled=True)  56.8 us
    ppermute x6, waiting for transfers between devices, shift(): return lax.ppermute(array, ('dp', 'tp'), pairs)  26.7 us
    ppermute x6, starting transfers between devices, shift(): return lax.ppermute(array, ('dp', 'tp'), pairs)  21 us
    all_to_all x1, starting transfers between devices, exchange(): return lax.all_to_all(array, axis, split_axis=0, concat_axis=0, tiled=True)  13.1 us
    pallas_call x4, Pallas kernels, cut(): pl.pallas_call(kernel, out_shape=jax.ShapeDtypeStruct(shape, jnp.bfloat16...  8.51 us
    dot_general x3, matrix products, product(): return jnp.dot(received, weights, preferred_element_type=jnp.float32)  4.46 us
    ppermute x2, starting transfers between devices, swap(): return lax.ppermute(array, 'dp', [(0, 1), (1, 0)])  3.82 us
    pallas_call x1, Pallas kernels, dispatch(): pl.pallas_call(dispatch_kernel, out_shape=(jax.ShapeDtypeStruct((capacity...  3.21 us
  transfers between devices with their start and end apart: 9, of which 3 were waited for; matrix products, arithmetic and copies ran while one was open for 3% of the time, Pallas kernels for 6%

profile of v4, /device:TPU:8, one launch (start us, length us, event | category | flops | bytes accessed | tf_op | source)
XLA Modules:
  0.0 144.3 jit_solution(12439832404154833697)
XLA Ops:
  0.0 1.4 copy.7.ids_ref
  1.4 1.4 copy.8.route_ref
  2.7 0.6 pad_add_fusion.where_ref
  3.4 3.2 %dispatch.1 = (bf16[256,2432]{1,0:T(8,128)(2,1)}, bf16[2,24,256]{2,1,0:T(8,128)(2,1)}) custom-call(s32[2]{0:T(128)} %pad_add_fusion.where_ref, s32[24,8]{1,0:T(8,128)} %copy.7.ids_ref, f32[24,8]{1,0:T(8,128)} %copy.8.route_ref, bf16[24,7168]{1,0:T(8,128)(2,1)} %tokens_ref.1), custom_call_target="tpu_custom_call" | custom-call | flops 29884416 | bytes 2097152 | tf_op jit(solution)/shard_map/dispatch/pallas_call | solution.py:132
  6.6 13.1 %all-to-all-start = ((bf16[32,8,2432]{2,1,0:T(8,128)(2,1)}), bf16[32,8,2432]{2,1,0:T(8,128)(2,1)S(1)}, u32[]{:S(2)}, u32[]{:S(2)}) async-start(bf16[32,8,2432]{2,1,0:T(8,128)(2,1)} %bitcast.35), calls=%async_computation | async-start | bytes 2490368 | tf_op jit(solution)/shard_map/all_to_all | solution.py:30
  19.7 2.3 %shard_map.64 = bf16[2432,256]{1,0:T(8,128)(2,1)} custom-call(s32[1]{0:T(128)} %bitcast.5.start_ref, bf16[1,7168,128]{2,1,0:T(8,128)(2,1)} %gate_ref.1, bf16[1,7168,128]{2,1,0:T(8,128)(2,1)} %up_ref.1), custom_call_target="tpu_custom_call" | custom-call | flops 311296000 | bytes 2490368 | tf_op jit(solution)/shard_map/pallas_call | solution.py:67
  22.0 1.9 %collective-permute-start = (bf16[2432,256]{1,0:T(8,128)(2,1)}, bf16[2432,256]{1,0:T(8,128)(2,1)S(1)}, u32[]{:S(2)}, u32[]{:S(2)}) collective-permute-start(bf16[2432,256]{1,0:T(8,128)(2,1)} %shard_map.64), channel_id=1, source_target_pairs={{0,1},{1,2},{2,3},{3,4},{4,5},{5,6},{6,7},{7,8},{8,9},{9,10},{10,1... | collective-permute-start | bytes 3735560 | tf_op jit(solution)/shard_map/ppermute | solution.py:22
  23.9 24.9 %collective-permute-done = bf16[2432,256]{1,0:T(8,128)(2,1)S(1)} collective-permute-done((bf16[2432,256]{1,0:T(8,128)(2,1)}, bf16[2432,256]{1,0:T(8,128)(2,1)S(1)}, u32[]{:S(2)}, u32[]{:S(2)}) %collective-permute-start) | collective-permute-done | bytes 1245216 | tf_op jit(solution)/shard_map/ppermute | solution.py:22
  48.8 1.9 %collective-permute-start.2 = (bf16[2432,256]{1,0:T(8,128)(2,1)S(1)}, bf16[2432,256]{1,0:T(8,128)(2,1)}, u32[]{:S(2)}, u32[]{:S(2)}) collective-permute-start(bf16[2432,256]{1,0:T(8,128)(2,1)S(1)} %collective-permute-done), channel_id=1, source_target_pairs={{0,12},{12,0},{1,13},{13,1},{2,14},{14,2},{3,15},{15,3},{4,16},{16... | collective-permute-start | bytes 3735560 | tf_op jit(solution)/shard_map/ppermute | solution.py:26
  50.7 1.9 %shard_map.66 = bf16[128,2432]{1,0:T(8,128)(2,1)} custom-call(s32[1]{0:T(128)} %bitcast.5.start_ref, bf16[1,128,7168]{2,1,0:T(8,128)(2,1)} %down_ref.1), custom_call_target="tpu_custom_call" | custom-call | flops 155648000 | bytes 1245184 | tf_op jit(solution)/shard_map/pallas_call | solution.py:67
  52.6 1.9 %collective-permute-start.6 = (bf16[128,2432]{1,0:T(8,128)(2,1)}, bf16[128,2432]{1,0:T(8,128)(2,1)S(1)}, u32[]{:S(2)}, u32[]{:S(2)}) collective-permute-start(bf16[128,2432]{1,0:T(8,128)(2,1)} %shard_map.66), channel_id=1, source_target_pairs={{0,1},{1,2},{2,3},{3,4},{4,5},{5,6},{6,7},{7,8},{8,9},{9,10},{10,1... | collective-permute-start | bytes 1867784 | tf_op jit(solution)/shard_map/ppermute | solution.py:22
  54.6 0.0 all-to-all-done
  54.6 0.6 fusion.20
  55.2 8.2 %collective-permute-start.1 = (bf16[256,256]{0,1:T(8,128)(2,1)S(1)}, bf16[256,256]{0,1:T(8,128)(2,1)S(1)}, u32[]{:S(2)}, u32[]{:S(2)}) collective-permute-start(bf16[256,256]{0,1:T(8,128)(2,1)S(1)} %fusion.20), channel_id=1, source_target_pairs={{0,11},{1,0},{2,1},{3,2},{4,3},{5,4},{6,5},{7,6},{8,7},{9,8},{10,9... | collective-permute-start | bytes 393224 | tf_op jit(solution)/shard_map/ppermute | solution.py:22
  63.4 0.0 collective-permute-done.2
  63.4 1.9 %fusion.23 = bf16[256,256]{0,1:T(8,128)(2,1)S(1)} fusion(bf16[2432,256]{1,0:T(8,128)(2,1)} %collective-permute-done.2, bf16[32,8,2432]{2,1,0:T(8,128)(2,1)S(1)} %all-to-all-done), kind=kOutput, calls=%fused_computation.18 | convolution fusion | flops 318832640 | bytes 2621440 | tf_op jit(solution)/shard_map/dot_general | solution.py:184
  65.3 1.9 %collective-permute-start.3 = (bf16[256,256]{0,1:T(8,128)(2,1)S(1)}, bf16[256,256]{0,1:T(8,128)(2,1)S(1)}, u32[]{:S(2)}, u32[]{:S(2)}) collective-permute-start(bf16[256,256]{0,1:T(8,128)(2,1)S(1)} %fusion.23), channel_id=1, source_target_pairs={{0,1},{1,2},{2,3},{3,4},{4,5},{5,6},{6,7},{7,8},{8,9},{9,10},{10,1... | collective-permute-start | bytes 393224 | tf_op jit(solution)/shard_map/ppermute | solution.py:22
  67.2 0.4 collective-permute-done.6
  67.6 1.9 %collective-permute-start.7 = (bf16[128,2432]{1,0:T(8,128)(2,1)S(1)}, bf16[128,2432]{1,0:T(8,128)(2,1)S(1)}, u32[]{:S(2)}, u32[]{:S(2)}) collective-permute-start(bf16[128,2432]{1,0:T(8,128)(2,1)S(1)} %collective-permute-done.6), channel_id=1, source_target_pairs={{0,12},{12,0},{1,13},{13,1},{2,14},{14,2},{3,15},{15,3},{4,16},{16... | collective-permute-start | bytes 1867784 | tf_op jit(solution)/shard_map/ppermute | solution.py:26
  69.5 2.3 %shard_map.65 = bf16[2432,256]{1,0:T(8,128)(2,1)} custom-call(s32[1]{0:T(128)} %bitcast.start_ref, bf16[1,7168,128]{2,1,0:T(8,128)(2,1)} %gate_ref.1, bf16[1,7168,128]{2,1,0:T(8,128)(2,1)} %up_ref.1), custom_call_target="tpu_custom_call" | custom-call | flops 311296000 | bytes 2490368 | tf_op jit(solution)/shard_map/pallas_call | solution.py:67
  71.8 0.0 collective-permute-done.1
  71.9 1.5 %collective-permute-done.3 = bf16[256,256]{0,1:T(8,128)(2,1)S(1)} collective-permute-done((bf16[256,256]{0,1:T(8,128)(2,1)S(1)}, bf16[256,256]{0,1:T(8,128)(2,1)S(1)}, u32[]{:S(2)}, u32[]{:S(2)}) %collective-permute-start.3) | collective-permute-done | bytes 131104 | tf_op jit(solution)/shard_map/ppermute | solution.py:22
  73.4 1.9 %fusion.17 = f32[256,256]{0,1:T(8,128)S(1)} fusion(bf16[2432,256]{1,0:T(8,128)(2,1)} %shard_map.65, bf16[32,8,2432]{2,1,0:T(8,128)(2,1)S(1)} %all-to-all-done, bf16[256,256]{0,1:T(8,128)(2,1)S(1)} %collective-permute-done.3, bf16[256,256]{0,1:T(8,128)(2,1)S(1)} %collective-permute-done.1), kind=kOutput, calls=%fused_computation.16 | convolution fusion | flops 319029248 | bytes 3014656 | tf_op jit(solution)/shard_map/dot_general | solution.py:184
  75.4 1.9 %collective-permute-start.4 = (bf16[256,128]{0,1:T(8,128)(2,1)S(1)}, bf16[256,128]{0,1:T(8,128)(2,1)S(1)}, u32[]{:S(2)}, u32[]{:S(2)}) collective-permute-start(bf16[256,128]{0,1:T(8,128)(2,1)S(1)} %fusion.32), channel_id=1, source_target_pairs={{0,1},{1,2},{2,3},{3,4},{4,5},{5,6},{6,7},{7,8},{8,9},{9,10},{10,1... | collective-permute-start | bytes 196616 | tf_op jit(solution)/shard_map/ppermute | solution.py:22
  77.3 5.1 %collective-permute-start.5 = (bf16[256,128]{0,1:T(8,128)(2,1)S(1)}, bf16[256,128]{0,1:T(8,128)(2,1)S(1)}, u32[]{:S(2)}, u32[]{:S(2)}) collective-permute-start(bf16[256,128]{0,1:T(8,128)(2,1)S(1)} %fusion.32), channel_id=1, source_target_pairs={{0,11},{1,0},{2,1},{3,2},{4,3},{5,4},{6,5},{7,6},{8,7},{9,8},{10,9... | collective-permute-start | bytes 196616 | tf_op jit(solution)/shard_map/ppermute | solution.py:22
  82.4 1.9 %shard_map.67 = bf16[128,2432]{1,0:T(8,128)(2,1)} custom-call(s32[1]{0:T(128)} %bitcast.start_ref, bf16[1,128,7168]{2,1,0:T(8,128)(2,1)} %down_ref.1), custom_call_target="tpu_custom_call" | custom-call | flops 155648000 | bytes 1245184 | tf_op jit(solution)/shard_map/pallas_call | solution.py:67
  84.4 0.0 collective-permute-done.7
  84.4 0.0 collective-permute-done.4
  84.4 0.0 collective-permute-done.5
  84.4 1.9 %fusion = bf16[32,8,2432]{2,1,0:T(8,128)(2,1)S(1)} fusion(bf16[128,2432]{1,0:T(8,128)(2,1)S(1)} %collective-permute-done.7, bf16[128,2432]{1,0:T(8,128)(2,1)} %shard_map.67, bf16[128,2432]{1,0:T(8,128)(2,1)S(1)} %collective-permute-done.6, bf16[256,128]{0,1:T(8,128)(2,1)S(1)} %collective-permute-done.5, bf16[256,128]{0,1:T(8,128)(2,1)S(1)} %fusion.32, ...), kind=kOutput, calls=%fused_computation.1 | convolution fusion | flops 484966400 | bytes 3309568 | tf_op jit(solution)/shard_map/dot_general | solution.py:192
  86.3 0.0 copy-start
  86.3 41.7 %all_to_all.15 = bf16[32,8,2432]{2,1,0:T(8,128)(2,1)S(1)} all-to-all(bf16[32,8,2432]{2,1,0:T(8,128)(2,1)S(1)} %fusion), channel_id=1, replica_groups=mesh['ep'=32,'dp'=2,'tp'=12] {'ep'}, dimensions={0} | all-to-all | bytes 2490368 | tf_op jit(solution)/shard_map/all_to_all | solution.py:30
  128.0 0.0 copy-done
  128.0 0.3 fusion.6
  128.4 15.1 %all_to_all.16 = bf16[12,2,2432]{2,1,0:T(2,128)(2,1)S(1)} all-to-all(bf16[12,2,2432]{2,1,0:T(2,128)(2,1)S(1)} %reshape.39), channel_id=1, replica_groups=mesh['ep'=32,'dp'=2,'tp'=12] {'tp'}, dimensions={0} | all-to-all | bytes 233472 | tf_op jit(solution)/shard_map/all_to_all | solution.py:30
  143.6 0.1 add_convert_fusion
  143.7 0.6 pad_maximum_fusion
  (5 shorter events, 0.2 us)
Async XLA Ops:
  6.6 48.0 %all-to-all-start = ((bf16[32,8,2432]{2,1,0:T(8,128)(2,1)}), bf16[32,8,2432]{2,1,0:T(8,128)(2,1)S(1)}, u32[]{:S(2)}, u32[]{:S(2)}) async-start(bf16[32,8,2432]{2,1,0:T(8,128)(2,1)} %bitcast.35), calls=%async_computation | async-start | bytes 2490368 | tf_op jit(solution)/shard_map/all_to_all | solution.py:30
  22.0 26.8 %collective-permute-start = (bf16[2432,256]{1,0:T(8,128)(2,1)}, bf16[2432,256]{1,0:T(8,128)(2,1)S(1)}, u32[]{:S(2)}, u32[]{:S(2)}) collective-permute-start(bf16[2432,256]{1,0:T(8,128)(2,1)} %shard_map.64), channel_id=1, source_target_pairs={{0,1},{1,2},{2,3},{3,4},{4,5},{5,6},{6,7},{7,8},{8,9},{9,10},{10,1... | collective-permute-start | bytes 3735560 | tf_op jit(solution)/shard_map/ppermute | solution.py:22
  48.8 14.6 %collective-permute-start.2 = (bf16[2432,256]{1,0:T(8,128)(2,1)S(1)}, bf16[2432,256]{1,0:T(8,128)(2,1)}, u32[]{:S(2)}, u32[]{:S(2)}) collective-permute-start(bf16[2432,256]{1,0:T(8,128)(2,1)S(1)} %collective-permute-done), channel_id=1, source_target_pairs={{0,12},{12,0},{1,13},{13,1},{2,14},{14,2},{3,15},{15,3},{4,16},{16... | collective-permute-start | bytes 3735560 | tf_op jit(solution)/shard_map/ppermute | solution.py:26
  52.6 15.0 %collective-permute-start.6 = (bf16[128,2432]{1,0:T(8,128)(2,1)}, bf16[128,2432]{1,0:T(8,128)(2,1)S(1)}, u32[]{:S(2)}, u32[]{:S(2)}) collective-permute-start(bf16[128,2432]{1,0:T(8,128)(2,1)} %shard_map.66), channel_id=1, source_target_pairs={{0,1},{1,2},{2,3},{3,4},{4,5},{5,6},{6,7},{7,8},{8,9},{9,10},{10,1... | collective-permute-start | bytes 1867784 | tf_op jit(solution)/shard_map/ppermute | solution.py:22
  55.2 16.6 %collective-permute-start.1 = (bf16[256,256]{0,1:T(8,128)(2,1)S(1)}, bf16[256,256]{0,1:T(8,128)(2,1)S(1)}, u32[]{:S(2)}, u32[]{:S(2)}) collective-permute-start(bf16[256,256]{0,1:T(8,128)(2,1)S(1)} %fusion.20), channel_id=1, source_target_pairs={{0,11},{1,0},{2,1},{3,2},{4,3},{5,4},{6,5},{7,6},{8,7},{9,8},{10,9... | collective-permute-start | bytes 393224 | tf_op jit(solution)/shard_map/ppermute | solution.py:22
  65.3 8.1 %collective-permute-start.3 = (bf16[256,256]{0,1:T(8,128)(2,1)S(1)}, bf16[256,256]{0,1:T(8,128)(2,1)S(1)}, u32[]{:S(2)}, u32[]{:S(2)}) collective-permute-start(bf16[256,256]{0,1:T(8,128)(2,1)S(1)} %fusion.23), channel_id=1, source_target_pairs={{0,1},{1,2},{2,3},{3,4},{4,5},{5,6},{6,7},{7,8},{8,9},{9,10},{10,1... | collective-permute-start | bytes 393224 | tf_op jit(solution)/shard_map/ppermute | solution.py:22
  67.6 16.8 %collective-permute-start.7 = (bf16[128,2432]{1,0:T(8,128)(2,1)S(1)}, bf16[128,2432]{1,0:T(8,128)(2,1)S(1)}, u32[]{:S(2)}, u32[]{:S(2)}) collective-permute-start(bf16[128,2432]{1,0:T(8,128)(2,1)S(1)} %collective-permute-done.6), channel_id=1, source_target_pairs={{0,12},{12,0},{1,13},{13,1},{2,14},{14,2},{3,15},{15,3},{4,16},{16... | collective-permute-start | bytes 1867784 | tf_op jit(solution)/shard_map/ppermute | solution.py:26
  75.4 9.0 %collective-permute-start.4 = (bf16[256,128]{0,1:T(8,128)(2,1)S(1)}, bf16[256,128]{0,1:T(8,128)(2,1)S(1)}, u32[]{:S(2)}, u32[]{:S(2)}) collective-permute-start(bf16[256,128]{0,1:T(8,128)(2,1)S(1)} %fusion.32), channel_id=1, source_target_pairs={{0,1},{1,2},{2,3},{3,4},{4,5},{5,6},{6,7},{7,8},{8,9},{9,10},{10,1... | collective-permute-start | bytes 196616 | tf_op jit(solution)/shard_map/ppermute | solution.py:22
  77.3 7.1 %collective-permute-start.5 = (bf16[256,128]{0,1:T(8,128)(2,1)S(1)}, bf16[256,128]{0,1:T(8,128)(2,1)S(1)}, u32[]{:S(2)}, u32[]{:S(2)}) collective-permute-start(bf16[256,128]{0,1:T(8,128)(2,1)S(1)} %fusion.32), channel_id=1, source_target_pairs={{0,11},{1,0},{2,1},{3,2},{4,3},{5,4},{6,5},{7,6},{8,7},{9,8},{10,9... | collective-permute-start | bytes 196616 | tf_op jit(solution)/shard_map/ppermute | solution.py:22
  86.3 41.7 %copy-start = (bf16[2,24,256]{2,1,0:T(8,128)(2,1)S(1)}, bf16[2,24,256]{2,1,0:T(8,128)(2,1)}, u32[]{:S(2)}) copy-start(bf16[2,24,256]{2,1,0:T(8,128)(2,1)} %get-tuple-element.14) | copy-start | bytes 73732

commit v5 on v4

--- a/solution.py
+++ b/solution.py
@@ -10,6 +10,7 @@
 MOST = 8
 LANES = 128
 PARTS = 3
+BLOCK = 5 * LANES
 
 
 def shift(array, step):
@@ -89,62 +90,98 @@
     return cut(cut_down, piece_start(index, width), (down_weight,), shape)
 
 
-def dispatch_kernel(where_ref, ids_ref, route_ref, tokens_ref, rows_ref, weights_ref, held, sem):
-    tokens, piece = held.shape
-    capacity = rows_ref.shape[0]
-    start = pl.multiple_of(where_ref[0], LANES)
-    copy = pltpu.make_async_copy(tokens_ref.at[:, pl.ds(start, piece)], held, sem.at[0])
-    copy.start()
-    lane = lax.broadcasted_iota(jnp.int32, (tokens, capacity), 1)
+def dispatch_kernel(start_ref, ids_ref, tokens_ref, rows_ref, held, chosen, sem):
+    capacity, count = chosen.shape
+    width = tokens_ref.shape[1]
+    piece = piece_width(width)
+    block = rows_ref.shape[1]
+    step = pl.program_id(0)
+
+    @pl.when(step == 0)
+    def _():
+        start = pl.multiple_of(start_ref[0], LANES)
+        copy = pltpu.make_async_copy(
+            tokens_ref.at[:, pl.ds(start, piece)], held.at[:, pl.ds(0, piece)], sem.at[0]
+        )
+        copy.start()
+        line = lax.broadcasted_iota(jnp.int32, (capacity, count), 0)
+        expert, slot = line // MOST, line % MOST
+        member = jnp.zeros((capacity, count), jnp.float32)
+        for k in range(TOP):
+            member = jnp.where(ids_ref[k : k + 1, :] == expert, 1.0, member)
+        row = lax.broadcasted_iota(jnp.int32, (count, count), 0)
+        column = lax.broadcasted_iota(jnp.int32, (count, count), 1)
+        before = jnp.where(row < column, 1.0, 0.0).astype(jnp.bfloat16)
+        earlier = jnp.dot(member.astype(jnp.bfloat16), before, preferred_element_type=jnp.float32)
+        here = earlier == slot.astype(jnp.float32)
+        chosen[...] = jnp.where(here, member, 0.0).astype(jnp.bfloat16)
+        copy.wait()
+
+    first = jnp.where(start_ref[0] == width - piece, PARTS * piece - width, 0)
+    source = held[:, pl.ds(pl.multiple_of(step * block, LANES), block)]
+    wide = lax.broadcasted_iota(jnp.int32, source.shape, 1) + step * block
+    source = jnp.where(wide >= first, source.astype(jnp.float32), 0.0).astype(jnp.bfloat16)
+    rows_ref[...] = jnp.dot(chosen[...], source, preferred_element_type=jnp.float32).astype(
+        jnp.bfloat16
+    )
+
+
+def dispatch(tokens, expert_ids, index):
+    count, width = tokens.shape
+    piece, capacity = piece_width(width), EXPERTS * MOST
+    steps = -(-piece // BLOCK)
+    return pl.pallas_call(
+        dispatch_kernel,
+        grid=(steps,),
+        out_shape=jax.ShapeDtypeStruct((capacity, piece), jnp.bfloat16),
+        in_specs=[
+            pl.BlockSpec(memory_space=pltpu.SMEM),
+            pl.BlockSpec((TOP, count), lambda i: (0, 0)),
+            pl.BlockSpec(memory_space=pl.ANY),
+        ],
+        out_specs=pl.BlockSpec((capacity, BLOCK), lambda i: (0, i)),
+        scratch_shapes=[
+            pltpu.VMEM((count, steps * BLOCK), jnp.bfloat16),
+            pltpu.VMEM((capacity, count), jnp.bfloat16),
+            pltpu.SemaphoreType.DMA((1,)),
+        ],
+        cost_estimate=pl.CostEstimate(
+            flops=2 * count * piece * capacity, bytes_accessed=2**21, transcendentals=0
+        ),
+        name="dispatch",
+    )(piece_start(index, width).reshape(1), expert_ids.T, tokens)
+
+
+def weigh_kernel(ids_ref, route_ref, weights_ref):
+    count, capacity = weights_ref.shape[1:]
+    lane = lax.broadcasted_iota(jnp.int32, (count, capacity), 1)
     expert, slot = lane // MOST, lane % MOST
-    member = jnp.zeros((tokens, capacity), jnp.float32)
-    weight = jnp.zeros((tokens, capacity), jnp.float32)
+    member = jnp.zeros((count, capacity), jnp.float32)
+    weight = jnp.zeros((count, capacity), jnp.float32)
     for k in range(TOP):
         same = ids_ref[:, k : k + 1] == expert
         member = jnp.where(same, 1.0, member)
         weight = jnp.where(same, route_ref[:, k : k + 1], weight)
-    row = lax.broadcasted_iota(jnp.int32, (tokens, tokens), 0)
-    column = lax.broadcasted_iota(jnp.int32, (tokens, tokens), 1)
+    row = lax.broadcasted_iota(jnp.int32, (count, count), 0)
+    column = lax.broadcasted_iota(jnp.int32, (count, count), 1)
     above = jnp.where(column < row, 1.0, 0.0).astype(jnp.bfloat16)
     earlier = jnp.dot(above, member.astype(jnp.bfloat16), preferred_element_type=jnp.float32)
-    here = earlier == slot.astype(jnp.float32)
-    chosen = jnp.where(here, member, 0.0).astype(jnp.bfloat16)
-    weight = jnp.where(here, weight, 0.0)
+    weight = jnp.where(earlier == slot.astype(jnp.float32), weight, 0.0)
     high = weight.astype(jnp.bfloat16)
     weights_ref[0] = high
     weights_ref[1] = (weight - high.astype(jnp.float32)).astype(jnp.bfloat16)
-    copy.wait()
-    wide = lax.broadcasted_iota(jnp.int32, (tokens, piece), 1)
-    source = jnp.where(wide >= where_ref[1], held[...].astype(jnp.float32), 0.0)
-    rows_ref[...] = lax.dot_general(
-        chosen,
-        source.astype(jnp.bfloat16),
-        (((0,), (0,)), ((), ())),
-        preferred_element_type=jnp.float32,
-    ).astype(jnp.bfloat16)
-
-
-def dispatch(tokens, expert_ids, route_weight, index):
-    count, width = tokens.shape
-    piece, capacity = piece_width(width), EXPERTS * MOST
-    start = piece_start(index, width)
-    where = jnp.stack([start, lax.rem(index, PARTS) * piece - start])
+
+
+def weigh(expert_ids, route_weight):
+    shape = (2, expert_ids.shape[0], EXPERTS * MOST)
     return pl.pallas_call(
-        dispatch_kernel,
-        out_shape=(
-            jax.ShapeDtypeStruct((capacity, piece), jnp.bfloat16),
-            jax.ShapeDtypeStruct((2, count, capacity), jnp.bfloat16),
+        weigh_kernel,
+        out_shape=jax.ShapeDtypeStruct(shape, jnp.bfloat16),
+        cost_estimate=pl.CostEstimate(
+            flops=2**26, bytes_accessed=2**15, transcendentals=0
         ),
-        in_specs=[pl.BlockSpec(memory_space=pltpu.SMEM)]
-        + [pl.BlockSpec(memory_space=pltpu.VMEM)] * 2
-        + [pl.BlockSpec(memory_space=pl.ANY)],
-        out_specs=(pl.BlockSpec(memory_space=pltpu.VMEM),) * 2,
-        scratch_shapes=[pltpu.VMEM((count, piece), jnp.bfloat16), pltpu.SemaphoreType.DMA((1,))],
-        cost_estimate=pl.CostEstimate(
-            flops=2 * count * piece * capacity, bytes_accessed=2**21, transcendentals=0
-        ),
-        name="dispatch",
-    )(where, expert_ids, route_weight, tokens)
+        name="weigh",
+    )(expert_ids, route_weight)
 
 
 def combine(weights, returned):
@@ -163,9 +200,11 @@
     here = lax.axis_index("tp")
     target = lax.rem(here + jnp.where(lax.axis_index("dp") == 0, 1, tp_size - 1), tp_size)
 
-    outgoing, weights = dispatch(tokens, expert_ids, route_weight, here)
-    outgoing, gate_weight, up_weight, down_weight = lax.optimization_barrier(
-        (outgoing, gate_weight, up_weight, down_weight)
+    outgoing = dispatch(tokens, expert_ids, here)
+    outgoing, gate_weight, up_weight, down_weight, expert_ids, route_weight = (
+        lax.optimization_barrier(
+            (outgoing, gate_weight, up_weight, down_weight, expert_ids, route_weight)
+        )
     )
     received = exchange(outgoing.reshape(EXPERTS, MOST, piece), "ep")
     received = received.reshape(capacity, piece)
@@ -174,11 +213,9 @@
     gate_up_far = swap(gate_up_near)
     down_near = shift(down_piece(down_weight, target), 1)
     down_far = swap(down_near)
-    gate_weight, up_weight, down_weight, _ = lax.optimization_barrier(
-        (gate_weight, up_weight, down_weight, gate_up_near)
-    )
     gate_up_here = gate_up_piece(gate_weight, up_weight, here)
     down_here = down_piece(down_weight, here)
+    weights = weigh(expert_ids, route_weight)
 
     def product(weights):
         return jnp.dot(received, weights, preferred_element_type=jnp.float32)

time: 145 us -> 153 us (1.055)
  the two profiles are of different devices: /device:TPU:8 before, /device:TPU:4 now
where the time goes in v5:
time: 153 us; the launch traced here: 152 us
  waiting for transfers between devices  68.3 us (45%)
  starting transfers between devices  43.7 us (29%)
  blocking collectives  16.4 us (11%)
  Pallas kernels  13.9 us (9%)
  matrix products  7.43 us (5%)
    ppermute x6, waiting for transfers between devices, shift(): return lax.ppermute(array, ('dp', 'tp'), pairs)  39 us
    all_to_all x2, waiting for transfers between devices, exchange(): return lax.all_to_all(array, axis, split_axis=0, concat_axis=0, tiled=True)  29.3 us
    all_to_all x2, starting transfers between devices, exchange(): return lax.all_to_all(array, axis, split_axis=0, concat_axis=0, tiled=True)  23 us
    ppermute x6, starting transfers between devices, shift(): return lax.ppermute(array, ('dp', 'tp'), pairs)  16.9 us
    all_to_all x1, blocking collectives, exchange(): return lax.all_to_all(array, axis, split_axis=0, concat_axis=0, tiled=True)  16.4 us
    pallas_call x4, Pallas kernels, cut(): pl.pallas_call(kernel, out_shape=jax.ShapeDtypeStruct(shape, jnp.bfloat16...  8.48 us
    pallas_call x1, Pallas kernels, dispatch(): pl.pallas_call(dispatch_kernel, grid=(steps,), out_shape=jax.ShapeDtypeSt...  3.84 us
    ppermute x2, starting transfers between devices, swap(): return lax.ppermute(array, 'dp', [(0, 1), (1, 0)])  3.82 us
  transfers between devices with their start and end apart: 10, of which 4 were waited for; matrix products, arithmetic and copies ran while one was open for 3% of the time, Pallas kernels for 7%

profile of v5, /device:TPU:4, one launch (start us, length us, event | category | flops | bytes accessed | tf_op | source)
XLA Modules:
  0.0 152.3 jit_solution(2987656678376528472)
XLA Ops:
  0.0 3.8 %dispatch.1 = bf16[256,2432]{1,0:T(8,128)(2,1)} custom-call(s32[1]{0:T(128)} %bitcast.start_ref, s32[8,24]{1,0:T(8,128)} %bitcast.33, bf16[24,7168]{1,0:T(8,128)(2,1)} %tokens_ref.1), custom_call_target="tpu_custom_call" | custom-call | flops 29884416 | bytes 2097152 | tf_op jit(solution)/shard_map/dispatch/pallas_call | solution.py:133
  3.8 13.1 %all-to-all-start = ((bf16[32,8,2432]{2,1,0:T(8,128)(2,1)}), bf16[32,8,2432]{2,1,0:T(8,128)(2,1)S(1)}, u32[]{:S(2)}, u32[]{:S(2)}) async-start(bf16[32,8,2432]{2,1,0:T(8,128)(2,1)} %bitcast.31), calls=%async_computation | async-start | bytes 2490368 | tf_op jit(solution)/shard_map/all_to_all | solution.py:31
  17.0 2.3 %shard_map.65 = bf16[2432,256]{1,0:T(8,128)(2,1)} custom-call(s32[1]{0:T(128)} %bitcast.5.start_ref, bf16[1,7168,128]{2,1,0:T(8,128)(2,1)} %gate_ref.1, bf16[1,7168,128]{2,1,0:T(8,128)(2,1)} %up_ref.1), custom_call_target="tpu_custom_call" | custom-call | flops 311296000 | bytes 2490368 | tf_op jit(solution)/shard_map/pallas_call | solution.py:68
  19.3 1.9 %collective-permute-start = (bf16[2432,256]{1,0:T(8,128)(2,1)}, bf16[2432,256]{1,0:T(8,128)(2,1)S(1)}, u32[]{:S(2)}, u32[]{:S(2)}) collective-permute-start(bf16[2432,256]{1,0:T(8,128)(2,1)} %shard_map.65), channel_id=1, source_target_pairs={{0,1},{1,2},{2,3},{3,4},{4,5},{5,6},{6,7},{7,8},{8,9},{9,10},{10,1... | collective-permute-start | bytes 3735560 | tf_op jit(solution)/shard_map/ppermute | solution.py:23
  21.2 24.9 %collective-permute-done = bf16[2432,256]{1,0:T(8,128)(2,1)S(1)} collective-permute-done((bf16[2432,256]{1,0:T(8,128)(2,1)}, bf16[2432,256]{1,0:T(8,128)(2,1)S(1)}, u32[]{:S(2)}, u32[]{:S(2)}) %collective-permute-start) | collective-permute-done | bytes 1245216 | tf_op jit(solution)/shard_map/ppermute | solution.py:23
  46.1 1.9 %collective-permute-start.2 = (bf16[2432,256]{1,0:T(8,128)(2,1)S(1)}, bf16[2432,256]{1,0:T(8,128)(2,1)}, u32[]{:S(2)}, u32[]{:S(2)}) collective-permute-start(bf16[2432,256]{1,0:T(8,128)(2,1)S(1)} %collective-permute-done), channel_id=1, source_target_pairs={{0,12},{12,0},{1,13},{13,1},{2,14},{14,2},{3,15},{15,3},{4,16},{16... | collective-permute-start | bytes 3735560 | tf_op jit(solution)/shard_map/ppermute | solution.py:27
  48.0 1.9 %shard_map.66 = bf16[128,2432]{1,0:T(8,128)(2,1)} custom-call(s32[1]{0:T(128)} %bitcast.5.start_ref, bf16[1,128,7168]{2,1,0:T(8,128)(2,1)} %down_ref.1), custom_call_target="tpu_custom_call" | custom-call | flops 155648000 | bytes 1245184 | tf_op jit(solution)/shard_map/pallas_call | solution.py:68
  50.0 1.9 %collective-permute-start.6 = (bf16[128,2432]{1,0:T(8,128)(2,1)}, bf16[128,2432]{1,0:T(8,128)(2,1)S(1)}, u32[]{:S(2)}, u32[]{:S(2)}) collective-permute-start(bf16[128,2432]{1,0:T(8,128)(2,1)} %shard_map.66), channel_id=1, source_target_pairs={{0,1},{1,2},{2,3},{3,4},{4,5},{5,6},{6,7},{7,8},{8,9},{9,10},{10,1... | collective-permute-start | bytes 1867784 | tf_op jit(solution)/shard_map/ppermute | solution.py:23
  51.9 2.3 %shard_map.64 = bf16[2432,256]{1,0:T(8,128)(2,1)} custom-call(s32[1]{0:T(128)} %bitcast.start_ref, bf16[1,7168,128]{2,1,0:T(8,128)(2,1)} %gate_ref.1, bf16[1,7168,128]{2,1,0:T(8,128)(2,1)} %up_ref.1), custom_call_target="tpu_custom_call" | custom-call | flops 311296000 | bytes 2490368 | tf_op jit(solution)/shard_map/pallas_call | solution.py:68
  54.2 9.3 %collective-permute-done.6 = bf16[128,2432]{1,0:T(8,128)(2,1)S(1)} collective-permute-done((bf16[128,2432]{1,0:T(8,128)(2,1)}, bf16[128,2432]{1,0:T(8,128)(2,1)S(1)}, u32[]{:S(2)}, u32[]{:S(2)}) %collective-permute-start.6) | collective-permute-done | bytes 622624 | tf_op jit(solution)/shard_map/ppermute | solution.py:23
  63.5 1.9 %collective-permute-start.7 = (bf16[128,2432]{1,0:T(8,128)(2,1)S(1)}, bf16[128,2432]{1,0:T(8,128)(2,1)}, u32[]{:S(2)}, u32[]{:S(2)}) collective-permute-start(bf16[128,2432]{1,0:T(8,128)(2,1)S(1)} %collective-permute-done.6), channel_id=1, source_target_pairs={{0,12},{12,0},{1,13},{13,1},{2,14},{14,2},{3,15},{15,3},{4,16},{16... | collective-permute-start | bytes 1867784 | tf_op jit(solution)/shard_map/ppermute | solution.py:27
  65.4 0.0 all-to-all-done
  65.4 0.6 fusion.14
  66.1 0.0 copy-start
  66.1 3.4 %collective-permute-start.1 = (bf16[256,256]{0,1:T(8,128)(2,1)S(1)}, bf16[256,256]{0,1:T(8,128)(2,1)S(1)}, u32[]{:S(2)}, u32[]{:S(2)}) collective-permute-start(bf16[256,256]{0,1:T(8,128)(2,1)S(1)} %fusion.14), channel_id=1, source_target_pairs={{0,11},{1,0},{2,1},{3,2},{4,3},{5,4},{6,5},{7,6},{8,7},{9,8},{10,9... | collective-permute-start | bytes 393224 | tf_op jit(solution)/shard_map/ppermute | solution.py:23
  69.5 0.0 collective-permute-done.2
  69.5 1.9 %fusion.17 = bf16[256,256]{0,1:T(8,128)(2,1)S(1)} fusion(bf16[2432,256]{1,0:T(8,128)(2,1)} %collective-permute-done.2, bf16[32,8,2432]{2,1,0:T(8,128)(2,1)S(1)} %all-to-all-done), kind=kOutput, calls=%fused_computation.16 | convolution fusion | flops 318832640 | bytes 2621440 | tf_op jit(solution)/shard_map/dot_general | solution.py:221
  71.4 2.6 %collective-permute-start.3 = (bf16[256,256]{0,1:T(8,128)(2,1)S(1)}, bf16[256,256]{0,1:T(8,128)(2,1)S(1)}, u32[]{:S(2)}, u32[]{:S(2)}) collective-permute-start(bf16[256,256]{0,1:T(8,128)(2,1)S(1)} %fusion.17), channel_id=1, source_target_pairs={{0,1},{1,2},{2,3},{3,4},{4,5},{5,6},{6,7},{7,8},{8,9},{9,10},{10,1... | collective-permute-start | bytes 393224 | tf_op jit(solution)/shard_map/ppermute | solution.py:23
  74.0 0.0 copy-done
  74.0 0.6 fusion.12
  74.7 0.0 collective-permute-done.1
  74.7 4.8 %collective-permute-done.3 = bf16[256,256]{0,1:T(8,128)(2,1)S(1)} collective-permute-done((bf16[256,256]{0,1:T(8,128)(2,1)S(1)}, bf16[256,256]{0,1:T(8,128)(2,1)S(1)}, u32[]{:S(2)}, u32[]{:S(2)}) %collective-permute-start.3) | collective-permute-done | bytes 131104 | tf_op jit(solution)/shard_map/ppermute | solution.py:23
  79.6 1.9 %collective-permute-start.4 = (bf16[256,128]{0,1:T(8,128)(2,1)S(1)}, bf16[256,128]{0,1:T(8,128)(2,1)S(1)}, u32[]{:S(2)}, u32[]{:S(2)}) collective-permute-start(bf16[256,128]{0,1:T(8,128)(2,1)S(1)} %fusion.26), channel_id=1, source_target_pairs={{0,1},{1,2},{2,3},{3,4},{4,5},{5,6},{6,7},{7,8},{8,9},{9,10},{10,1... | collective-permute-start | bytes 196616 | tf_op jit(solution)/shard_map/ppermute | solution.py:23
  81.5 5.1 %collective-permute-start.5 = (bf16[256,128]{0,1:T(8,128)(2,1)S(1)}, bf16[256,128]{0,1:T(8,128)(2,1)S(1)}, u32[]{:S(2)}, u32[]{:S(2)}) collective-permute-start(bf16[256,128]{0,1:T(8,128)(2,1)S(1)} %fusion.26), channel_id=1, source_target_pairs={{0,11},{1,0},{2,1},{3,2},{4,3},{5,4},{6,5},{7,6},{8,7},{9,8},{10,9... | collective-permute-start | bytes 196616 | tf_op jit(solution)/shard_map/ppermute | solution.py:23
  86.6 1.9 %shard_map.67 = bf16[128,2432]{1,0:T(8,128)(2,1)} custom-call(s32[1]{0:T(128)} %bitcast.start_ref, bf16[1,128,7168]{2,1,0:T(8,128)(2,1)} %down_ref.1), custom_call_target="tpu_custom_call" | custom-call | flops 155648000 | bytes 1245184 | tf_op jit(solution)/shard_map/pallas_call | solution.py:68
  88.6 0.0 collective-permute-done.7
  88.6 0.0 collective-permute-done.4
  88.6 0.0 collective-permute-done.5
  88.6 3.2 %fusion = bf16[32,8,2432]{2,1,0:T(8,128)(2,1)} fusion(bf16[128,2432]{1,0:T(8,128)(2,1)} %collective-permute-done.7, bf16[128,2432]{1,0:T(8,128)(2,1)} %shard_map.67, bf16[128,2432]{1,0:T(8,128)(2,1)S(1)} %collective-permute-done.6, bf16[256,128]{0,1:T(8,128)(2,1)S(1)} %collective-permute-done.5, bf16[256,128]{0,1:T(8,128)(2,1)S(1)} %fusion.26, ...), kind=kOutput, calls=%fused_computation.1 | convolution fusion | flops 484966400 | bytes 3309568 | tf_op jit(solution)/shard_map/dot_general | solution.py:229
  91.8 0.0 copy-start.1
  91.8 0.0 copy-start.2
  91.8 9.9 %all-to-all-start.1 = ((bf16[32,8,2432]{2,1,0:T(8,128)(2,1)}), bf16[32,8,2432]{2,1,0:T(8,128)(2,1)S(1)}, u32[]{:S(2)}, u32[]{:S(2)}) async-start(bf16[32,8,2432]{2,1,0:T(8,128)(2,1)} %fusion), calls=%async_computation.1 | async-start | bytes 2490368 | tf_op jit(solution)/shard_map/all_to_all | solution.py:31
  101.7 0.0 copy-done.1
  101.7 0.7 copy.7.ids_ref
  102.4 0.0 copy-done.2
  102.4 0.7 copy.8.route_ref
  103.1 1.6 %weigh.1 = bf16[2,24,256]{2,1,0:T(8,128)(2,1)} custom-call(s32[24,8]{1,0:T(8,128)} %copy.7.ids_ref, f32[24,8]{1,0:T(8,128)} %copy.8.route_ref), custom_call_target="tpu_custom_call" | custom-call | flops 67108864 | bytes 32768 | tf_op jit(solution)/shard_map/weigh/pallas_call | solution.py:177
  104.6 29.3 %all-to-all-done.1 = bf16[32,8,2432]{2,1,0:T(8,128)(2,1)S(1)} async-done(((bf16[32,8,2432]{2,1,0:T(8,128)(2,1)}), bf16[32,8,2432]{2,1,0:T(8,128)(2,1)S(1)}, u32[]{:S(2)}, u32[]{:S(2)}) %all-to-all-start.1) | async-done | bytes 1245216 | tf_op jit(solution)/shard_map/all_to_all | solution.py:31
  133.9 1.1 fusion.6
  135.1 16.4 %all_to_all.15 = bf16[12,2,2432]{2,1,0:T(2,128)(2,1)S(1)} all-to-all(bf16[12,2,2432]{2,1,0:T(2,128)(2,1)S(1)} %reshape.43), channel_id=1, replica_groups=mesh['ep'=32,'dp'=2,'tp'=12] {'tp'}, dimensions={0} | all-to-all | bytes 233472 | tf_op jit(solution)/shard_map/all_to_all | solution.py:31
  151.5 0.1 add_convert_fusion
  151.6 0.6 pad_maximum_fusion
  (6 shorter events, 0.2 us)
Async XLA Ops:
  3.8 61.6 %all-to-all-start = ((bf16[32,8,2432]{2,1,0:T(8,128)(2,1)}), bf16[32,8,2432]{2,1,0:T(8,128)(2,1)S(1)}, u32[]{:S(2)}, u32[]{:S(2)}) async-start(bf16[32,8,2432]{2,1,0:T(8,128)(2,1)} %bitcast.31), calls=%async_computation | async-start | bytes 2490368 | tf_op jit(solution)/shard_map/all_to_all | solution.py:31
  19.3 26.8 %collective-permute-start = (bf16[2432,256]{1,0:T(8,128)(2,1)}, bf16[2432,256]{1,0:T(8,128)(2,1)S(1)}, u32[]{:S(2)}, u32[]{:S(2)}) collective-permute-start(bf16[2432,256]{1,0:T(8,128)(2,1)} %shard_map.65), channel_id=1, source_target_pairs={{0,1},{1,2},{2,3},{3,4},{4,5},{5,6},{6,7},{7,8},{8,9},{9,10},{10,1... | collective-permute-start | bytes 3735560 | tf_op jit(solution)/shard_map/ppermute | solution.py:23
  46.1 23.4 %collective-permute-start.2 = (bf16[2432,256]{1,0:T(8,128)(2,1)S(1)}, bf16[2432,256]{1,0:T(8,128)(2,1)}, u32[]{:S(2)}, u32[]{:S(2)}) collective-permute-start(bf16[2432,256]{1,0:T(8,128)(2,1)S(1)} %collective-permute-done), channel_id=1, source_target_pairs={{0,12},{12,0},{1,13},{13,1},{2,14},{14,2},{3,15},{15,3},{4,16},{16... | collective-permute-start | bytes 3735560 | tf_op jit(solution)/shard_map/ppermute | solution.py:27
  50.0 13.5 %collective-permute-start.6 = (bf16[128,2432]{1,0:T(8,128)(2,1)}, bf16[128,2432]{1,0:T(8,128)(2,1)S(1)}, u32[]{:S(2)}, u32[]{:S(2)}) collective-permute-start(bf16[128,2432]{1,0:T(8,128)(2,1)} %shard_map.66), channel_id=1, source_target_pairs={{0,1},{1,2},{2,3},{3,4},{4,5},{5,6},{6,7},{7,8},{8,9},{9,10},{10,1... | collective-permute-start | bytes 1867784 | tf_op jit(solution)/shard_map/ppermute | solution.py:23
  63.5 25.1 %collective-permute-start.7 = (bf16[128,2432]{1,0:T(8,128)(2,1)S(1)}, bf16[128,2432]{1,0:T(8,128)(2,1)}, u32[]{:S(2)}, u32[]{:S(2)}) collective-permute-start(bf16[128,2432]{1,0:T(8,128)(2,1)S(1)} %collective-permute-done.6), channel_id=1, source_target_pairs={{0,12},{12,0},{1,13},{13,1},{2,14},{14,2},{3,15},{15,3},{4,16},{16... | collective-permute-start | bytes 1867784 | tf_op jit(solution)/shard_map/ppermute | solution.py:27
  66.1 7.9 %copy-start = (bf16[2432,256]{1,0:T(8,128)(2,1)S(1)}, bf16[2432,256]{1,0:T(8,128)(2,1)}, u32[]{:S(2)}) copy-start(bf16[2432,256]{1,0:T(8,128)(2,1)} %shard_map.64) | copy-start | bytes 3735556
  66.1 8.6 %collective-permute-start.1 = (bf16[256,256]{0,1:T(8,128)(2,1)S(1)}, bf16[256,256]{0,1:T(8,128)(2,1)S(1)}, u32[]{:S(2)}, u32[]{:S(2)}) collective-permute-start(bf16[256,256]{0,1:T(8,128)(2,1)S(1)} %fusion.14), channel_id=1, source_target_pairs={{0,11},{1,0},{2,1},{3,2},{4,3},{5,4},{6,5},{7,6},{8,7},{9,8},{10,9... | collective-permute-start | bytes 393224 | tf_op jit(solution)/shard_map/ppermute | solution.py:23
  71.4 8.1 %collective-permute-start.3 = (bf16[256,256]{0,1:T(8,128)(2,1)S(1)}, bf16[256,256]{0,1:T(8,128)(2,1)S(1)}, u32[]{:S(2)}, u32[]{:S(2)}) collective-permute-start(bf16[256,256]{0,1:T(8,128)(2,1)S(1)} %fusion.17), channel_id=1, source_target_pairs={{0,1},{1,2},{2,3},{3,4},{4,5},{5,6},{6,7},{7,8},{8,9},{9,10},{10,1... | collective-permute-start | bytes 393224 | tf_op jit(solution)/shard_map/ppermute | solution.py:23
  79.6 9.0 %collective-permute-start.4 = (bf16[256,128]{0,1:T(8,128)(2,1)S(1)}, bf16[256,128]{0,1:T(8,128)(2,1)S(1)}, u32[]{:S(2)}, u32[]{:S(2)}) collective-permute-start(bf16[256,128]{0,1:T(8,128)(2,1)S(1)} %fusion.26), channel_id=1, source_target_pairs={{0,1},{1,2},{2,3},{3,4},{4,5},{5,6},{6,7},{7,8},{8,9},{9,10},{10,1... | collective-permute-start | bytes 196616 | tf_op jit(solution)/shard_map/ppermute | solution.py:23
  81.5 7.1 %collective-permute-start.5 = (bf16[256,128]{0,1:T(8,128)(2,1)S(1)}, bf16[256,128]{0,1:T(8,128)(2,1)S(1)}, u32[]{:S(2)}, u32[]{:S(2)}) collective-permute-start(bf16[256,128]{0,1:T(8,128)(2,1)S(1)} %fusion.26), channel_id=1, source_target_pairs={{0,11},{1,0},{2,1},{3,2},{4,3},{5,4},{6,5},{7,6},{8,7},{9,8},{10,9... | collective-permute-start | bytes 196616 | tf_op jit(solution)/shard_map/ppermute | solution.py:23
  91.8 9.9 %copy-start.1 = (s32[24,8]{0,1:T(8,128)S(1)}, s32[24,8]{0,1:T(8,128)}, u32[]{:S(2)}) copy-start(s32[24,8]{0,1:T(8,128)} %param.7) | copy-start | bytes 2308
  91.8 10.6 %copy-start.2 = (f32[24,8]{0,1:T(8,128)S(1)}, f32[24,8]{0,1:T(8,128)}, u32[]{:S(2)}) copy-start(f32[24,8]{0,1:T(8,128)} %param.8) | copy-start | bytes 2308
  91.8 42.1 %all-to-all-start.1 = ((bf16[32,8,2432]{2,1,0:T(8,128)(2,1)}), bf16[32,8,2432]{2,1,0:T(8,128)(2,1)S(1)}, u32[]{:S(2)}, u32[]{:S(2)}) async-start(bf16[32,8,2432]{2,1,0:T(8,128)(2,1)} %fusion), calls=%async_computation.1 | async-start | bytes 2490368 | tf_op jit(solution)/shard_map/all_to_all | solution.py:31

commit v6 on v5

--- a/solution.py
+++ b/solution.py
@@ -90,7 +90,7 @@
     return cut(cut_down, piece_start(index, width), (down_weight,), shape)
 
 
-def dispatch_kernel(start_ref, ids_ref, tokens_ref, rows_ref, held, chosen, sem):
+def dispatch_kernel(start_ref, ids_ref, tokens_ref, rows_ref, ids, held, chosen, sem):
     capacity, count = chosen.shape
     width = tokens_ref.shape[1]
     piece = piece_width(width)
@@ -99,6 +99,8 @@
 
     @pl.when(step == 0)
     def _():
+        ids_copy = pltpu.make_async_copy(ids_ref, ids, sem.at[1])
+        ids_copy.start()
         start = pl.multiple_of(start_ref[0], LANES)
         copy = pltpu.make_async_copy(
             tokens_ref.at[:, pl.ds(start, piece)], held.at[:, pl.ds(0, piece)], sem.at[0]
@@ -107,8 +109,9 @@
         line = lax.broadcasted_iota(jnp.int32, (capacity, count), 0)
         expert, slot = line // MOST, line % MOST
         member = jnp.zeros((capacity, count), jnp.float32)
+        ids_copy.wait()
         for k in range(TOP):
-            member = jnp.where(ids_ref[k : k + 1, :] == expert, 1.0, member)
+            member = jnp.where(ids[k : k + 1, :] == expert, 1.0, member)
         row = lax.broadcasted_iota(jnp.int32, (count, count), 0)
         column = lax.broadcasted_iota(jnp.int32, (count, count), 1)
         before = jnp.where(row < column, 1.0, 0.0).astype(jnp.bfloat16)
@@ -136,14 +139,15 @@
         out_shape=jax.ShapeDtypeStruct((capacity, piece), jnp.bfloat16),
         in_specs=[
             pl.BlockSpec(memory_space=pltpu.SMEM),
-            pl.BlockSpec((TOP, count), lambda i: (0, 0)),
+            pl.BlockSpec(memory_space=pl.ANY),
             pl.BlockSpec(memory_space=pl.ANY),
         ],
         out_specs=pl.BlockSpec((capacity, BLOCK), lambda i: (0, i)),
         scratch_shapes=[
+            pltpu.VMEM((TOP, count), jnp.int32),
             pltpu.VMEM((count, steps * BLOCK), jnp.bfloat16),
             pltpu.VMEM((capacity, count), jnp.bfloat16),
-            pltpu.SemaphoreType.DMA((1,)),
+            pltpu.SemaphoreType.DMA((2,)),
         ],
         cost_estimate=pl.CostEstimate(
             flops=2 * count * piece * capacity, bytes_accessed=2**21, transcendentals=0

time: 153 us -> 153 us (level)
  no operation moved by 1% of the time
where the time goes in v6:
time: 153 us; the launch traced here: 152 us
  waiting for transfers between devices  68.3 us (45%)
  starting transfers between devices  43.7 us (29%)
  blocking collectives  16.4 us (11%)
  Pallas kernels  13.2 us (9%)
  matrix products  7.43 us (5%)
    ppermute x6, waiting for transfers between devices, shift(): return lax.ppermute(array, ('dp', 'tp'), pairs)  39 us
    all_to_all x2, waiting for transfers between devices, exchange(): return lax.all_to_all(array, axis, split_axis=0, concat_axis=0, tiled=True)  29.3 us
    all_to_all x2, starting transfers between devices, exchange(): return lax.all_to_all(array, axis, split_axis=0, concat_axis=0, tiled=True)  23 us
    ppermute x6, starting transfers between devices, shift(): return lax.ppermute(array, ('dp', 'tp'), pairs)  16.9 us
    all_to_all x1, blocking collectives, exchange(): return lax.all_to_all(array, axis, split_axis=0, concat_axis=0, tiled=True)  16.4 us
    pallas_call x4, Pallas kernels, cut(): pl.pallas_call(kernel, out_shape=jax.ShapeDtypeStruct(shape, jnp.bfloat16...  8.48 us
    ppermute x2, starting transfers between devices, swap(): return lax.ppermute(array, 'dp', [(0, 1), (1, 0)])  3.82 us
    dot_general x1, matrix products, per_device(): jnp.dot(jnp.concatenate([hidden_near, hidden, hidden_far], 1), jnp.concat...  3.19 us
  transfers between devices with their start and end apart: 10, of which 4 were waited for; matrix products, arithmetic and copies ran while one was open for 3% of the time, Pallas kernels for 7%

profile of v6, /device:TPU:4, one launch (start us, length us, event | category | flops | bytes accessed | tf_op | source)
XLA Modules:
  0.0 151.6 jit_solution(14151295819709999114)
XLA Ops:
  0.0 3.2 %dispatch.1 = bf16[256,2432]{1,0:T(8,128)(2,1)} custom-call(s32[1]{0:T(128)} %bitcast.start_ref, s32[8,24]{1,0:T(8,128)} %bitcast.33, bf16[24,7168]{1,0:T(8,128)(2,1)} %tokens_ref.1), custom_call_target="tpu_custom_call" | custom-call | flops 29884416 | bytes 2097152 | tf_op jit(solution)/shard_map/dispatch/pallas_call | solution.py:136
  3.2 13.1 %all-to-all-start = ((bf16[32,8,2432]{2,1,0:T(8,128)(2,1)}), bf16[32,8,2432]{2,1,0:T(8,128)(2,1)S(1)}, u32[]{:S(2)}, u32[]{:S(2)}) async-start(bf16[32,8,2432]{2,1,0:T(8,128)(2,1)} %bitcast.31), calls=%async_computation | async-start | bytes 2490368 | tf_op jit(solution)/shard_map/all_to_all | solution.py:31
  16.3 2.3 %shard_map.65 = bf16[2432,256]{1,0:T(8,128)(2,1)} custom-call(s32[1]{0:T(128)} %bitcast.5.start_ref, bf16[1,7168,128]{2,1,0:T(8,128)(2,1)} %gate_ref.1, bf16[1,7168,128]{2,1,0:T(8,128)(2,1)} %up_ref.1), custom_call_target="tpu_custom_call" | custom-call | flops 311296000 | bytes 2490368 | tf_op jit(solution)/shard_map/pallas_call | solution.py:68
  18.6 1.9 %collective-permute-start = (bf16[2432,256]{1,0:T(8,128)(2,1)}, bf16[2432,256]{1,0:T(8,128)(2,1)S(1)}, u32[]{:S(2)}, u32[]{:S(2)}) collective-permute-start(bf16[2432,256]{1,0:T(8,128)(2,1)} %shard_map.65), channel_id=1, source_target_pairs={{0,1},{1,2},{2,3},{3,4},{4,5},{5,6},{6,7},{7,8},{8,9},{9,10},{10,1... | collective-permute-start | bytes 3735560 | tf_op jit(solution)/shard_map/ppermute | solution.py:23
  20.6 24.9 %collective-permute-done = bf16[2432,256]{1,0:T(8,128)(2,1)S(1)} collective-permute-done((bf16[2432,256]{1,0:T(8,128)(2,1)}, bf16[2432,256]{1,0:T(8,128)(2,1)S(1)}, u32[]{:S(2)}, u32[]{:S(2)}) %collective-permute-start) | collective-permute-done | bytes 1245216 | tf_op jit(solution)/shard_map/ppermute | solution.py:23
  45.4 1.9 %collective-permute-start.2 = (bf16[2432,256]{1,0:T(8,128)(2,1)S(1)}, bf16[2432,256]{1,0:T(8,128)(2,1)}, u32[]{:S(2)}, u32[]{:S(2)}) collective-permute-start(bf16[2432,256]{1,0:T(8,128)(2,1)S(1)} %collective-permute-done), channel_id=1, source_target_pairs={{0,12},{12,0},{1,13},{13,1},{2,14},{14,2},{3,15},{15,3},{4,16},{16... | collective-permute-start | bytes 3735560 | tf_op jit(solution)/shard_map/ppermute | solution.py:27
  47.4 1.9 %shard_map.66 = bf16[128,2432]{1,0:T(8,128)(2,1)} custom-call(s32[1]{0:T(128)} %bitcast.5.start_ref, bf16[1,128,7168]{2,1,0:T(8,128)(2,1)} %down_ref.1), custom_call_target="tpu_custom_call" | custom-call | flops 155648000 | bytes 1245184 | tf_op jit(solution)/shard_map/pallas_call | solution.py:68
  49.3 1.9 %collective-permute-start.6 = (bf16[128,2432]{1,0:T(8,128)(2,1)}, bf16[128,2432]{1,0:T(8,128)(2,1)S(1)}, u32[]{:S(2)}, u32[]{:S(2)}) collective-permute-start(bf16[128,2432]{1,0:T(8,128)(2,1)} %shard_map.66), channel_id=1, source_target_pairs={{0,1},{1,2},{2,3},{3,4},{4,5},{5,6},{6,7},{7,8},{8,9},{9,10},{10,1... | collective-permute-start | bytes 1867784 | tf_op jit(solution)/shard_map/ppermute | solution.py:23
  51.2 2.3 %shard_map.64 = bf16[2432,256]{1,0:T(8,128)(2,1)} custom-call(s32[1]{0:T(128)} %bitcast.start_ref, bf16[1,7168,128]{2,1,0:T(8,128)(2,1)} %gate_ref.1, bf16[1,7168,128]{2,1,0:T(8,128)(2,1)} %up_ref.1), custom_call_target="tpu_custom_call" | custom-call | flops 311296000 | bytes 2490368 | tf_op jit(solution)/shard_map/pallas_call | solution.py:68
  53.5 9.3 %collective-permute-done.6 = bf16[128,2432]{1,0:T(8,128)(2,1)S(1)} collective-permute-done((bf16[128,2432]{1,0:T(8,128)(2,1)}, bf16[128,2432]{1,0:T(8,128)(2,1)S(1)}, u32[]{:S(2)}, u32[]{:S(2)}) %collective-permute-start.6) | collective-permute-done | bytes 622624 | tf_op jit(solution)/shard_map/ppermute | solution.py:23
  62.8 1.9 %collective-permute-start.7 = (bf16[128,2432]{1,0:T(8,128)(2,1)S(1)}, bf16[128,2432]{1,0:T(8,128)(2,1)}, u32[]{:S(2)}, u32[]{:S(2)}) collective-permute-start(bf16[128,2432]{1,0:T(8,128)(2,1)S(1)} %collective-permute-done.6), channel_id=1, source_target_pairs={{0,12},{12,0},{1,13},{13,1},{2,14},{14,2},{3,15},{15,3},{4,16},{16... | collective-permute-start | bytes 1867784 | tf_op jit(solution)/shard_map/ppermute | solution.py:27
  64.7 0.0 all-to-all-done
  64.8 0.6 fusion.14
  65.4 0.0 copy-start
  65.4 3.4 %collective-permute-start.1 = (bf16[256,256]{0,1:T(8,128)(2,1)S(1)}, bf16[256,256]{0,1:T(8,128)(2,1)S(1)}, u32[]{:S(2)}, u32[]{:S(2)}) collective-permute-start(bf16[256,256]{0,1:T(8,128)(2,1)S(1)} %fusion.14), channel_id=1, source_target_pairs={{0,11},{1,0},{2,1},{3,2},{4,3},{5,4},{6,5},{7,6},{8,7},{9,8},{10,9... | collective-permute-start | bytes 393224 | tf_op jit(solution)/shard_map/ppermute | solution.py:23
  68.8 0.0 collective-permute-done.2
  68.8 1.9 %fusion.17 = bf16[256,256]{0,1:T(8,128)(2,1)S(1)} fusion(bf16[2432,256]{1,0:T(8,128)(2,1)} %collective-permute-done.2, bf16[32,8,2432]{2,1,0:T(8,128)(2,1)S(1)} %all-to-all-done), kind=kOutput, calls=%fused_computation.16 | convolution fusion | flops 318832640 | bytes 2621440 | tf_op jit(solution)/shard_map/dot_general | solution.py:225
  70.7 2.6 %collective-permute-start.3 = (bf16[256,256]{0,1:T(8,128)(2,1)S(1)}, bf16[256,256]{0,1:T(8,128)(2,1)S(1)}, u32[]{:S(2)}, u32[]{:S(2)}) collective-permute-start(bf16[256,256]{0,1:T(8,128)(2,1)S(1)} %fusion.17), channel_id=1, source_target_pairs={{0,1},{1,2},{2,3},{3,4},{4,5},{5,6},{6,7},{7,8},{8,9},{9,10},{10,1... | collective-permute-start | bytes 393224 | tf_op jit(solution)/shard_map/ppermute | solution.py:23
  73.3 0.0 copy-done
  73.3 0.6 fusion.12
  74.0 0.0 collective-permute-done.1
  74.0 4.8 %collective-permute-done.3 = bf16[256,256]{0,1:T(8,128)(2,1)S(1)} collective-permute-done((bf16[256,256]{0,1:T(8,128)(2,1)S(1)}, bf16[256,256]{0,1:T(8,128)(2,1)S(1)}, u32[]{:S(2)}, u32[]{:S(2)}) %collective-permute-start.3) | collective-permute-done | bytes 131104 | tf_op jit(solution)/shard_map/ppermute | solution.py:23
  78.9 1.9 %collective-permute-start.4 = (bf16[256,128]{0,1:T(8,128)(2,1)S(1)}, bf16[256,128]{0,1:T(8,128)(2,1)S(1)}, u32[]{:S(2)}, u32[]{:S(2)}) collective-permute-start(bf16[256,128]{0,1:T(8,128)(2,1)S(1)} %fusion.26), channel_id=1, source_target_pairs={{0,1},{1,2},{2,3},{3,4},{4,5},{5,6},{6,7},{7,8},{8,9},{9,10},{10,1... | collective-permute-start | bytes 196616 | tf_op jit(solution)/shard_map/ppermute | solution.py:23
  80.8 5.1 %collective-permute-start.5 = (bf16[256,128]{0,1:T(8,128)(2,1)S(1)}, bf16[256,128]{0,1:T(8,128)(2,1)S(1)}, u32[]{:S(2)}, u32[]{:S(2)}) collective-permute-start(bf16[256,128]{0,1:T(8,128)(2,1)S(1)} %fusion.26), channel_id=1, source_target_pairs={{0,11},{1,0},{2,1},{3,2},{4,3},{5,4},{6,5},{7,6},{8,7},{9,8},{10,9... | collective-permute-start | bytes 196616 | tf_op jit(solution)/shard_map/ppermute | solution.py:23
  86.0 1.9 %shard_map.67 = bf16[128,2432]{1,0:T(8,128)(2,1)} custom-call(s32[1]{0:T(128)} %bitcast.start_ref, bf16[1,128,7168]{2,1,0:T(8,128)(2,1)} %down_ref.1), custom_call_target="tpu_custom_call" | custom-call | flops 155648000 | bytes 1245184 | tf_op jit(solution)/shard_map/pallas_call | solution.py:68
  87.9 0.0 collective-permute-done.7
  87.9 0.0 collective-permute-done.4
  87.9 0.0 collective-permute-done.5
  87.9 3.2 %fusion = bf16[32,8,2432]{2,1,0:T(8,128)(2,1)} fusion(bf16[128,2432]{1,0:T(8,128)(2,1)} %collective-permute-done.7, bf16[128,2432]{1,0:T(8,128)(2,1)} %shard_map.67, bf16[128,2432]{1,0:T(8,128)(2,1)S(1)} %collective-permute-done.6, bf16[256,128]{0,1:T(8,128)(2,1)S(1)} %collective-permute-done.5, bf16[256,128]{0,1:T(8,128)(2,1)S(1)} %fusion.26, ...), kind=kOutput, calls=%fused_computation.1 | convolution fusion | flops 484966400 | bytes 3309568 | tf_op jit(solution)/shard_map/dot_general | solution.py:233
  91.1 0.0 copy-start.1
  91.1 0.0 copy-start.2
  91.1 9.9 %all-to-all-start.1 = ((bf16[32,8,2432]{2,1,0:T(8,128)(2,1)}), bf16[32,8,2432]{2,1,0:T(8,128)(2,1)S(1)}, u32[]{:S(2)}, u32[]{:S(2)}) async-start(bf16[32,8,2432]{2,1,0:T(8,128)(2,1)} %fusion), calls=%async_computation.1 | async-start | bytes 2490368 | tf_op jit(solution)/shard_map/all_to_all | solution.py:31
  101.0 0.0 copy-done.1
  101.1 0.7 copy.7.ids_ref
  101.7 0.0 copy-done.2
  101.7 0.7 copy.8.route_ref
  102.4 1.6 %weigh.1 = bf16[2,24,256]{2,1,0:T(8,128)(2,1)} custom-call(s32[24,8]{1,0:T(8,128)} %copy.7.ids_ref, f32[24,8]{1,0:T(8,128)} %copy.8.route_ref), custom_call_target="tpu_custom_call" | custom-call | flops 67108864 | bytes 32768 | tf_op jit(solution)/shard_map/weigh/pallas_call | solution.py:181
  104.0 29.3 %all-to-all-done.1 = bf16[32,8,2432]{2,1,0:T(8,128)(2,1)S(1)} async-done(((bf16[32,8,2432]{2,1,0:T(8,128)(2,1)}), bf16[32,8,2432]{2,1,0:T(8,128)(2,1)S(1)}, u32[]{:S(2)}, u32[]{:S(2)}) %all-to-all-start.1) | async-done | bytes 1245216 | tf_op jit(solution)/shard_map/all_to_all | solution.py:31
  133.3 1.1 fusion.6
  134.4 16.4 %all_to_all.15 = bf16[12,2,2432]{2,1,0:T(2,128)(2,1)S(1)} all-to-all(bf16[12,2,2432]{2,1,0:T(2,128)(2,1)S(1)} %reshape.43), channel_id=1, replica_groups=mesh['ep'=32,'dp'=2,'tp'=12] {'tp'}, dimensions={0} | all-to-all | bytes 233472 | tf_op jit(solution)/shard_map/all_to_all | solution.py:31
  150.8 0.1 add_convert_fusion
  150.9 0.6 pad_maximum_fusion
  (6 shorter events, 0.2 us)
Async XLA Ops:
  3.2 61.6 %all-to-all-start = ((bf16[32,8,2432]{2,1,0:T(8,128)(2,1)}), bf16[32,8,2432]{2,1,0:T(8,128)(2,1)S(1)}, u32[]{:S(2)}, u32[]{:S(2)}) async-start(bf16[32,8,2432]{2,1,0:T(8,128)(2,1)} %bitcast.31), calls=%async_computation | async-start | bytes 2490368 | tf_op jit(solution)/shard_map/all_to_all | solution.py:31
  18.6 26.8 %collective-permute-start = (bf16[2432,256]{1,0:T(8,128)(2,1)}, bf16[2432,256]{1,0:T(8,128)(2,1)S(1)}, u32[]{:S(2)}, u32[]{:S(2)}) collective-permute-start(bf16[2432,256]{1,0:T(8,128)(2,1)} %shard_map.65), channel_id=1, source_target_pairs={{0,1},{1,2},{2,3},{3,4},{4,5},{5,6},{6,7},{7,8},{8,9},{9,10},{10,1... | collective-permute-start | bytes 3735560 | tf_op jit(solution)/shard_map/ppermute | solution.py:23
  45.4 23.4 %collective-permute-start.2 = (bf16[2432,256]{1,0:T(8,128)(2,1)S(1)}, bf16[2432,256]{1,0:T(8,128)(2,1)}, u32[]{:S(2)}, u32[]{:S(2)}) collective-permute-start(bf16[2432,256]{1,0:T(8,128)(2,1)S(1)} %collective-permute-done), channel_id=1, source_target_pairs={{0,12},{12,0},{1,13},{13,1},{2,14},{14,2},{3,15},{15,3},{4,16},{16... | collective-permute-start | bytes 3735560 | tf_op jit(solution)/shard_map/ppermute | solution.py:27
  49.3 13.5 %collective-permute-start.6 = (bf16[128,2432]{1,0:T(8,128)(2,1)}, bf16[128,2432]{1,0:T(8,128)(2,1)S(1)}, u32[]{:S(2)}, u32[]{:S(2)}) collective-permute-start(bf16[128,2432]{1,0:T(8,128)(2,1)} %shard_map.66), channel_id=1, source_target_pairs={{0,1},{1,2},{2,3},{3,4},{4,5},{5,6},{6,7},{7,8},{8,9},{9,10},{10,1... | collective-permute-start | bytes 1867784 | tf_op jit(solution)/shard_map/ppermute | solution.py:23
  62.8 25.1 %collective-permute-start.7 = (bf16[128,2432]{1,0:T(8,128)(2,1)S(1)}, bf16[128,2432]{1,0:T(8,128)(2,1)}, u32[]{:S(2)}, u32[]{:S(2)}) collective-permute-start(bf16[128,2432]{1,0:T(8,128)(2,1)S(1)} %collective-permute-done.6), channel_id=1, source_target_pairs={{0,12},{12,0},{1,13},{13,1},{2,14},{14,2},{3,15},{15,3},{4,16},{16... | collective-permute-start | bytes 1867784 | tf_op jit(solution)/shard_map/ppermute | solution.py:27
  65.4 7.9 %copy-start = (bf16[2432,256]{1,0:T(8,128)(2,1)S(1)}, bf16[2432,256]{1,0:T(8,128)(2,1)}, u32[]{:S(2)}) copy-start(bf16[2432,256]{1,0:T(8,128)(2,1)} %shard_map.64) | copy-start | bytes 3735556
  65.4 8.6 %collective-permute-start.1 = (bf16[256,256]{0,1:T(8,128)(2,1)S(1)}, bf16[256,256]{0,1:T(8,128)(2,1)S(1)}, u32[]{:S(2)}, u32[]{:S(2)}) collective-permute-start(bf16[256,256]{0,1:T(8,128)(2,1)S(1)} %fusion.14), channel_id=1, source_target_pairs={{0,11},{1,0},{2,1},{3,2},{4,3},{5,4},{6,5},{7,6},{8,7},{9,8},{10,9... | collective-permute-start | bytes 393224 | tf_op jit(solution)/shard_map/ppermute | solution.py:23
  70.7 8.1 %collective-permute-start.3 = (bf16[256,256]{0,1:T(8,128)(2,1)S(1)}, bf16[256,256]{0,1:T(8,128)(2,1)S(1)}, u32[]{:S(2)}, u32[]{:S(2)}) collective-permute-start(bf16[256,256]{0,1:T(8,128)(2,1)S(1)} %fusion.17), channel_id=1, source_target_pairs={{0,1},{1,2},{2,3},{3,4},{4,5},{5,6},{6,7},{7,8},{8,9},{9,10},{10,1... | collective-permute-start | bytes 393224 | tf_op jit(solution)/shard_map/ppermute | solution.py:23
  78.9 9.0 %collective-permute-start.4 = (bf16[256,128]{0,1:T(8,128)(2,1)S(1)}, bf16[256,128]{0,1:T(8,128)(2,1)S(1)}, u32[]{:S(2)}, u32[]{:S(2)}) collective-permute-start(bf16[256,128]{0,1:T(8,128)(2,1)S(1)} %fusion.26), channel_id=1, source_target_pairs={{0,1},{1,2},{2,3},{3,4},{4,5},{5,6},{6,7},{7,8},{8,9},{9,10},{10,1... | collective-permute-start | bytes 196616 | tf_op jit(solution)/shard_map/ppermute | solution.py:23
  80.8 7.1 %collective-permute-start.5 = (bf16[256,128]{0,1:T(8,128)(2,1)S(1)}, bf16[256,128]{0,1:T(8,128)(2,1)S(1)}, u32[]{:S(2)}, u32[]{:S(2)}) collective-permute-start(bf16[256,128]{0,1:T(8,128)(2,1)S(1)} %fusion.26), channel_id=1, source_target_pairs={{0,11},{1,0},{2,1},{3,2},{4,3},{5,4},{6,5},{7,6},{8,7},{9,8},{10,9... | collective-permute-start | bytes 196616 | tf_op jit(solution)/shard_map/ppermute | solution.py:23
  91.1 9.9 %copy-start.1 = (s32[24,8]{0,1:T(8,128)S(1)}, s32[24,8]{0,1:T(8,128)}, u32[]{:S(2)}) copy-start(s32[24,8]{0,1:T(8,128)} %param.7) | copy-start | bytes 2308
  91.1 10.6 %copy-start.2 = (f32[24,8]{0,1:T(8,128)S(1)}, f32[24,8]{0,1:T(8,128)}, u32[]{:S(2)}) copy-start(f32[24,8]{0,1:T(8,128)} %param.8) | copy-start | bytes 2308
  91.1 42.1 %all-to-all-start.1 = ((bf16[32,8,2432]{2,1,0:T(8,128)(2,1)}), bf16[32,8,2432]{2,1,0:T(8,128)(2,1)S(1)}, u32[]{:S(2)}, u32[]{:S(2)}) async-start(bf16[32,8,2432]{2,1,0:T(8,128)(2,1)} %fusion), calls=%async_computation.1 | async-start | bytes 2490368 | tf_op jit(solution)/shard_map/all_to_all | solution.py:31

commit v7 on v6

--- a/solution.py
+++ b/solution.py
@@ -10,6 +10,7 @@
 MOST = 8
 LANES = 128
 PARTS = 3
+BACK = 4
 BLOCK = 5 * LANES
 
 
@@ -29,6 +30,13 @@
 
 def exchange(array, axis):
     return lax.all_to_all(array, axis, split_axis=0, concat_axis=0, tiled=True)
+
+
+def hop_two(array):
+    size = lax.axis_size("tp")
+    return lax.ppermute(
+        array, "tp", [(i, (i + (2 if i % 2 else size - 2)) % size) for i in range(size)]
+    )
 
 
 def piece_width(width):
@@ -84,10 +92,14 @@
     return cut(cut_gate_up, piece_start(index, width), (gate_weight, up_weight), shape)
 
 
-def down_piece(down_weight, index):
+def down_piece(down_weight, index, half=None):
     units, width = down_weight.shape[1:]
-    shape = (units, piece_width(width))
-    return cut(cut_down, piece_start(index, width), (down_weight,), shape)
+    size = width // BACK
+    start = lax.rem(index, BACK) * size
+    if half is not None:
+        size //= 2
+        start = start + half * size
+    return cut(cut_down, start, (down_weight,), (units, size))
 
 
 def dispatch_kernel(start_ref, ids_ref, tokens_ref, rows_ref, ids, held, chosen, sem):
@@ -202,7 +214,9 @@
     capacity = EXPERTS * MOST
     tp_size = lax.axis_size("tp")
     here = lax.axis_index("tp")
-    target = lax.rem(here + jnp.where(lax.axis_index("dp") == 0, 1, tp_size - 1), tp_size)
+    core = lax.axis_index("dp")
+    target = lax.rem(here + jnp.where(core == 0, 1, tp_size - 1), tp_size)
+    target_two = lax.rem(here + jnp.where(lax.rem(here, 2) == 0, tp_size - 2, 2), tp_size)
 
     outgoing = dispatch(tokens, expert_ids, here)
     outgoing, gate_weight, up_weight, down_weight, expert_ids, route_weight = (
@@ -217,6 +231,11 @@
     gate_up_far = swap(gate_up_near)
     down_near = shift(down_piece(down_weight, target), 1)
     down_far = swap(down_near)
+    mine = hop_two(down_piece(down_weight, target_two, core))
+    other = swap(mine)
+    down_two = jnp.concatenate(
+        [jnp.where(core == 0, mine, other), jnp.where(core == 0, other, mine)], 1
+    )
     gate_up_here = gate_up_piece(gate_weight, up_weight, here)
     down_here = down_piece(down_weight, here)
     weights = weigh(expert_ids, route_weight)
@@ -229,23 +248,20 @@
     gate_up = product(gate_up_here)
     gate_up = gate_up + from_far.astype(jnp.float32) + from_near.astype(jnp.float32)
     hidden = (jax.nn.silu(gate_up[:, :units]) * gate_up[:, units:]).astype(jnp.bfloat16)
-    hidden_near, hidden_far = shift(hidden, 1), shift(hidden, -1)
+    hidden_near, hidden_far, hidden_two = shift(hidden, 1), shift(hidden, -1), hop_two(hidden)
     partial_rows = jnp.dot(
-        jnp.concatenate([hidden_near, hidden, hidden_far], 1),
-        jnp.concatenate([down_near, down_here, down_far], 0),
+        jnp.concatenate([hidden_near, hidden, hidden_far, hidden_two], 1),
+        jnp.concatenate([down_near, down_here, down_far, down_two], 0),
         preferred_element_type=jnp.float32,
     ).astype(jnp.bfloat16)
-    returned = exchange(partial_rows.reshape(EXPERTS, MOST, piece), "ep")
-    combined = combine(weights, returned.reshape(capacity, piece)).astype(jnp.bfloat16)
-
-    pieces = combined.reshape(tp_size, rows_here // tp_size, piece)
-    arrived = exchange(pieces, "tp")
-    arrived = arrived.reshape(tp_size // PARTS, PARTS, rows_here // tp_size, piece)
-    arrived = sum(arrived[i].astype(jnp.float32) for i in range(tp_size // PARTS))
-    skip = PARTS * piece - width
-    parts = [arrived[i] for i in range(PARTS)]
-    parts[-1] = parts[-1][:, skip:]
-    return jnp.concatenate(parts, 1).astype(jnp.bfloat16)
+    size = width // BACK
+    returned = exchange(partial_rows.reshape(EXPERTS, MOST, size), "ep")
+    combined = combine(weights, returned.reshape(capacity, size)).astype(jnp.bfloat16)
+
+    arrived = exchange(combined.reshape(tp_size, rows_here // tp_size, size), "tp")
+    arrived = arrived.reshape(tp_size // BACK, BACK, rows_here // tp_size, size)
+    arrived = sum(arrived[i].astype(jnp.float32) for i in range(tp_size // BACK))
+    return jnp.concatenate([arrived[i] for i in range(BACK)], 1).astype(jnp.bfloat16)
 
 
 def solution(mesh):

time: 153 us -> 152 us (level)
  waiting for transfers between devices: 68.3 us -> 53.6 us
  starting transfers between devices: 43.7 us -> 55.4 us
    all_to_all x2, waiting for transfers between devices: 29.3 us -> 17.9 us  [exchange(): return lax.all_to_all(array, axis, split_axis=0, concat_axis=0, tiled=True)]
    ppermute x6, waiting for transfers between devices: 39 us -> 29.7 us  [shift(): return lax.ppermute(array, ('dp', 'tp'), pairs)]
    ppermute x0 -> x2, starting transfers between devices: none -> 7.81 us  [hop_two(): lax.ppermute(array, 'tp', [(i, (i + (2 if i % 2 else size - 2)) % size) f...]
    ppermute x0 -> x2, waiting for transfers between devices: none -> 6 us  [hop_two(): lax.ppermute(array, 'tp', [(i, (i + (2 if i % 2 else size - 2)) % size) f...]
    ppermute x2 -> x3, starting transfers between devices: 3.82 us -> 6.23 us  [swap(): return lax.ppermute(array, 'dp', [(0, 1), (1, 0)])]
    pallas_call x4 -> x5, Pallas kernels: 8.48 us -> 9.94 us  [cut(): pl.pallas_call(kernel, out_shape=jax.ShapeDtypeStruct(shape, jnp.bfloat16...]
  transfers between devices with their start and end apart: 10 -> 13, of which waited for: 4 -> 5; matrix products, arithmetic and copies ran while one was open for 3% -> 3% of each run, Pallas kernels for 7% -> 8%
where the time goes in v7:
time: 152 us; the launch traced here: 151 us
  starting transfers between devices  55.4 us (36%)
  waiting for transfers between devices  53.6 us (35%)
  blocking collectives  17.6 us (12%)
  Pallas kernels  14.7 us (10%)
  matrix products  6.83 us (4%)
    ppermute x6, waiting for transfers between devices, shift(): return lax.ppermute(array, ('dp', 'tp'), pairs)  29.7 us
    all_to_all x2, starting transfers between devices, exchange(): return lax.all_to_all(array, axis, split_axis=0, concat_axis=0, tiled=True)  23 us
    ppermute x6, starting transfers between devices, shift(): return lax.ppermute(array, ('dp', 'tp'), pairs)  18.4 us
    all_to_all x2, waiting for transfers between devices, exchange(): return lax.all_to_all(array, axis, split_axis=0, concat_axis=0, tiled=True)  17.9 us
    all_to_all x1, blocking collectives, exchange(): return lax.all_to_all(array, axis, split_axis=0, concat_axis=0, tiled=True)  17.6 us
    pallas_call x5, Pallas kernels, cut(): pl.pallas_call(kernel, out_shape=jax.ShapeDtypeStruct(shape, jnp.bfloat16...  9.94 us
    ppermute x2, starting transfers between devices, hop_two(): lax.ppermute(array, 'tp', [(i, (i + (2 if i % 2 else size - 2)) % size) f...  7.81 us
    ppermute x3, starting transfers between devices, swap(): return lax.ppermute(array, 'dp', [(0, 1), (1, 0)])  6.23 us
  transfers between devices with their start and end apart: 13, of which 5 were waited for; matrix products, arithmetic and copies ran while one was open for 3% of the time, Pallas kernels for 8%

profile of v7, /device:TPU:4, one launch (start us, length us, event | category | flops | bytes accessed | tf_op | source)
XLA Modules:
  0.0 150.8 jit_solution(12102644052939459710)
XLA Ops:
  0.0 3.1 %dispatch.1 = bf16[256,2432]{1,0:T(8,128)(2,1)} custom-call(s32[1]{0:T(128)} %bitcast.start_ref, s32[8,24]{1,0:T(8,128)} %bitcast.38, bf16[24,7168]{1,0:T(8,128)(2,1)} %tokens_ref.1), custom_call_target="tpu_custom_call" | custom-call | flops 29884416 | bytes 2097152 | tf_op jit(solution)/shard_map/dispatch/pallas_call | solution.py:148
  3.2 13.1 %all-to-all-start = ((bf16[32,8,2432]{2,1,0:T(8,128)(2,1)}), bf16[32,8,2432]{2,1,0:T(8,128)(2,1)S(1)}, u32[]{:S(2)}, u32[]{:S(2)}) async-start(bf16[32,8,2432]{2,1,0:T(8,128)(2,1)} %bitcast.36), calls=%async_computation | async-start | bytes 2490368 | tf_op jit(solution)/shard_map/all_to_all | solution.py:32
  16.3 2.3 %shard_map.65 = bf16[2432,256]{1,0:T(8,128)(2,1)} custom-call(s32[1]{0:T(128)} %bitcast.5.start_ref, bf16[1,7168,128]{2,1,0:T(8,128)(2,1)} %gate_ref.1, bf16[1,7168,128]{2,1,0:T(8,128)(2,1)} %up_ref.1), custom_call_target="tpu_custom_call" | custom-call | flops 311296000 | bytes 2490368 | tf_op jit(solution)/shard_map/pallas_call | solution.py:76
  18.6 1.9 %collective-permute-start = (bf16[2432,256]{1,0:T(8,128)(2,1)}, bf16[2432,256]{1,0:T(8,128)(2,1)S(1)}, u32[]{:S(2)}, u32[]{:S(2)}) collective-permute-start(bf16[2432,256]{1,0:T(8,128)(2,1)} %shard_map.65), channel_id=1, source_target_pairs={{0,1},{1,2},{2,3},{3,4},{4,5},{5,6},{6,7},{7,8},{8,9},{9,10},{10,1... | collective-permute-start | bytes 3735560 | tf_op jit(solution)/shard_map/ppermute | solution.py:24
  20.6 24.9 %collective-permute-done = bf16[2432,256]{1,0:T(8,128)(2,1)S(1)} collective-permute-done((bf16[2432,256]{1,0:T(8,128)(2,1)}, bf16[2432,256]{1,0:T(8,128)(2,1)S(1)}, u32[]{:S(2)}, u32[]{:S(2)}) %collective-permute-start) | collective-permute-done | bytes 1245216 | tf_op jit(solution)/shard_map/ppermute | solution.py:24
  45.4 1.9 %collective-permute-start.2 = (bf16[2432,256]{1,0:T(8,128)(2,1)S(1)}, bf16[2432,256]{1,0:T(8,128)(2,1)}, u32[]{:S(2)}, u32[]{:S(2)}) collective-permute-start(bf16[2432,256]{1,0:T(8,128)(2,1)S(1)} %collective-permute-done), channel_id=1, source_target_pairs={{0,12},{12,0},{1,13},{13,1},{2,14},{14,2},{3,15},{15,3},{4,16},{16... | collective-permute-start | bytes 3735560 | tf_op jit(solution)/shard_map/ppermute | solution.py:28
  47.4 1.8 %shard_map.66 = bf16[128,1792]{1,0:T(8,128)(2,1)} custom-call(s32[1]{0:T(128)} %bitcast.6.start_ref, bf16[1,128,7168]{2,1,0:T(8,128)(2,1)} %down_ref.2), custom_call_target="tpu_custom_call" | custom-call | flops 114688000 | bytes 917504 | tf_op jit(solution)/shard_map/pallas_call | solution.py:76
  49.2 1.9 %collective-permute-start.7 = (bf16[128,1792]{1,0:T(8,128)(2,1)}, bf16[128,1792]{1,0:T(8,128)(2,1)S(1)}, u32[]{:S(2)}, u32[]{:S(2)}) collective-permute-start(bf16[128,1792]{1,0:T(8,128)(2,1)} %shard_map.66), channel_id=1, source_target_pairs={{0,1},{1,2},{2,3},{3,4},{4,5},{5,6},{6,7},{7,8},{8,9},{9,10},{10,1... | collective-permute-start | bytes 1376264 | tf_op jit(solution)/shard_map/ppermute | solution.py:24
  51.2 1.7 %shard_map.68 = bf16[128,896]{1,0:T(8,128)(2,1)} custom-call(s32[1]{0:T(128)} %bitcast.8.start_ref, bf16[1,128,7168]{2,1,0:T(8,128)(2,1)} %down_ref.2), custom_call_target="tpu_custom_call" | custom-call | flops 57344000 | bytes 458752 | tf_op jit(solution)/shard_map/pallas_call | solution.py:76
  52.8 5.4 %collective-permute-start.9 = (bf16[128,896]{1,0:T(8,128)(2,1)}, bf16[128,896]{1,0:T(8,128)(2,1)S(1)}, u32[]{:S(2)}, u32[]{:S(2)}) collective-permute-start(bf16[128,896]{1,0:T(8,128)(2,1)} %shard_map.68), channel_id=1, source_target_pairs={{0,10},{1,3},{2,0},{3,5},{4,2},{5,7},{6,4},{7,9},{8,6},{9,11},{10,... | collective-permute-start | bytes 688136 | tf_op jit(solution)/shard_map/ppermute | solution.py:37
  58.2 1.8 %shard_map.67 = bf16[128,1792]{1,0:T(8,128)(2,1)} custom-call(s32[1]{0:T(128)} %bitcast.7.start_ref, bf16[1,128,7168]{2,1,0:T(8,128)(2,1)} %down_ref.2), custom_call_target="tpu_custom_call" | custom-call | flops 114688000 | bytes 917504 | tf_op jit(solution)/shard_map/pallas_call | solution.py:76
  60.0 2.3 %shard_map.64 = bf16[2432,256]{1,0:T(8,128)(2,1)} custom-call(s32[1]{0:T(128)} %bitcast.start_ref, bf16[1,7168,128]{2,1,0:T(8,128)(2,1)} %gate_ref.1, bf16[1,7168,128]{2,1,0:T(8,128)(2,1)} %up_ref.1), custom_call_target="tpu_custom_call" | custom-call | flops 311296000 | bytes 2490368 | tf_op jit(solution)/shard_map/pallas_call | solution.py:76
  62.4 1.5 collective-permute-done.9
  63.9 2.2 %collective-permute-start.10 = (bf16[128,896]{1,0:T(8,128)(2,1)S(1)}, bf16[128,896]{1,0:T(8,128)(2,1)S(1)}, u32[]{:S(2)}, u32[]{:S(2)}) collective-permute-start(bf16[128,896]{1,0:T(8,128)(2,1)S(1)} %collective-permute-done.9), channel_id=1, source_target_pairs={{0,12},{12,0},{1,13},{13,1},{2,14},{14,2},{3,15},{15,3},{4,16},{16... | collective-permute-start | bytes 688136 | tf_op jit(solution)/shard_map/ppermute | solution.py:28
  66.0 0.0 collective-permute-done.7
  66.0 2.1 %collective-permute-start.8 = (bf16[128,1792]{1,0:T(8,128)(2,1)S(1)}, bf16[128,1792]{1,0:T(8,128)(2,1)}, u32[]{:S(2)}, u32[]{:S(2)}) collective-permute-start(bf16[128,1792]{1,0:T(8,128)(2,1)S(1)} %collective-permute-done.7), channel_id=1, source_target_pairs={{0,12},{12,0},{1,13},{13,1},{2,14},{14,2},{3,15},{15,3},{4,16},{16... | collective-permute-start | bytes 1376264 | tf_op jit(solution)/shard_map/ppermute | solution.py:28
  68.2 0.0 all-to-all-done
  68.2 0.6 fusion.16
  68.8 0.0 copy-start
  68.8 4.9 %collective-permute-start.1 = (bf16[256,256]{0,1:T(8,128)(2,1)S(1)}, bf16[256,256]{0,1:T(8,128)(2,1)S(1)}, u32[]{:S(2)}, u32[]{:S(2)}) collective-permute-start(bf16[256,256]{0,1:T(8,128)(2,1)S(1)} %fusion.16), channel_id=1, source_target_pairs={{0,11},{1,0},{2,1},{3,2},{4,3},{5,4},{6,5},{7,6},{8,7},{9,8},{10,9... | collective-permute-start | bytes 393224 | tf_op jit(solution)/shard_map/ppermute | solution.py:24
  73.7 0.0 collective-permute-done.2
  73.8 1.9 %fusion.19 = bf16[256,256]{0,1:T(8,128)(2,1)S(1)} fusion(bf16[2432,256]{1,0:T(8,128)(2,1)} %collective-permute-done.2, bf16[32,8,2432]{2,1,0:T(8,128)(2,1)S(1)} %all-to-all-done), kind=kOutput, calls=%fused_computation.18 | convolution fusion | flops 318832640 | bytes 2621440 | tf_op jit(solution)/shard_map/dot_general | solution.py:244
  75.7 2.6 %collective-permute-start.3 = (bf16[256,256]{0,1:T(8,128)(2,1)S(1)}, bf16[256,256]{0,1:T(8,128)(2,1)S(1)}, u32[]{:S(2)}, u32[]{:S(2)}) collective-permute-start(bf16[256,256]{0,1:T(8,128)(2,1)S(1)} %fusion.19), channel_id=1, source_target_pairs={{0,1},{1,2},{2,3},{3,4},{4,5},{5,6},{6,7},{7,8},{8,9},{9,10},{10,1... | collective-permute-start | bytes 393224 | tf_op jit(solution)/shard_map/ppermute | solution.py:24
  78.3 0.0 copy-done
  78.3 0.6 fusion.14
  78.9 0.0 copy-start.1
  78.9 0.0 collective-permute-done.1
  78.9 4.8 %collective-permute-done.3 = bf16[256,256]{0,1:T(8,128)(2,1)S(1)} collective-permute-done((bf16[256,256]{0,1:T(8,128)(2,1)S(1)}, bf16[256,256]{0,1:T(8,128)(2,1)S(1)}, u32[]{:S(2)}, u32[]{:S(2)}) %collective-permute-start.3) | collective-permute-done | bytes 131104 | tf_op jit(solution)/shard_map/ppermute | solution.py:24
  83.7 0.1 convert_add_fusion
  83.9 1.9 %collective-permute-start.4 = (bf16[256,128]{0,1:T(8,128)(2,1)S(1)}, bf16[256,128]{0,1:T(8,128)(2,1)S(1)}, u32[]{:S(2)}, u32[]{:S(2)}) collective-permute-start(bf16[256,128]{0,1:T(8,128)(2,1)S(1)} %fusion.32), channel_id=1, source_target_pairs={{0,1},{1,2},{2,3},{3,4},{4,5},{5,6},{6,7},{7,8},{8,9},{9,10},{10,1... | collective-permute-start | bytes 196616 | tf_op jit(solution)/shard_map/ppermute | solution.py:24
  85.8 5.1 %collective-permute-start.5 = (bf16[256,128]{0,1:T(8,128)(2,1)S(1)}, bf16[256,128]{0,1:T(8,128)(2,1)S(1)}, u32[]{:S(2)}, u32[]{:S(2)}) collective-permute-start(bf16[256,128]{0,1:T(8,128)(2,1)S(1)} %fusion.32), channel_id=1, source_target_pairs={{0,11},{1,0},{2,1},{3,2},{4,3},{5,4},{6,5},{7,6},{8,7},{9,8},{10,9... | collective-permute-start | bytes 196616 | tf_op jit(solution)/shard_map/ppermute | solution.py:24
  90.9 2.4 %collective-permute-start.6 = (bf16[256,128]{0,1:T(8,128)(2,1)S(1)}, bf16[256,128]{0,1:T(8,128)(2,1)S(1)}, u32[]{:S(2)}, u32[]{:S(2)}) collective-permute-start(bf16[256,128]{0,1:T(8,128)(2,1)S(1)} %fusion.32), channel_id=1, source_target_pairs={{0,10},{1,3},{2,0},{3,5},{4,2},{5,7},{6,4},{7,9},{8,6},{9,11},{10,... | collective-permute-start | bytes 196616 | tf_op jit(solution)/shard_map/ppermute | solution.py:37
  93.4 0.0 collective-permute-done.10
  93.4 0.1 broadcast_select_fusion.1
  93.4 0.0 collective-permute-done.8
  93.5 0.0 collective-permute-done.4
  93.5 0.0 collective-permute-done.5
  93.5 4.5 %collective-permute-done.6 = bf16[256,128]{0,1:T(8,128)(2,1)S(1)} collective-permute-done((bf16[256,128]{0,1:T(8,128)(2,1)S(1)}, bf16[256,128]{0,1:T(8,128)(2,1)S(1)}, u32[]{:S(2)}, u32[]{:S(2)}) %collective-permute-start.6) | collective-permute-done | bytes 65568 | tf_op jit(solution)/shard_map/ppermute | solution.py:37
  98.0 0.0 copy-done.1
  98.0 2.6 %fusion = bf16[32,8,1792]{2,1,0:T(8,128)(2,1)} fusion(bf16[128,896]{1,0:T(8,128)(2,1)S(1)} %get-tuple-element.18, bf16[128,896]{1,0:T(8,128)(2,1)S(1)} %get-tuple-element.17, bf16[128,1792]{1,0:T(8,128)(2,1)} %collective-permute-done.8, bf16[128,1792]{1,0:T(8,128)(2,1)S(1)} %copy-done.1, bf16[128,1792]{1,0:T(8,128)(2,1)S(1)} %collective-permute-done.7, ...), kind=kOutput, calls=%fused_computation.1 | convolution fusion | flops 480444416 | bytes 3014656 | tf_op jit(solution)/shard_map/dot_general | solution.py:252
  100.6 9.9 %all-to-all-start.1 = ((bf16[32,8,1792]{2,1,0:T(8,128)(2,1)}), bf16[32,8,1792]{2,1,0:T(8,128)(2,1)S(1)}, u32[]{:S(2)}, u32[]{:S(2)}) async-start(bf16[32,8,1792]{2,1,0:T(8,128)(2,1)} %fusion), calls=%async_computation.1 | async-start | bytes 1835008 | tf_op jit(solution)/shard_map/all_to_all | solution.py:32
  110.5 0.7 copy.7.ids_ref
  111.2 0.7 copy.8.route_ref
  111.9 1.6 %weigh.1 = bf16[2,24,256]{2,1,0:T(8,128)(2,1)} custom-call(s32[24,8]{1,0:T(8,128)} %copy.7.ids_ref, f32[24,8]{1,0:T(8,128)} %copy.8.route_ref), custom_call_target="tpu_custom_call" | custom-call | flops 67108864 | bytes 32768 | tf_op jit(solution)/shard_map/weigh/pallas_call | solution.py:193
  113.4 17.9 %all-to-all-done.1 = bf16[32,8,1792]{2,1,0:T(8,128)(2,1)S(1)} async-done(((bf16[32,8,1792]{2,1,0:T(8,128)(2,1)}), bf16[32,8,1792]{2,1,0:T(8,128)(2,1)S(1)}, u32[]{:S(2)}, u32[]{:S(2)}) %all-to-all-start.1) | async-done | bytes 917536 | tf_op jit(solution)/shard_map/all_to_all | solution.py:32
  131.3 1.0 fusion.22
  132.4 17.6 %all_to_all.15 = bf16[12,2,1792]{2,1,0:T(2,128)(2,1)S(1)} all-to-all(bf16[12,2,1792]{2,1,0:T(2,128)(2,1)S(1)} %reshape.51), channel_id=1, replica_groups=mesh['ep'=32,'dp'=2,'tp'=12] {'tp'}, dimensions={0} | all-to-all | bytes 172032 | tf_op jit(solution)/shard_map/all_to_all | solution.py:32
  150.1 0.6 pad_maximum_fusion
  (9 shorter events, 0.2 us)
Async XLA Ops:
  3.2 65.0 %all-to-all-start = ((bf16[32,8,2432]{2,1,0:T(8,128)(2,1)}), bf16[32,8,2432]{2,1,0:T(8,128)(2,1)S(1)}, u32[]{:S(2)}, u32[]{:S(2)}) async-start(bf16[32,8,2432]{2,1,0:T(8,128)(2,1)} %bitcast.36), calls=%async_computation | async-start | bytes 2490368 | tf_op jit(solution)/shard_map/all_to_all | solution.py:32
  18.6 26.8 %collective-permute-start = (bf16[2432,256]{1,0:T(8,128)(2,1)}, bf16[2432,256]{1,0:T(8,128)(2,1)S(1)}, u32[]{:S(2)}, u32[]{:S(2)}) collective-permute-start(bf16[2432,256]{1,0:T(8,128)(2,1)} %shard_map.65), channel_id=1, source_target_pairs={{0,1},{1,2},{2,3},{3,4},{4,5},{5,6},{6,7},{7,8},{8,9},{9,10},{10,1... | collective-permute-start | bytes 3735560 | tf_op jit(solution)/shard_map/ppermute | solution.py:24
  45.4 28.3 %collective-permute-start.2 = (bf16[2432,256]{1,0:T(8,128)(2,1)S(1)}, bf16[2432,256]{1,0:T(8,128)(2,1)}, u32[]{:S(2)}, u32[]{:S(2)}) collective-permute-start(bf16[2432,256]{1,0:T(8,128)(2,1)S(1)} %collective-permute-done), channel_id=1, source_target_pairs={{0,12},{12,0},{1,13},{13,1},{2,14},{14,2},{3,15},{15,3},{4,16},{16... | collective-permute-start | bytes 3735560 | tf_op jit(solution)/shard_map/ppermute | solution.py:28
  49.2 16.8 %collective-permute-start.7 = (bf16[128,1792]{1,0:T(8,128)(2,1)}, bf16[128,1792]{1,0:T(8,128)(2,1)S(1)}, u32[]{:S(2)}, u32[]{:S(2)}) collective-permute-start(bf16[128,1792]{1,0:T(8,128)(2,1)} %shard_map.66), channel_id=1, source_target_pairs={{0,1},{1,2},{2,3},{3,4},{4,5},{5,6},{6,7},{7,8},{8,9},{9,10},{10,1... | collective-permute-start | bytes 1376264 | tf_op jit(solution)/shard_map/ppermute | solution.py:24
  52.8 11.0 %collective-permute-start.9 = (bf16[128,896]{1,0:T(8,128)(2,1)}, bf16[128,896]{1,0:T(8,128)(2,1)S(1)}, u32[]{:S(2)}, u32[]{:S(2)}) collective-permute-start(bf16[128,896]{1,0:T(8,128)(2,1)} %shard_map.68), channel_id=1, source_target_pairs={{0,10},{1,3},{2,0},{3,5},{4,2},{5,7},{6,4},{7,9},{8,6},{9,11},{10,... | collective-permute-start | bytes 688136 | tf_op jit(solution)/shard_map/ppermute | solution.py:37
  63.9 29.5 %collective-permute-start.10 = (bf16[128,896]{1,0:T(8,128)(2,1)S(1)}, bf16[128,896]{1,0:T(8,128)(2,1)S(1)}, u32[]{:S(2)}, u32[]{:S(2)}) collective-permute-start(bf16[128,896]{1,0:T(8,128)(2,1)S(1)} %collective-permute-done.9), channel_id=1, source_target_pairs={{0,12},{12,0},{1,13},{13,1},{2,14},{14,2},{3,15},{15,3},{4,16},{16... | collective-permute-start | bytes 688136 | tf_op jit(solution)/shard_map/ppermute | solution.py:28
  66.0 27.4 %collective-permute-start.8 = (bf16[128,1792]{1,0:T(8,128)(2,1)S(1)}, bf16[128,1792]{1,0:T(8,128)(2,1)}, u32[]{:S(2)}, u32[]{:S(2)}) collective-permute-start(bf16[128,1792]{1,0:T(8,128)(2,1)S(1)} %collective-permute-done.7), channel_id=1, source_target_pairs={{0,12},{12,0},{1,13},{13,1},{2,14},{14,2},{3,15},{15,3},{4,16},{16... | collective-permute-start | bytes 1376264 | tf_op jit(solution)/shard_map/ppermute | solution.py:28
  68.8 9.4 %copy-start = (bf16[2432,256]{1,0:T(8,128)(2,1)S(1)}, bf16[2432,256]{1,0:T(8,128)(2,1)}, u32[]{:S(2)}) copy-start(bf16[2432,256]{1,0:T(8,128)(2,1)} %shard_map.64) | copy-start | bytes 3735556
  68.8 10.1 %collective-permute-start.1 = (bf16[256,256]{0,1:T(8,128)(2,1)S(1)}, bf16[256,256]{0,1:T(8,128)(2,1)S(1)}, u32[]{:S(2)}, u32[]{:S(2)}) collective-permute-start(bf16[256,256]{0,1:T(8,128)(2,1)S(1)} %fusion.16), channel_id=1, source_target_pairs={{0,11},{1,0},{2,1},{3,2},{4,3},{5,4},{6,5},{7,6},{8,7},{9,8},{10,9... | collective-permute-start | bytes 393224 | tf_op jit(solution)/shard_map/ppermute | solution.py:24
  75.7 8.1 %collective-permute-start.3 = (bf16[256,256]{0,1:T(8,128)(2,1)S(1)}, bf16[256,256]{0,1:T(8,128)(2,1)S(1)}, u32[]{:S(2)}, u32[]{:S(2)}) collective-permute-start(bf16[256,256]{0,1:T(8,128)(2,1)S(1)} %fusion.19), channel_id=1, source_target_pairs={{0,1},{1,2},{2,3},{3,4},{4,5},{5,6},{6,7},{7,8},{8,9},{9,10},{10,1... | collective-permute-start | bytes 393224 | tf_op jit(solution)/shard_map/ppermute | solution.py:24
  78.9 19.1 %copy-start.1 = (bf16[128,1792]{1,0:T(8,128)(2,1)S(1)}, bf16[128,1792]{1,0:T(8,128)(2,1)}, u32[]{:S(2)}) copy-start(bf16[128,1792]{1,0:T(8,128)(2,1)} %shard_map.67) | copy-start | bytes 1376260
  83.9 9.6 %collective-permute-start.4 = (bf16[256,128]{0,1:T(8,128)(2,1)S(1)}, bf16[256,128]{0,1:T(8,128)(2,1)S(1)}, u32[]{:S(2)}, u32[]{:S(2)}) collective-permute-start(bf16[256,128]{0,1:T(8,128)(2,1)S(1)} %fusion.32), channel_id=1, source_target_pairs={{0,1},{1,2},{2,3},{3,4},{4,5},{5,6},{6,7},{7,8},{8,9},{9,10},{10,1... | collective-permute-start | bytes 196616 | tf_op jit(solution)/shard_map/ppermute | solution.py:24
  85.8 7.7 %collective-permute-start.5 = (bf16[256,128]{0,1:T(8,128)(2,1)S(1)}, bf16[256,128]{0,1:T(8,128)(2,1)S(1)}, u32[]{:S(2)}, u32[]{:S(2)}) collective-permute-start(bf16[256,128]{0,1:T(8,128)(2,1)S(1)} %fusion.32), channel_id=1, source_target_pairs={{0,11},{1,0},{2,1},{3,2},{4,3},{5,4},{6,5},{7,6},{8,7},{9,8},{10,9... | collective-permute-start | bytes 196616 | tf_op jit(solution)/shard_map/ppermute | solution.py:24
  90.9 7.1 %collective-permute-start.6 = (bf16[256,128]{0,1:T(8,128)(2,1)S(1)}, bf16[256,128]{0,1:T(8,128)(2,1)S(1)}, u32[]{:S(2)}, u32[]{:S(2)}) collective-permute-start(bf16[256,128]{0,1:T(8,128)(2,1)S(1)} %fusion.32), channel_id=1, source_target_pairs={{0,10},{1,3},{2,0},{3,5},{4,2},{5,7},{6,4},{7,9},{8,6},{9,11},{10,... | collective-permute-start | bytes 196616 | tf_op jit(solution)/shard_map/ppermute | solution.py:37
  100.6 9.9 %copy-start.2 = (s32[24,8]{0,1:T(8,128)S(1)}, s32[24,8]{0,1:T(8,128)}, u32[]{:S(2)}) copy-start(s32[24,8]{0,1:T(8,128)} %param.7) | copy-start | bytes 2308
  100.6 10.6 %copy-start.3 = (f32[24,8]{0,1:T(8,128)S(1)}, f32[24,8]{0,1:T(8,128)}, u32[]{:S(2)}) copy-start(f32[24,8]{0,1:T(8,128)} %param.8) | copy-start | bytes 2308
  100.6 30.7 %all-to-all-start.1 = ((bf16[32,8,1792]{2,1,0:T(8,128)(2,1)}), bf16[32,8,1792]{2,1,0:T(8,128)(2,1)S(1)}, u32[]{:S(2)}, u32[]{:S(2)}) async-start(bf16[32,8,1792]{2,1,0:T(8,128)(2,1)} %fusion), calls=%async_computation.1 | async-start | bytes 1835008 | tf_op jit(solution)/shard_map/all_to_all | solution.py:32

commit v8 on v7

--- a/solution.py
+++ b/solution.py
@@ -11,6 +11,7 @@
 LANES = 128
 PARTS = 3
 BACK = 4
+STRIPS = 4
 BLOCK = 5 * LANES
 
 
@@ -49,19 +50,35 @@
     return jnp.minimum(lax.rem(index, PARTS) * piece, width - piece)
 
 
-def cut_gate_up(start_ref, gate_ref, up_ref, out_ref, sem):
+def cut_gate_up(start_ref, gate_ref, up_ref, out_ref, held, in_sem, out_sem):
     piece, units = out_ref.shape[0], gate_ref.shape[2]
-    rows = pl.ds(pl.multiple_of(start_ref[0], LANES), piece)
-    copies = [
-        pltpu.make_async_copy(
-            ref.at[0, rows, :], out_ref.at[:, pl.ds(i * units, units)], sem.at[i]
+    rows = piece // STRIPS
+    arriving, leaving = [], []
+    for strip in range(STRIPS):
+        source = pl.ds(pl.multiple_of(start_ref[0] + strip * rows, 16), rows)
+        target = pl.ds(strip * rows, rows)
+        arriving.append(
+            [
+                pltpu.make_async_copy(
+                    ref.at[0, source, :],
+                    held.at[target, pl.ds(i * units, units)],
+                    in_sem.at[strip, i],
+                )
+                for i, ref in enumerate((gate_ref, up_ref))
+            ]
         )
-        for i, ref in enumerate((gate_ref, up_ref))
-    ]
-    for copy in copies:
-        copy.start()
-    for copy in copies:
-        copy.wait()
+        leaving.append(
+            pltpu.make_async_copy(held.at[target, :], out_ref.at[target, :], out_sem.at[strip])
+        )
+    for pair in arriving:
+        for copy in pair:
+            copy.start()
+    for pair, out in zip(arriving, leaving):
+        for copy in pair:
+            copy.wait()
+        out.start()
+    for out in leaving:
+        out.wait()
 
 
 def cut_down(start_ref, down_ref, out_ref, sem):
@@ -71,15 +88,15 @@
     copy.wait()
 
 
-def cut(kernel, start, arrays, shape):
+def cut(kernel, start, arrays, shape, out_space, scratch):
     size = shape[0] * shape[1]
     return pl.pallas_call(
         kernel,
         out_shape=jax.ShapeDtypeStruct(shape, jnp.bfloat16),
         in_specs=[pl.BlockSpec(memory_space=pltpu.SMEM)]
         + [pl.BlockSpec(memory_space=pl.ANY)] * len(arrays),
-        out_specs=pl.BlockSpec(memory_space=pltpu.VMEM),
-        scratch_shapes=[pltpu.SemaphoreType.DMA((2,))],
+        out_specs=pl.BlockSpec(memory_space=out_space),
+        scratch_shapes=scratch,
         cost_estimate=pl.CostEstimate(
             flops=500 * size, bytes_accessed=4 * size, transcendentals=0
         ),
@@ -89,7 +106,13 @@
 def gate_up_piece(gate_weight, up_weight, index):
     width, units = gate_weight.shape[1:]
     shape = (piece_width(width), 2 * units)
-    return cut(cut_gate_up, piece_start(index, width), (gate_weight, up_weight), shape)
+    scratch = [
+        pltpu.VMEM(shape, jnp.bfloat16),
+        pltpu.SemaphoreType.DMA((STRIPS, 2)),
+        pltpu.SemaphoreType.DMA((STRIPS,)),
+    ]
+    arrays = (gate_weight, up_weight)
+    return cut(cut_gate_up, piece_start(index, width), arrays, shape, pl.ANY, scratch)
 
 
 def down_piece(down_weight, index, half=None):
@@ -99,7 +122,8 @@
     if half is not None:
         size //= 2
         start = start + half * size
-    return cut(cut_down, start, (down_weight,), (units, size))
+    scratch = [pltpu.SemaphoreType.DMA((1,))]
+    return cut(cut_down, start, (down_weight,), (units, size), pltpu.VMEM, scratch)
 
 
 def dispatch_kernel(start_ref, ids_ref, tokens_ref, rows_ref, ids, held, chosen, sem):
@@ -248,7 +272,9 @@
     gate_up = product(gate_up_here)
     gate_up = gate_up + from_far.astype(jnp.float32) + from_near.astype(jnp.float32)
     hidden = (jax.nn.silu(gate_up[:, :units]) * gate_up[:, units:]).astype(jnp.bfloat16)
-    hidden_near, hidden_far, hidden_two = shift(hidden, 1), shift(hidden, -1), hop_two(hidden)
+    hidden_two = hop_two(hidden)
+    hidden_near = shift(hidden, 1)
+    hidden_far = shift(hidden, -1)
     partial_rows = jnp.dot(
         jnp.concatenate([hidden_near, hidden, hidden_far, hidden_two], 1),
         jnp.concatenate([down_near, down_here, down_far, down_two], 0),

time: 152 us -> 152 us (level)
  transfers between devices with their start and end apart: 13 -> 13, of which waited for: 5 -> 5; matrix products, arithmetic and copies ran while one was open for 3% -> 3% of each run, Pallas kernels for 8% -> 7%
where the time goes in v8:
time: 152 us; the launch traced here: 151 us
  starting transfers between devices  55.4 us (36%)
  waiting for transfers between devices  53.7 us (35%)
  blocking collectives  17.6 us (12%)
  Pallas kernels  14.4 us (9%)
  matrix products  6.83 us (4%)
    ppermute x6, waiting for transfers between devices, shift(): return lax.ppermute(array, ('dp', 'tp'), pairs)  29.7 us
    all_to_all x2, starting transfers between devices, exchange(): return lax.all_to_all(array, axis, split_axis=0, concat_axis=0, tiled=True)  23 us
    ppermute x6, starting transfers between devices, shift(): return lax.ppermute(array, ('dp', 'tp'), pairs)  18.4 us
    all_to_all x2, waiting for transfers between devices, exchange(): return lax.all_to_all(array, axis, split_axis=0, concat_axis=0, tiled=True)  17.9 us
    all_to_all x1, blocking collectives, exchange(): return lax.all_to_all(array, axis, split_axis=0, concat_axis=0, tiled=True)  17.6 us
    pallas_call x5, Pallas kernels, cut(): pl.pallas_call(kernel, out_shape=jax.ShapeDtypeStruct(shape, jnp.bfloat16...  9.69 us
    ppermute x2, starting transfers between devices, hop_two(): lax.ppermute(array, 'tp', [(i, (i + (2 if i % 2 else size - 2)) % size) f...  7.81 us
    ppermute x3, starting transfers between devices, swap(): return lax.ppermute(array, 'dp', [(0, 1), (1, 0)])  6.23 us
  transfers between devices with their start and end apart: 13, of which 5 were waited for; matrix products, arithmetic and copies ran while one was open for 3% of the time, Pallas kernels for 7%

profile of v8, /device:TPU:4, one launch (start us, length us, event | category | flops | bytes accessed | tf_op | source)
XLA Modules:
  0.0 150.7 jit_solution(657801208224112420)
XLA Ops:
  0.0 3.1 %dispatch.1 = bf16[256,2432]{1,0:T(8,128)(2,1)} custom-call(s32[1]{0:T(128)} %bitcast.start_ref, s32[8,24]{1,0:T(8,128)} %bitcast.38, bf16[24,7168]{1,0:T(8,128)(2,1)} %tokens_ref.1), custom_call_target="tpu_custom_call" | custom-call | flops 29884416 | bytes 2097152 | tf_op jit(solution)/shard_map/dispatch/pallas_call | solution.py:172
  3.2 13.1 %all-to-all-start = ((bf16[32,8,2432]{2,1,0:T(8,128)(2,1)}), bf16[32,8,2432]{2,1,0:T(8,128)(2,1)S(1)}, u32[]{:S(2)}, u32[]{:S(2)}) async-start(bf16[32,8,2432]{2,1,0:T(8,128)(2,1)} %bitcast.36), calls=%async_computation | async-start | bytes 2490368 | tf_op jit(solution)/shard_map/all_to_all | solution.py:33
  16.3 2.2 %shard_map.65 = bf16[2432,256]{1,0:T(8,128)(2,1)} custom-call(s32[1]{0:T(128)} %bitcast.5.start_ref, bf16[1,7168,128]{2,1,0:T(8,128)(2,1)} %gate_ref.1, bf16[1,7168,128]{2,1,0:T(8,128)(2,1)} %up_ref.1), custom_call_target="tpu_custom_call" | custom-call | flops 311296000 | bytes 2490368 | tf_op jit(solution)/shard_map/pallas_call | solution.py:93
  18.5 1.9 %collective-permute-start = (bf16[2432,256]{1,0:T(8,128)(2,1)}, bf16[2432,256]{1,0:T(8,128)(2,1)S(1)}, u32[]{:S(2)}, u32[]{:S(2)}) collective-permute-start(bf16[2432,256]{1,0:T(8,128)(2,1)} %shard_map.65), channel_id=1, source_target_pairs={{0,1},{1,2},{2,3},{3,4},{4,5},{5,6},{6,7},{7,8},{8,9},{9,10},{10,1... | collective-permute-start | bytes 3735560 | tf_op jit(solution)/shard_map/ppermute | solution.py:25
  20.4 24.9 %collective-permute-done = bf16[2432,256]{1,0:T(8,128)(2,1)S(1)} collective-permute-done((bf16[2432,256]{1,0:T(8,128)(2,1)}, bf16[2432,256]{1,0:T(8,128)(2,1)S(1)}, u32[]{:S(2)}, u32[]{:S(2)}) %collective-permute-start) | collective-permute-done | bytes 1245216 | tf_op jit(solution)/shard_map/ppermute | solution.py:25
  45.3 1.9 %collective-permute-start.2 = (bf16[2432,256]{1,0:T(8,128)(2,1)S(1)}, bf16[2432,256]{1,0:T(8,128)(2,1)}, u32[]{:S(2)}, u32[]{:S(2)}) collective-permute-start(bf16[2432,256]{1,0:T(8,128)(2,1)S(1)} %collective-permute-done), channel_id=1, source_target_pairs={{0,12},{12,0},{1,13},{13,1},{2,14},{14,2},{3,15},{15,3},{4,16},{16... | collective-permute-start | bytes 3735560 | tf_op jit(solution)/shard_map/ppermute | solution.py:29
  47.3 1.8 %shard_map.66 = bf16[128,1792]{1,0:T(8,128)(2,1)} custom-call(s32[1]{0:T(128)} %bitcast.6.start_ref, bf16[1,128,7168]{2,1,0:T(8,128)(2,1)} %down_ref.2), custom_call_target="tpu_custom_call" | custom-call | flops 114688000 | bytes 917504 | tf_op jit(solution)/shard_map/pallas_call | solution.py:93
  49.1 1.9 %collective-permute-start.7 = (bf16[128,1792]{1,0:T(8,128)(2,1)}, bf16[128,1792]{1,0:T(8,128)(2,1)S(1)}, u32[]{:S(2)}, u32[]{:S(2)}) collective-permute-start(bf16[128,1792]{1,0:T(8,128)(2,1)} %shard_map.66), channel_id=1, source_target_pairs={{0,1},{1,2},{2,3},{3,4},{4,5},{5,6},{6,7},{7,8},{8,9},{9,10},{10,1... | collective-permute-start | bytes 1376264 | tf_op jit(solution)/shard_map/ppermute | solution.py:25
  51.0 1.7 %shard_map.68 = bf16[128,896]{1,0:T(8,128)(2,1)} custom-call(s32[1]{0:T(128)} %bitcast.8.start_ref, bf16[1,128,7168]{2,1,0:T(8,128)(2,1)} %down_ref.2), custom_call_target="tpu_custom_call" | custom-call | flops 57344000 | bytes 458752 | tf_op jit(solution)/shard_map/pallas_call | solution.py:93
  52.7 5.4 %collective-permute-start.9 = (bf16[128,896]{1,0:T(8,128)(2,1)}, bf16[128,896]{1,0:T(8,128)(2,1)S(1)}, u32[]{:S(2)}, u32[]{:S(2)}) collective-permute-start(bf16[128,896]{1,0:T(8,128)(2,1)} %shard_map.68), channel_id=1, source_target_pairs={{0,10},{1,3},{2,0},{3,5},{4,2},{5,7},{6,4},{7,9},{8,6},{9,11},{10,... | collective-permute-start | bytes 688136 | tf_op jit(solution)/shard_map/ppermute | solution.py:38
  58.1 1.8 %shard_map.67 = bf16[128,1792]{1,0:T(8,128)(2,1)} custom-call(s32[1]{0:T(128)} %bitcast.7.start_ref, bf16[1,128,7168]{2,1,0:T(8,128)(2,1)} %down_ref.2), custom_call_target="tpu_custom_call" | custom-call | flops 114688000 | bytes 917504 | tf_op jit(solution)/shard_map/pallas_call | solution.py:93
  59.9 2.2 %shard_map.64 = bf16[2432,256]{1,0:T(8,128)(2,1)} custom-call(s32[1]{0:T(128)} %bitcast.start_ref, bf16[1,7168,128]{2,1,0:T(8,128)(2,1)} %gate_ref.1, bf16[1,7168,128]{2,1,0:T(8,128)(2,1)} %up_ref.1), custom_call_target="tpu_custom_call" | custom-call | flops 311296000 | bytes 2490368 | tf_op jit(solution)/shard_map/pallas_call | solution.py:93
  62.1 1.6 %collective-permute-done.9 = bf16[128,896]{1,0:T(8,128)(2,1)S(1)} collective-permute-done((bf16[128,896]{1,0:T(8,128)(2,1)}, bf16[128,896]{1,0:T(8,128)(2,1)S(1)}, u32[]{:S(2)}, u32[]{:S(2)}) %collective-permute-start.9) | collective-permute-done | bytes 229408 | tf_op jit(solution)/shard_map/ppermute | solution.py:38
  63.7 2.2 %collective-permute-start.10 = (bf16[128,896]{1,0:T(8,128)(2,1)S(1)}, bf16[128,896]{1,0:T(8,128)(2,1)S(1)}, u32[]{:S(2)}, u32[]{:S(2)}) collective-permute-start(bf16[128,896]{1,0:T(8,128)(2,1)S(1)} %collective-permute-done.9), channel_id=1, source_target_pairs={{0,12},{12,0},{1,13},{13,1},{2,14},{14,2},{3,15},{15,3},{4,16},{16... | collective-permute-start | bytes 688136 | tf_op jit(solution)/shard_map/ppermute | solution.py:29
  65.9 0.0 collective-permute-done.7
  65.9 2.2 %collective-permute-start.8 = (bf16[128,1792]{1,0:T(8,128)(2,1)S(1)}, bf16[128,1792]{1,0:T(8,128)(2,1)}, u32[]{:S(2)}, u32[]{:S(2)}) collective-permute-start(bf16[128,1792]{1,0:T(8,128)(2,1)S(1)} %collective-permute-done.7), channel_id=1, source_target_pairs={{0,12},{12,0},{1,13},{13,1},{2,14},{14,2},{3,15},{15,3},{4,16},{16... | collective-permute-start | bytes 1376264 | tf_op jit(solution)/shard_map/ppermute | solution.py:29
  68.1 0.0 all-to-all-done
  68.1 0.6 fusion.16
  68.7 0.0 copy-start
  68.7 4.9 %collective-permute-start.1 = (bf16[256,256]{0,1:T(8,128)(2,1)S(1)}, bf16[256,256]{0,1:T(8,128)(2,1)S(1)}, u32[]{:S(2)}, u32[]{:S(2)}) collective-permute-start(bf16[256,256]{0,1:T(8,128)(2,1)S(1)} %fusion.16), channel_id=1, source_target_pairs={{0,11},{1,0},{2,1},{3,2},{4,3},{5,4},{6,5},{7,6},{8,7},{9,8},{10,9... | collective-permute-start | bytes 393224 | tf_op jit(solution)/shard_map/ppermute | solution.py:25
  73.6 0.0 collective-permute-done.2
  73.6 1.9 %fusion.19 = bf16[256,256]{0,1:T(8,128)(2,1)S(1)} fusion(bf16[2432,256]{1,0:T(8,128)(2,1)} %collective-permute-done.2, bf16[32,8,2432]{2,1,0:T(8,128)(2,1)S(1)} %all-to-all-done), kind=kOutput, calls=%fused_computation.18 | convolution fusion | flops 318832640 | bytes 2621440 | tf_op jit(solution)/shard_map/dot_general | solution.py:268
  75.6 2.6 %collective-permute-start.3 = (bf16[256,256]{0,1:T(8,128)(2,1)S(1)}, bf16[256,256]{0,1:T(8,128)(2,1)S(1)}, u32[]{:S(2)}, u32[]{:S(2)}) collective-permute-start(bf16[256,256]{0,1:T(8,128)(2,1)S(1)} %fusion.19), channel_id=1, source_target_pairs={{0,1},{1,2},{2,3},{3,4},{4,5},{5,6},{6,7},{7,8},{8,9},{9,10},{10,1... | collective-permute-start | bytes 393224 | tf_op jit(solution)/shard_map/ppermute | solution.py:25
  78.2 0.6 fusion.14
  78.8 0.0 copy-start.1
  78.8 0.0 collective-permute-done.1
  78.8 4.8 %collective-permute-done.3 = bf16[256,256]{0,1:T(8,128)(2,1)S(1)} collective-permute-done((bf16[256,256]{0,1:T(8,128)(2,1)S(1)}, bf16[256,256]{0,1:T(8,128)(2,1)S(1)}, u32[]{:S(2)}, u32[]{:S(2)}) %collective-permute-start.3) | collective-permute-done | bytes 131104 | tf_op jit(solution)/shard_map/ppermute | solution.py:25
  83.6 0.1 convert_add_fusion
  83.7 1.9 %collective-permute-start.4 = (bf16[256,128]{0,1:T(8,128)(2,1)S(1)}, bf16[256,128]{0,1:T(8,128)(2,1)S(1)}, u32[]{:S(2)}, u32[]{:S(2)}) collective-permute-start(bf16[256,128]{0,1:T(8,128)(2,1)S(1)} %fusion.32), channel_id=1, source_target_pairs={{0,1},{1,2},{2,3},{3,4},{4,5},{5,6},{6,7},{7,8},{8,9},{9,10},{10,1... | collective-permute-start | bytes 196616 | tf_op jit(solution)/shard_map/ppermute | solution.py:25
  85.7 5.1 %collective-permute-start.5 = (bf16[256,128]{0,1:T(8,128)(2,1)S(1)}, bf16[256,128]{0,1:T(8,128)(2,1)S(1)}, u32[]{:S(2)}, u32[]{:S(2)}) collective-permute-start(bf16[256,128]{0,1:T(8,128)(2,1)S(1)} %fusion.32), channel_id=1, source_target_pairs={{0,11},{1,0},{2,1},{3,2},{4,3},{5,4},{6,5},{7,6},{8,7},{9,8},{10,9... | collective-permute-start | bytes 196616 | tf_op jit(solution)/shard_map/ppermute | solution.py:25
  90.8 2.4 %collective-permute-start.6 = (bf16[256,128]{0,1:T(8,128)(2,1)S(1)}, bf16[256,128]{0,1:T(8,128)(2,1)S(1)}, u32[]{:S(2)}, u32[]{:S(2)}) collective-permute-start(bf16[256,128]{0,1:T(8,128)(2,1)S(1)} %fusion.32), channel_id=1, source_target_pairs={{0,10},{1,3},{2,0},{3,5},{4,2},{5,7},{6,4},{7,9},{8,6},{9,11},{10,... | collective-permute-start | bytes 196616 | tf_op jit(solution)/shard_map/ppermute | solution.py:38
  93.3 0.0 collective-permute-done.10
  93.3 0.1 broadcast_select_fusion.1
  93.3 0.0 collective-permute-done.8
  93.3 0.0 collective-permute-done.4
  93.3 0.0 collective-permute-done.5
  93.4 4.5 %collective-permute-done.6 = bf16[256,128]{0,1:T(8,128)(2,1)S(1)} collective-permute-done((bf16[256,128]{0,1:T(8,128)(2,1)S(1)}, bf16[256,128]{0,1:T(8,128)(2,1)S(1)}, u32[]{:S(2)}, u32[]{:S(2)}) %collective-permute-start.6) | collective-permute-done | bytes 65568 | tf_op jit(solution)/shard_map/ppermute | solution.py:38
  97.9 0.0 copy-done.1
  97.9 2.6 %fusion = bf16[32,8,1792]{2,1,0:T(8,128)(2,1)} fusion(bf16[128,896]{1,0:T(8,128)(2,1)S(1)} %get-tuple-element.18, bf16[128,896]{1,0:T(8,128)(2,1)S(1)} %get-tuple-element.17, bf16[128,1792]{1,0:T(8,128)(2,1)} %collective-permute-done.8, bf16[128,1792]{1,0:T(8,128)(2,1)S(1)} %copy-done.1, bf16[128,1792]{1,0:T(8,128)(2,1)S(1)} %collective-permute-done.7, ...), kind=kOutput, calls=%fused_computation.1 | convolution fusion | flops 480444416 | bytes 3014656 | tf_op jit(solution)/shard_map/dot_general | solution.py:278
  100.5 9.9 %all-to-all-start.1 = ((bf16[32,8,1792]{2,1,0:T(8,128)(2,1)}), bf16[32,8,1792]{2,1,0:T(8,128)(2,1)S(1)}, u32[]{:S(2)}, u32[]{:S(2)}) async-start(bf16[32,8,1792]{2,1,0:T(8,128)(2,1)} %fusion), calls=%async_computation.1 | async-start | bytes 1835008 | tf_op jit(solution)/shard_map/all_to_all | solution.py:33
  110.4 0.0 copy-done.2
  110.4 0.7 copy.7.ids_ref
  111.1 0.7 copy.8.route_ref
  111.8 1.6 %weigh.1 = bf16[2,24,256]{2,1,0:T(8,128)(2,1)} custom-call(s32[24,8]{1,0:T(8,128)} %copy.7.ids_ref, f32[24,8]{1,0:T(8,128)} %copy.8.route_ref), custom_call_target="tpu_custom_call" | custom-call | flops 67108864 | bytes 32768 | tf_op jit(solution)/shard_map/weigh/pallas_call | solution.py:217
  113.3 17.9 %all-to-all-done.1 = bf16[32,8,1792]{2,1,0:T(8,128)(2,1)S(1)} async-done(((bf16[32,8,1792]{2,1,0:T(8,128)(2,1)}), bf16[32,8,1792]{2,1,0:T(8,128)(2,1)S(1)}, u32[]{:S(2)}, u32[]{:S(2)}) %all-to-all-start.1) | async-done | bytes 917536 | tf_op jit(solution)/shard_map/all_to_all | solution.py:33
  131.2 1.0 fusion.22
  132.3 17.6 %all_to_all.15 = bf16[12,2,1792]{2,1,0:T(2,128)(2,1)S(1)} all-to-all(bf16[12,2,1792]{2,1,0:T(2,128)(2,1)S(1)} %reshape.51), channel_id=1, replica_groups=mesh['ep'=32,'dp'=2,'tp'=12] {'tp'}, dimensions={0} | all-to-all | bytes 172032 | tf_op jit(solution)/shard_map/all_to_all | solution.py:33
  150.0 0.6 pad_maximum_fusion
  (9 shorter events, 0.2 us)
Async XLA Ops:
  3.2 64.9 %all-to-all-start = ((bf16[32,8,2432]{2,1,0:T(8,128)(2,1)}), bf16[32,8,2432]{2,1,0:T(8,128)(2,1)S(1)}, u32[]{:S(2)}, u32[]{:S(2)}) async-start(bf16[32,8,2432]{2,1,0:T(8,128)(2,1)} %bitcast.36), calls=%async_computation | async-start | bytes 2490368 | tf_op jit(solution)/shard_map/all_to_all | solution.py:33
  18.5 26.8 %collective-permute-start = (bf16[2432,256]{1,0:T(8,128)(2,1)}, bf16[2432,256]{1,0:T(8,128)(2,1)S(1)}, u32[]{:S(2)}, u32[]{:S(2)}) collective-permute-start(bf16[2432,256]{1,0:T(8,128)(2,1)} %shard_map.65), channel_id=1, source_target_pairs={{0,1},{1,2},{2,3},{3,4},{4,5},{5,6},{6,7},{7,8},{8,9},{9,10},{10,1... | collective-permute-start | bytes 3735560 | tf_op jit(solution)/shard_map/ppermute | solution.py:25
  45.3 28.3 %collective-permute-start.2 = (bf16[2432,256]{1,0:T(8,128)(2,1)S(1)}, bf16[2432,256]{1,0:T(8,128)(2,1)}, u32[]{:S(2)}, u32[]{:S(2)}) collective-permute-start(bf16[2432,256]{1,0:T(8,128)(2,1)S(1)} %collective-permute-done), channel_id=1, source_target_pairs={{0,12},{12,0},{1,13},{13,1},{2,14},{14,2},{3,15},{15,3},{4,16},{16... | collective-permute-start | bytes 3735560 | tf_op jit(solution)/shard_map/ppermute | solution.py:29
  49.1 16.8 %collective-permute-start.7 = (bf16[128,1792]{1,0:T(8,128)(2,1)}, bf16[128,1792]{1,0:T(8,128)(2,1)S(1)}, u32[]{:S(2)}, u32[]{:S(2)}) collective-permute-start(bf16[128,1792]{1,0:T(8,128)(2,1)} %shard_map.66), channel_id=1, source_target_pairs={{0,1},{1,2},{2,3},{3,4},{4,5},{5,6},{6,7},{7,8},{8,9},{9,10},{10,1... | collective-permute-start | bytes 1376264 | tf_op jit(solution)/shard_map/ppermute | solution.py:25
  52.7 11.0 %collective-permute-start.9 = (bf16[128,896]{1,0:T(8,128)(2,1)}, bf16[128,896]{1,0:T(8,128)(2,1)S(1)}, u32[]{:S(2)}, u32[]{:S(2)}) collective-permute-start(bf16[128,896]{1,0:T(8,128)(2,1)} %shard_map.68), channel_id=1, source_target_pairs={{0,10},{1,3},{2,0},{3,5},{4,2},{5,7},{6,4},{7,9},{8,6},{9,11},{10,... | collective-permute-start | bytes 688136 | tf_op jit(solution)/shard_map/ppermute | solution.py:38
  63.7 29.5 %collective-permute-start.10 = (bf16[128,896]{1,0:T(8,128)(2,1)S(1)}, bf16[128,896]{1,0:T(8,128)(2,1)S(1)}, u32[]{:S(2)}, u32[]{:S(2)}) collective-permute-start(bf16[128,896]{1,0:T(8,128)(2,1)S(1)} %collective-permute-done.9), channel_id=1, source_target_pairs={{0,12},{12,0},{1,13},{13,1},{2,14},{14,2},{3,15},{15,3},{4,16},{16... | collective-permute-start | bytes 688136 | tf_op jit(solution)/shard_map/ppermute | solution.py:29
  65.9 27.4 %collective-permute-start.8 = (bf16[128,1792]{1,0:T(8,128)(2,1)S(1)}, bf16[128,1792]{1,0:T(8,128)(2,1)}, u32[]{:S(2)}, u32[]{:S(2)}) collective-permute-start(bf16[128,1792]{1,0:T(8,128)(2,1)S(1)} %collective-permute-done.7), channel_id=1, source_target_pairs={{0,12},{12,0},{1,13},{13,1},{2,14},{14,2},{3,15},{15,3},{4,16},{16... | collective-permute-start | bytes 1376264 | tf_op jit(solution)/shard_map/ppermute | solution.py:29
  68.7 9.4 %copy-start = (bf16[2432,256]{1,0:T(8,128)(2,1)S(1)}, bf16[2432,256]{1,0:T(8,128)(2,1)}, u32[]{:S(2)}) copy-start(bf16[2432,256]{1,0:T(8,128)(2,1)} %shard_map.64) | copy-start | bytes 3735556
  68.7 10.1 %collective-permute-start.1 = (bf16[256,256]{0,1:T(8,128)(2,1)S(1)}, bf16[256,256]{0,1:T(8,128)(2,1)S(1)}, u32[]{:S(2)}, u32[]{:S(2)}) collective-permute-start(bf16[256,256]{0,1:T(8,128)(2,1)S(1)} %fusion.16), channel_id=1, source_target_pairs={{0,11},{1,0},{2,1},{3,2},{4,3},{5,4},{6,5},{7,6},{8,7},{9,8},{10,9... | collective-permute-start | bytes 393224 | tf_op jit(solution)/shard_map/ppermute | solution.py:25
  75.6 8.1 %collective-permute-start.3 = (bf16[256,256]{0,1:T(8,128)(2,1)S(1)}, bf16[256,256]{0,1:T(8,128)(2,1)S(1)}, u32[]{:S(2)}, u32[]{:S(2)}) collective-permute-start(bf16[256,256]{0,1:T(8,128)(2,1)S(1)} %fusion.19), channel_id=1, source_target_pairs={{0,1},{1,2},{2,3},{3,4},{4,5},{5,6},{6,7},{7,8},{8,9},{9,10},{10,1... | collective-permute-start | bytes 393224 | tf_op jit(solution)/shard_map/ppermute | solution.py:25
  78.8 19.1 %copy-start.1 = (bf16[128,1792]{1,0:T(8,128)(2,1)S(1)}, bf16[128,1792]{1,0:T(8,128)(2,1)}, u32[]{:S(2)}) copy-start(bf16[128,1792]{1,0:T(8,128)(2,1)} %shard_map.67) | copy-start | bytes 1376260
  83.7 9.6 %collective-permute-start.4 = (bf16[256,128]{0,1:T(8,128)(2,1)S(1)}, bf16[256,128]{0,1:T(8,128)(2,1)S(1)}, u32[]{:S(2)}, u32[]{:S(2)}) collective-permute-start(bf16[256,128]{0,1:T(8,128)(2,1)S(1)} %fusion.32), channel_id=1, source_target_pairs={{0,1},{1,2},{2,3},{3,4},{4,5},{5,6},{6,7},{7,8},{8,9},{9,10},{10,1... | collective-permute-start | bytes 196616 | tf_op jit(solution)/shard_map/ppermute | solution.py:25
  85.7 7.7 %collective-permute-start.5 = (bf16[256,128]{0,1:T(8,128)(2,1)S(1)}, bf16[256,128]{0,1:T(8,128)(2,1)S(1)}, u32[]{:S(2)}, u32[]{:S(2)}) collective-permute-start(bf16[256,128]{0,1:T(8,128)(2,1)S(1)} %fusion.32), channel_id=1, source_target_pairs={{0,11},{1,0},{2,1},{3,2},{4,3},{5,4},{6,5},{7,6},{8,7},{9,8},{10,9... | collective-permute-start | bytes 196616 | tf_op jit(solution)/shard_map/ppermute | solution.py:25
  90.8 7.1 %collective-permute-start.6 = (bf16[256,128]{0,1:T(8,128)(2,1)S(1)}, bf16[256,128]{0,1:T(8,128)(2,1)S(1)}, u32[]{:S(2)}, u32[]{:S(2)}) collective-permute-start(bf16[256,128]{0,1:T(8,128)(2,1)S(1)} %fusion.32), channel_id=1, source_target_pairs={{0,10},{1,3},{2,0},{3,5},{4,2},{5,7},{6,4},{7,9},{8,6},{9,11},{10,... | collective-permute-start | bytes 196616 | tf_op jit(solution)/shard_map/ppermute | solution.py:38
  100.5 9.9 %copy-start.2 = (s32[24,8]{0,1:T(8,128)S(1)}, s32[24,8]{0,1:T(8,128)}, u32[]{:S(2)}) copy-start(s32[24,8]{0,1:T(8,128)} %param.7) | copy-start | bytes 2308
  100.5 10.6 %copy-start.3 = (f32[24,8]{0,1:T(8,128)S(1)}, f32[24,8]{0,1:T(8,128)}, u32[]{:S(2)}) copy-start(f32[24,8]{0,1:T(8,128)} %param.8) | copy-start | bytes 2308
  100.5 30.7 %all-to-all-start.1 = ((bf16[32,8,1792]{2,1,0:T(8,128)(2,1)}), bf16[32,8,1792]{2,1,0:T(8,128)(2,1)S(1)}, u32[]{:S(2)}, u32[]{:S(2)}) async-start(bf16[32,8,1792]{2,1,0:T(8,128)(2,1)} %fusion), calls=%async_computation.1 | async-start | bytes 1835008 | tf_op jit(solution)/shard_map/all_to_all | solution.py:33

commit v9 on v8

--- a/solution.py
+++ b/solution.py
@@ -31,13 +31,6 @@
 
 def exchange(array, axis):
     return lax.all_to_all(array, axis, split_axis=0, concat_axis=0, tiled=True)
-
-
-def hop_two(array):
-    size = lax.axis_size("tp")
-    return lax.ppermute(
-        array, "tp", [(i, (i + (2 if i % 2 else size - 2)) % size) for i in range(size)]
-    )
 
 
 def piece_width(width):
@@ -115,13 +108,10 @@
     return cut(cut_gate_up, piece_start(index, width), arrays, shape, pl.ANY, scratch)
 
 
-def down_piece(down_weight, index, half=None):
+def down_piece(down_weight, index):
     units, width = down_weight.shape[1:]
     size = width // BACK
     start = lax.rem(index, BACK) * size
-    if half is not None:
-        size //= 2
-        start = start + half * size
     scratch = [pltpu.SemaphoreType.DMA((1,))]
     return cut(cut_down, start, (down_weight,), (units, size), pltpu.VMEM, scratch)
 
@@ -240,7 +230,7 @@
     here = lax.axis_index("tp")
     core = lax.axis_index("dp")
     target = lax.rem(here + jnp.where(core == 0, 1, tp_size - 1), tp_size)
-    target_two = lax.rem(here + jnp.where(lax.rem(here, 2) == 0, tp_size - 2, 2), tp_size)
+    target_two = lax.rem(here + jnp.where(core == 0, tp_size - 2, 2), tp_size)
 
     outgoing = dispatch(tokens, expert_ids, here)
     outgoing, gate_weight, up_weight, down_weight, expert_ids, route_weight = (
@@ -255,11 +245,7 @@
     gate_up_far = swap(gate_up_near)
     down_near = shift(down_piece(down_weight, target), 1)
     down_far = swap(down_near)
-    mine = hop_two(down_piece(down_weight, target_two, core))
-    other = swap(mine)
-    down_two = jnp.concatenate(
-        [jnp.where(core == 0, mine, other), jnp.where(core == 0, other, mine)], 1
-    )
+    down_two = shift(down_piece(down_weight, target_two), -2)
     gate_up_here = gate_up_piece(gate_weight, up_weight, here)
     down_here = down_piece(down_weight, here)
     weights = weigh(expert_ids, route_weight)
@@ -272,7 +258,7 @@
     gate_up = product(gate_up_here)
     gate_up = gate_up + from_far.astype(jnp.float32) + from_near.astype(jnp.float32)
     hidden = (jax.nn.silu(gate_up[:, :units]) * gate_up[:, units:]).astype(jnp.bfloat16)
-    hidden_two = hop_two(hidden)
+    hidden_two = shift(hidden, -2)
     hidden_near = shift(hidden, 1)
     hidden_far = shift(hidden, -1)
     partial_rows = jnp.dot(

time: 152 us -> 151 us (level)
  the two profiles are of different devices: /device:TPU:4 before, /device:TPU:2 now
where the time goes in v9:
time: 151 us; the launch traced here: 150 us
  waiting for transfers between devices  53.5 us (35%)
  starting transfers between devices  51.4 us (34%)
  blocking collectives  20.8 us (14%)
  Pallas kernels  14.5 us (10%)
  matrix products  6.95 us (5%)
    ppermute x8, waiting for transfers between devices, shift(): return lax.ppermute(array, ('dp', 'tp'), pairs)  35.2 us
    ppermute x8, starting transfers between devices, shift(): return lax.ppermute(array, ('dp', 'tp'), pairs)  24.6 us
    all_to_all x2, starting transfers between devices, exchange(): return lax.all_to_all(array, axis, split_axis=0, concat_axis=0, tiled=True)  23 us
    all_to_all x1, blocking collectives, exchange(): return lax.all_to_all(array, axis, split_axis=0, concat_axis=0, tiled=True)  20.8 us
    all_to_all x2, waiting for transfers between devices, exchange(): return lax.all_to_all(array, axis, split_axis=0, concat_axis=0, tiled=True)  18.2 us
    pallas_call x5, Pallas kernels, cut(): pl.pallas_call(kernel, out_shape=jax.ShapeDtypeStruct(shape, jnp.bfloat16...  9.82 us
    ppermute x2, starting transfers between devices, swap(): return lax.ppermute(array, 'dp', [(0, 1), (1, 0)])  3.82 us
    dot_general x3, matrix products, product(): return jnp.dot(received, weights, preferred_element_type=jnp.float32)  3.18 us
  transfers between devices with their start and end apart: 12, of which 5 were waited for; matrix products, arithmetic and copies ran while one was open for 3% of the time, Pallas kernels for 8%

profile of v9, /device:TPU:2, one launch (start us, length us, event | category | flops | bytes accessed | tf_op | source)
XLA Modules:
  0.0 149.7 jit_solution(16836562727382783133)
XLA Ops:
  0.0 3.1 %dispatch.1 = bf16[256,2432]{1,0:T(8,128)(2,1)} custom-call(s32[1]{0:T(128)} %bitcast.start_ref, s32[8,24]{1,0:T(8,128)} %bitcast.38, bf16[24,7168]{1,0:T(8,128)(2,1)} %tokens_ref.1), custom_call_target="tpu_custom_call" | custom-call | flops 29884416 | bytes 2097152 | tf_op jit(solution)/shard_map/dispatch/pallas_call | solution.py:162
  3.2 13.1 %all-to-all-start = ((bf16[32,8,2432]{2,1,0:T(8,128)(2,1)}), bf16[32,8,2432]{2,1,0:T(8,128)(2,1)S(1)}, u32[]{:S(2)}, u32[]{:S(2)}) async-start(bf16[32,8,2432]{2,1,0:T(8,128)(2,1)} %bitcast.36), calls=%async_computation | async-start | bytes 2490368 | tf_op jit(solution)/shard_map/all_to_all | solution.py:33
  16.3 2.2 %shard_map.65 = bf16[2432,256]{1,0:T(8,128)(2,1)} custom-call(s32[1]{0:T(128)} %bitcast.5.start_ref, bf16[1,7168,128]{2,1,0:T(8,128)(2,1)} %gate_ref.1, bf16[1,7168,128]{2,1,0:T(8,128)(2,1)} %up_ref.1), custom_call_target="tpu_custom_call" | custom-call | flops 311296000 | bytes 2490368 | tf_op jit(solution)/shard_map/pallas_call | solution.py:86
  18.5 1.9 %collective-permute-start = (bf16[2432,256]{1,0:T(8,128)(2,1)}, bf16[2432,256]{1,0:T(8,128)(2,1)S(1)}, u32[]{:S(2)}, u32[]{:S(2)}) collective-permute-start(bf16[2432,256]{1,0:T(8,128)(2,1)} %shard_map.65), channel_id=1, source_target_pairs={{0,1},{1,2},{2,3},{3,4},{4,5},{5,6},{6,7},{7,8},{8,9},{9,10},{10,1... | collective-permute-start | bytes 3735560 | tf_op jit(solution)/shard_map/ppermute | solution.py:25
  20.5 24.9 %collective-permute-done = bf16[2432,256]{1,0:T(8,128)(2,1)S(1)} collective-permute-done((bf16[2432,256]{1,0:T(8,128)(2,1)}, bf16[2432,256]{1,0:T(8,128)(2,1)S(1)}, u32[]{:S(2)}, u32[]{:S(2)}) %collective-permute-start) | collective-permute-done | bytes 1245216 | tf_op jit(solution)/shard_map/ppermute | solution.py:25
  45.3 1.9 %collective-permute-start.2 = (bf16[2432,256]{1,0:T(8,128)(2,1)S(1)}, bf16[2432,256]{1,0:T(8,128)(2,1)}, u32[]{:S(2)}, u32[]{:S(2)}) collective-permute-start(bf16[2432,256]{1,0:T(8,128)(2,1)S(1)} %collective-permute-done), channel_id=1, source_target_pairs={{0,12},{12,0},{1,13},{13,1},{2,14},{14,2},{3,15},{15,3},{4,16},{16... | collective-permute-start | bytes 3735560 | tf_op jit(solution)/shard_map/ppermute | solution.py:29
  47.3 1.8 %shard_map.66 = bf16[128,1792]{1,0:T(8,128)(2,1)} custom-call(s32[1]{0:T(128)} %bitcast.6.start_ref, bf16[1,128,7168]{2,1,0:T(8,128)(2,1)} %down_ref.2), custom_call_target="tpu_custom_call" | custom-call | flops 114688000 | bytes 917504 | tf_op jit(solution)/shard_map/pallas_call | solution.py:86
  49.1 1.9 %collective-permute-start.7 = (bf16[128,1792]{1,0:T(8,128)(2,1)}, bf16[128,1792]{1,0:T(8,128)(2,1)S(1)}, u32[]{:S(2)}, u32[]{:S(2)}) collective-permute-start(bf16[128,1792]{1,0:T(8,128)(2,1)} %shard_map.66), channel_id=1, source_target_pairs={{0,1},{1,2},{2,3},{3,4},{4,5},{5,6},{6,7},{7,8},{8,9},{9,10},{10,1... | collective-permute-start | bytes 1376264 | tf_op jit(solution)/shard_map/ppermute | solution.py:25
  51.0 1.8 %shard_map.68 = bf16[128,1792]{1,0:T(8,128)(2,1)} custom-call(s32[1]{0:T(128)} %bitcast.8.start_ref, bf16[1,128,7168]{2,1,0:T(8,128)(2,1)} %down_ref.2), custom_call_target="tpu_custom_call" | custom-call | flops 114688000 | bytes 917504 | tf_op jit(solution)/shard_map/pallas_call | solution.py:86
  52.8 5.4 %collective-permute-start.9 = (bf16[128,1792]{1,0:T(8,128)(2,1)}, bf16[128,1792]{1,0:T(8,128)(2,1)S(1)}, u32[]{:S(2)}, u32[]{:S(2)}) collective-permute-start(bf16[128,1792]{1,0:T(8,128)(2,1)} %shard_map.68), channel_id=1, source_target_pairs={{0,10},{1,11},{2,0},{3,1},{4,2},{5,3},{6,4},{7,5},{8,6},{9,7},{10,... | collective-permute-start | bytes 1376264 | tf_op jit(solution)/shard_map/ppermute | solution.py:25
  58.2 2.2 %shard_map.64 = bf16[2432,256]{1,0:T(8,128)(2,1)} custom-call(s32[1]{0:T(128)} %bitcast.start_ref, bf16[1,7168,128]{2,1,0:T(8,128)(2,1)} %gate_ref.1, bf16[1,7168,128]{2,1,0:T(8,128)(2,1)} %up_ref.1), custom_call_target="tpu_custom_call" | custom-call | flops 311296000 | bytes 2490368 | tf_op jit(solution)/shard_map/pallas_call | solution.py:86
  60.4 0.9 collective-permute-done.7
  61.3 1.9 %collective-permute-start.8 = (bf16[128,1792]{1,0:T(8,128)(2,1)S(1)}, bf16[128,1792]{1,0:T(8,128)(2,1)}, u32[]{:S(2)}, u32[]{:S(2)}) collective-permute-start(bf16[128,1792]{1,0:T(8,128)(2,1)S(1)} %collective-permute-done.7), channel_id=1, source_target_pairs={{0,12},{12,0},{1,13},{13,1},{2,14},{14,2},{3,15},{15,3},{4,16},{16... | collective-permute-start | bytes 1376264 | tf_op jit(solution)/shard_map/ppermute | solution.py:29
  63.2 0.0 all-to-all-done
  63.2 0.6 fusion.14
  63.9 0.0 copy-start
  63.9 2.9 %collective-permute-start.1 = (bf16[256,256]{0,1:T(8,128)(2,1)S(1)}, bf16[256,256]{0,1:T(8,128)(2,1)S(1)}, u32[]{:S(2)}, u32[]{:S(2)}) collective-permute-start(bf16[256,256]{0,1:T(8,128)(2,1)S(1)} %fusion.14), channel_id=1, source_target_pairs={{0,11},{1,0},{2,1},{3,2},{4,3},{5,4},{6,5},{7,6},{8,7},{9,8},{10,9... | collective-permute-start | bytes 393224 | tf_op jit(solution)/shard_map/ppermute | solution.py:25
  66.8 0.0 collective-permute-done.2
  66.8 1.9 %fusion.17 = bf16[256,256]{0,1:T(8,128)(2,1)S(1)} fusion(bf16[2432,256]{1,0:T(8,128)(2,1)} %collective-permute-done.2, bf16[32,8,2432]{2,1,0:T(8,128)(2,1)S(1)} %all-to-all-done), kind=kOutput, calls=%fused_computation.16 | convolution fusion | flops 318832640 | bytes 2621440 | tf_op jit(solution)/shard_map/dot_general | solution.py:254
  68.8 3.0 %collective-permute-start.3 = (bf16[256,256]{0,1:T(8,128)(2,1)S(1)}, bf16[256,256]{0,1:T(8,128)(2,1)S(1)}, u32[]{:S(2)}, u32[]{:S(2)}) collective-permute-start(bf16[256,256]{0,1:T(8,128)(2,1)S(1)} %fusion.17), channel_id=1, source_target_pairs={{0,1},{1,2},{2,3},{3,4},{4,5},{5,6},{6,7},{7,8},{8,9},{9,10},{10,1... | collective-permute-start | bytes 393224 | tf_op jit(solution)/shard_map/ppermute | solution.py:25
  71.8 0.0 copy-done
  71.8 0.6 fusion.12
  72.5 0.0 collective-permute-done.1
  72.5 6.5 %collective-permute-done.3 = bf16[256,256]{0,1:T(8,128)(2,1)S(1)} collective-permute-done((bf16[256,256]{0,1:T(8,128)(2,1)S(1)}, bf16[256,256]{0,1:T(8,128)(2,1)S(1)}, u32[]{:S(2)}, u32[]{:S(2)}) %collective-permute-start.3) | collective-permute-done | bytes 131104 | tf_op jit(solution)/shard_map/ppermute | solution.py:25
  79.1 1.9 %collective-permute-start.4 = (bf16[256,128]{0,1:T(8,128)(2,1)S(1)}, bf16[256,128]{0,1:T(8,128)(2,1)S(1)}, u32[]{:S(2)}, u32[]{:S(2)}) collective-permute-start(bf16[256,128]{0,1:T(8,128)(2,1)S(1)} %fusion.30), channel_id=1, source_target_pairs={{0,1},{1,2},{2,3},{3,4},{4,5},{5,6},{6,7},{7,8},{8,9},{9,10},{10,1... | collective-permute-start | bytes 196616 | tf_op jit(solution)/shard_map/ppermute | solution.py:25
  81.0 5.1 %collective-permute-start.5 = (bf16[256,128]{0,1:T(8,128)(2,1)S(1)}, bf16[256,128]{0,1:T(8,128)(2,1)S(1)}, u32[]{:S(2)}, u32[]{:S(2)}) collective-permute-start(bf16[256,128]{0,1:T(8,128)(2,1)S(1)} %fusion.30), channel_id=1, source_target_pairs={{0,11},{1,0},{2,1},{3,2},{4,3},{5,4},{6,5},{7,6},{8,7},{9,8},{10,9... | collective-permute-start | bytes 196616 | tf_op jit(solution)/shard_map/ppermute | solution.py:25
  86.2 2.3 %collective-permute-start.6 = (bf16[256,128]{0,1:T(8,128)(2,1)S(1)}, bf16[256,128]{0,1:T(8,128)(2,1)S(1)}, u32[]{:S(2)}, u32[]{:S(2)}) collective-permute-start(bf16[256,128]{0,1:T(8,128)(2,1)S(1)} %fusion.30), channel_id=1, source_target_pairs={{0,10},{1,11},{2,0},{3,1},{4,2},{5,3},{6,4},{7,5},{8,6},{9,7},{10,... | collective-permute-start | bytes 196616 | tf_op jit(solution)/shard_map/ppermute | solution.py:25
  88.5 1.8 %shard_map.67 = bf16[128,1792]{1,0:T(8,128)(2,1)} custom-call(s32[1]{0:T(128)} %bitcast.7.start_ref, bf16[1,128,7168]{2,1,0:T(8,128)(2,1)} %down_ref.2), custom_call_target="tpu_custom_call" | custom-call | flops 114688000 | bytes 917504 | tf_op jit(solution)/shard_map/pallas_call | solution.py:86
  90.3 0.0 collective-permute-done.9
  90.3 0.0 collective-permute-done.8
  90.4 0.0 collective-permute-done.4
  90.4 0.0 collective-permute-done.5
  90.4 2.9 %collective-permute-done.6 = bf16[256,128]{0,1:T(8,128)(2,1)S(1)} collective-permute-done((bf16[256,128]{0,1:T(8,128)(2,1)S(1)}, bf16[256,128]{0,1:T(8,128)(2,1)S(1)}, u32[]{:S(2)}, u32[]{:S(2)}) %collective-permute-start.6) | collective-permute-done | bytes 65568 | tf_op jit(solution)/shard_map/ppermute | solution.py:25
  93.3 2.7 %fusion = bf16[32,8,1792]{2,1,0:T(8,128)(2,1)} fusion(bf16[128,1792]{1,0:T(8,128)(2,1)S(1)} %collective-permute-done.9, bf16[128,1792]{1,0:T(8,128)(2,1)} %collective-permute-done.8, bf16[128,1792]{1,0:T(8,128)(2,1)} %shard_map.67, bf16[128,1792]{1,0:T(8,128)(2,1)S(1)} %collective-permute-done.7, bf16[256,128]{0,1:T(8,128)(2,1)S(1)} %collective-permute-done.6, ...), kind=kOutput, calls=%fused_computation.1 | convolution fusion | flops 478609408 | bytes 3014656 | tf_op jit(solution)/shard_map/dot_general | solution.py:264
  96.0 0.0 copy-start.1
  96.0 0.0 copy-start.2
  96.0 9.9 %all-to-all-start.1 = ((bf16[32,8,1792]{2,1,0:T(8,128)(2,1)}), bf16[32,8,1792]{2,1,0:T(8,128)(2,1)S(1)}, u32[]{:S(2)}, u32[]{:S(2)}) async-start(bf16[32,8,1792]{2,1,0:T(8,128)(2,1)} %fusion), calls=%async_computation.1 | async-start | bytes 1835008 | tf_op jit(solution)/shard_map/all_to_all | solution.py:33
  105.9 0.0 copy-done.1
  105.9 0.7 copy.7.ids_ref
  106.6 0.0 copy-done.2
  106.6 0.7 copy.8.route_ref
  107.3 1.6 %weigh.1 = bf16[2,24,256]{2,1,0:T(8,128)(2,1)} custom-call(s32[24,8]{1,0:T(8,128)} %copy.7.ids_ref, f32[24,8]{1,0:T(8,128)} %copy.8.route_ref), custom_call_target="tpu_custom_call" | custom-call | flops 67108864 | bytes 32768 | tf_op jit(solution)/shard_map/weigh/pallas_call | solution.py:207
  108.9 18.2 %all-to-all-done.1 = bf16[32,8,1792]{2,1,0:T(8,128)(2,1)S(1)} async-done(((bf16[32,8,1792]{2,1,0:T(8,128)(2,1)}), bf16[32,8,1792]{2,1,0:T(8,128)(2,1)S(1)}, u32[]{:S(2)}, u32[]{:S(2)}) %all-to-all-start.1) | async-done | bytes 917536 | tf_op jit(solution)/shard_map/all_to_all | solution.py:33
  127.1 1.0 fusion.20
  128.2 20.8 %all_to_all.15 = bf16[12,2,1792]{2,1,0:T(2,128)(2,1)S(1)} all-to-all(bf16[12,2,1792]{2,1,0:T(2,128)(2,1)S(1)} %reshape.51), channel_id=1, replica_groups=mesh['ep'=32,'dp'=2,'tp'=12] {'tp'}, dimensions={0} | all-to-all | bytes 172032 | tf_op jit(solution)/shard_map/all_to_all | solution.py:33
  149.1 0.6 pad_maximum_fusion
  (6 shorter events, 0.2 us)
Async XLA Ops:
  3.2 60.1 %all-to-all-start = ((bf16[32,8,2432]{2,1,0:T(8,128)(2,1)}), bf16[32,8,2432]{2,1,0:T(8,128)(2,1)S(1)}, u32[]{:S(2)}, u32[]{:S(2)}) async-start(bf16[32,8,2432]{2,1,0:T(8,128)(2,1)} %bitcast.36), calls=%async_computation | async-start | bytes 2490368 | tf_op jit(solution)/shard_map/all_to_all | solution.py:33
  18.5 26.8 %collective-permute-start = (bf16[2432,256]{1,0:T(8,128)(2,1)}, bf16[2432,256]{1,0:T(8,128)(2,1)S(1)}, u32[]{:S(2)}, u32[]{:S(2)}) collective-permute-start(bf16[2432,256]{1,0:T(8,128)(2,1)} %shard_map.65), channel_id=1, source_target_pairs={{0,1},{1,2},{2,3},{3,4},{4,5},{5,6},{6,7},{7,8},{8,9},{9,10},{10,1... | collective-permute-start | bytes 3735560 | tf_op jit(solution)/shard_map/ppermute | solution.py:25
  45.3 21.5 %collective-permute-start.2 = (bf16[2432,256]{1,0:T(8,128)(2,1)S(1)}, bf16[2432,256]{1,0:T(8,128)(2,1)}, u32[]{:S(2)}, u32[]{:S(2)}) collective-permute-start(bf16[2432,256]{1,0:T(8,128)(2,1)S(1)} %collective-permute-done), channel_id=1, source_target_pairs={{0,12},{12,0},{1,13},{13,1},{2,14},{14,2},{3,15},{15,3},{4,16},{16... | collective-permute-start | bytes 3735560 | tf_op jit(solution)/shard_map/ppermute | solution.py:29
  49.1 12.2 %collective-permute-start.7 = (bf16[128,1792]{1,0:T(8,128)(2,1)}, bf16[128,1792]{1,0:T(8,128)(2,1)S(1)}, u32[]{:S(2)}, u32[]{:S(2)}) collective-permute-start(bf16[128,1792]{1,0:T(8,128)(2,1)} %shard_map.66), channel_id=1, source_target_pairs={{0,1},{1,2},{2,3},{3,4},{4,5},{5,6},{6,7},{7,8},{8,9},{9,10},{10,1... | collective-permute-start | bytes 1376264 | tf_op jit(solution)/shard_map/ppermute | solution.py:25
  52.8 37.5 %collective-permute-start.9 = (bf16[128,1792]{1,0:T(8,128)(2,1)}, bf16[128,1792]{1,0:T(8,128)(2,1)S(1)}, u32[]{:S(2)}, u32[]{:S(2)}) collective-permute-start(bf16[128,1792]{1,0:T(8,128)(2,1)} %shard_map.68), channel_id=1, source_target_pairs={{0,10},{1,11},{2,0},{3,1},{4,2},{5,3},{6,4},{7,5},{8,6},{9,7},{10,... | collective-permute-start | bytes 1376264 | tf_op jit(solution)/shard_map/ppermute | solution.py:25
  61.3 29.0 %collective-permute-start.8 = (bf16[128,1792]{1,0:T(8,128)(2,1)S(1)}, bf16[128,1792]{1,0:T(8,128)(2,1)}, u32[]{:S(2)}, u32[]{:S(2)}) collective-permute-start(bf16[128,1792]{1,0:T(8,128)(2,1)S(1)} %collective-permute-done.7), channel_id=1, source_target_pairs={{0,12},{12,0},{1,13},{13,1},{2,14},{14,2},{3,15},{15,3},{4,16},{16... | collective-permute-start | bytes 1376264 | tf_op jit(solution)/shard_map/ppermute | solution.py:29
  63.9 7.9 %copy-start = (bf16[2432,256]{1,0:T(8,128)(2,1)S(1)}, bf16[2432,256]{1,0:T(8,128)(2,1)}, u32[]{:S(2)}) copy-start(bf16[2432,256]{1,0:T(8,128)(2,1)} %shard_map.64) | copy-start | bytes 3735556
  63.9 8.6 %collective-permute-start.1 = (bf16[256,256]{0,1:T(8,128)(2,1)S(1)}, bf16[256,256]{0,1:T(8,128)(2,1)S(1)}, u32[]{:S(2)}, u32[]{:S(2)}) collective-permute-start(bf16[256,256]{0,1:T(8,128)(2,1)S(1)} %fusion.14), channel_id=1, source_target_pairs={{0,11},{1,0},{2,1},{3,2},{4,3},{5,4},{6,5},{7,6},{8,7},{9,8},{10,9... | collective-permute-start | bytes 393224 | tf_op jit(solution)/shard_map/ppermute | solution.py:25
  68.8 10.3 %collective-permute-start.3 = (bf16[256,256]{0,1:T(8,128)(2,1)S(1)}, bf16[256,256]{0,1:T(8,128)(2,1)S(1)}, u32[]{:S(2)}, u32[]{:S(2)}) collective-permute-start(bf16[256,256]{0,1:T(8,128)(2,1)S(1)} %fusion.17), channel_id=1, source_target_pairs={{0,1},{1,2},{2,3},{3,4},{4,5},{5,6},{6,7},{7,8},{8,9},{9,10},{10,1... | collective-permute-start | bytes 393224 | tf_op jit(solution)/shard_map/ppermute | solution.py:25
  79.1 11.2 %collective-permute-start.4 = (bf16[256,128]{0,1:T(8,128)(2,1)S(1)}, bf16[256,128]{0,1:T(8,128)(2,1)S(1)}, u32[]{:S(2)}, u32[]{:S(2)}) collective-permute-start(bf16[256,128]{0,1:T(8,128)(2,1)S(1)} %fusion.30), channel_id=1, source_target_pairs={{0,1},{1,2},{2,3},{3,4},{4,5},{5,6},{6,7},{7,8},{8,9},{9,10},{10,1... | collective-permute-start | bytes 196616 | tf_op jit(solution)/shard_map/ppermute | solution.py:25
  81.0 9.3 %collective-permute-start.5 = (bf16[256,128]{0,1:T(8,128)(2,1)S(1)}, bf16[256,128]{0,1:T(8,128)(2,1)S(1)}, u32[]{:S(2)}, u32[]{:S(2)}) collective-permute-start(bf16[256,128]{0,1:T(8,128)(2,1)S(1)} %fusion.30), channel_id=1, source_target_pairs={{0,11},{1,0},{2,1},{3,2},{4,3},{5,4},{6,5},{7,6},{8,7},{9,8},{10,9... | collective-permute-start | bytes 196616 | tf_op jit(solution)/shard_map/ppermute | solution.py:25
  86.2 7.1 %collective-permute-start.6 = (bf16[256,128]{0,1:T(8,128)(2,1)S(1)}, bf16[256,128]{0,1:T(8,128)(2,1)S(1)}, u32[]{:S(2)}, u32[]{:S(2)}) collective-permute-start(bf16[256,128]{0,1:T(8,128)(2,1)S(1)} %fusion.30), channel_id=1, source_target_pairs={{0,10},{1,11},{2,0},{3,1},{4,2},{5,3},{6,4},{7,5},{8,6},{9,7},{10,... | collective-permute-start | bytes 196616 | tf_op jit(solution)/shard_map/ppermute | solution.py:25
  96.0 9.9 %copy-start.1 = (s32[24,8]{0,1:T(8,128)S(1)}, s32[24,8]{0,1:T(8,128)}, u32[]{:S(2)}) copy-start(s32[24,8]{0,1:T(8,128)} %param.7) | copy-start | bytes 2308
  96.0 10.6 %copy-start.2 = (f32[24,8]{0,1:T(8,128)S(1)}, f32[24,8]{0,1:T(8,128)}, u32[]{:S(2)}) copy-start(f32[24,8]{0,1:T(8,128)} %param.8) | copy-start | bytes 2308
  96.0 31.1 %all-to-all-start.1 = ((bf16[32,8,1792]{2,1,0:T(8,128)(2,1)}), bf16[32,8,1792]{2,1,0:T(8,128)(2,1)S(1)}, u32[]{:S(2)}, u32[]{:S(2)}) async-start(bf16[32,8,1792]{2,1,0:T(8,128)(2,1)} %fusion), calls=%async_computation.1 | async-start | bytes 1835008 | tf_op jit(solution)/shard_map/all_to_all | solution.py:33

commit v10 on v8

--- a/solution.py
+++ b/solution.py
@@ -115,15 +115,81 @@
     return cut(cut_gate_up, piece_start(index, width), arrays, shape, pl.ANY, scratch)
 
 
-def down_piece(down_weight, index, half=None):
+def down_piece(down_weight, index):
     units, width = down_weight.shape[1:]
     size = width // BACK
+    scratch = [pltpu.SemaphoreType.DMA((1,))]
     start = lax.rem(index, BACK) * size
-    if half is not None:
-        size //= 2
-        start = start + half * size
-    scratch = [pltpu.SemaphoreType.DMA((1,))]
     return cut(cut_down, start, (down_weight,), (units, size), pltpu.VMEM, scratch)
+
+
+def cut_own_kernel(
+    gu_start, dn_start, two_start, gate_ref, up_ref, down_ref, gu_ref, dn_ref, two_ref,
+    gu, dn, two, in_sem, out_sem, down_sem,
+):
+    piece, units = gu.shape[0], gate_ref.shape[2]
+    rows = piece // STRIPS
+    arriving, leaving = [], []
+    for i, (start, held, out) in enumerate(((two_start, two, two_ref), (dn_start, dn, dn_ref))):
+        columns = pl.ds(pl.multiple_of(start[0], LANES), held.shape[1])
+        arriving.append(
+            [pltpu.make_async_copy(down_ref.at[0, :, columns], held, down_sem.at[0, i])]
+        )
+        leaving.append(pltpu.make_async_copy(held, out, down_sem.at[1, i]))
+    for strip in range(STRIPS):
+        source = pl.ds(pl.multiple_of(gu_start[0] + strip * rows, 16), rows)
+        target = pl.ds(strip * rows, rows)
+        arriving.append(
+            [
+                pltpu.make_async_copy(
+                    ref.at[0, source, :],
+                    gu.at[target, pl.ds(i * units, units)],
+                    in_sem.at[strip, i],
+                )
+                for i, ref in enumerate((gate_ref, up_ref))
+            ]
+        )
+        leaving.append(
+            pltpu.make_async_copy(gu.at[target, :], gu_ref.at[target, :], out_sem.at[strip])
+        )
+    for group in arriving:
+        for copy in group:
+            copy.start()
+    for group, out in zip(arriving, leaving):
+        for copy in group:
+            copy.wait()
+        out.start()
+    for out in leaving:
+        out.wait()
+
+
+def cut_own(gate_weight, up_weight, down_weight, here, target_two, core):
+    width, units = gate_weight.shape[1:]
+    size = width // BACK
+    shapes = ((piece_width(width), 2 * units), (units, size), (units, size // 2))
+    starts = (
+        piece_start(here, width),
+        lax.rem(here, BACK) * size,
+        lax.rem(target_two, BACK) * size + core * (size // 2),
+    )
+    total = sum(a * b for a, b in shapes)
+    return pl.pallas_call(
+        cut_own_kernel,
+        out_shape=tuple(jax.ShapeDtypeStruct(shape, jnp.bfloat16) for shape in shapes),
+        in_specs=[pl.BlockSpec(memory_space=pltpu.SMEM)] * 3
+        + [pl.BlockSpec(memory_space=pl.ANY)] * 3,
+        out_specs=(pl.BlockSpec(memory_space=pl.ANY),) * 3,
+        scratch_shapes=[pltpu.VMEM(shape, jnp.bfloat16) for shape in shapes]
+        + [
+            pltpu.SemaphoreType.DMA((STRIPS, 2)),
+            pltpu.SemaphoreType.DMA((STRIPS,)),
+            pltpu.SemaphoreType.DMA((2, 2)),
+        ],
+        cost_estimate=pl.CostEstimate(
+            flops=500 * total, bytes_accessed=4 * total, transcendentals=0
+        ),
+        name="cut_own",
+    )(*(start.reshape(1) for start in starts), gate_weight, up_weight, down_weight)
 
 
 def dispatch_kernel(start_ref, ids_ref, tokens_ref, rows_ref, ids, held, chosen, sem):
@@ -193,19 +259,19 @@
 
 
 def weigh_kernel(ids_ref, route_ref, weights_ref):
-    count, capacity = weights_ref.shape[1:]
-    lane = lax.broadcasted_iota(jnp.int32, (count, capacity), 1)
-    expert, slot = lane // MOST, lane % MOST
-    member = jnp.zeros((count, capacity), jnp.float32)
-    weight = jnp.zeros((count, capacity), jnp.float32)
+    capacity, count = weights_ref.shape[1:]
+    line = lax.broadcasted_iota(jnp.int32, (capacity, count), 0)
+    expert, slot = line // MOST, line % MOST
+    member = jnp.zeros((capacity, count), jnp.float32)
+    weight = jnp.zeros((capacity, count), jnp.float32)
     for k in range(TOP):
-        same = ids_ref[:, k : k + 1] == expert
+        same = ids_ref[k : k + 1, :] == expert
         member = jnp.where(same, 1.0, member)
-        weight = jnp.where(same, route_ref[:, k : k + 1], weight)
+        weight = jnp.where(same, route_ref[k : k + 1, :], weight)
     row = lax.broadcasted_iota(jnp.int32, (count, count), 0)
     column = lax.broadcasted_iota(jnp.int32, (count, count), 1)
-    above = jnp.where(column < row, 1.0, 0.0).astype(jnp.bfloat16)
-    earlier = jnp.dot(above, member.astype(jnp.bfloat16), preferred_element_type=jnp.float32)
+    before = jnp.where(row < column, 1.0, 0.0).astype(jnp.bfloat16)
+    earlier = jnp.dot(member.astype(jnp.bfloat16), before, preferred_element_type=jnp.float32)
     weight = jnp.where(earlier == slot.astype(jnp.float32), weight, 0.0)
     high = weight.astype(jnp.bfloat16)
     weights_ref[0] = high
@@ -213,7 +279,7 @@
 
 
 def weigh(expert_ids, route_weight):
-    shape = (2, expert_ids.shape[0], EXPERTS * MOST)
+    shape = (2, EXPERTS * MOST, expert_ids.shape[0])
     return pl.pallas_call(
         weigh_kernel,
         out_shape=jax.ShapeDtypeStruct(shape, jnp.bfloat16),
@@ -221,14 +287,12 @@
             flops=2**26, bytes_accessed=2**15, transcendentals=0
         ),
         name="weigh",
-    )(expert_ids, route_weight)
+    )(expert_ids.T, route_weight.T)
 
 
 def combine(weights, returned):
-    parts, rows, capacity = weights.shape
-    both = weights.reshape(parts * rows, capacity)
-    sums = jnp.dot(both, returned, preferred_element_type=jnp.float32)
-    return sums[:rows] + sums[rows:]
+    sums = jnp.einsum("ipt,pd->itd", weights, returned, preferred_element_type=jnp.float32)
+    return sums[0] + sums[1]
 
 
 def per_device(tokens, expert_ids, route_weight, gate_weight, up_weight, down_weight):
@@ -255,13 +319,14 @@
     gate_up_far = swap(gate_up_near)
     down_near = shift(down_piece(down_weight, target), 1)
     down_far = swap(down_near)
-    mine = hop_two(down_piece(down_weight, target_two, core))
+    gate_up_here, down_here, half = cut_own(
+        gate_weight, up_weight, down_weight, here, target_two, core
+    )
+    mine = hop_two(half)
     other = swap(mine)
     down_two = jnp.concatenate(
         [jnp.where(core == 0, mine, other), jnp.where(core == 0, other, mine)], 1
     )
-    gate_up_here = gate_up_piece(gate_weight, up_weight, here)
-    down_here = down_piece(down_weight, here)
     weights = weigh(expert_ids, route_weight)
 
     def product(weights):

time: 152 us -> 153 us (level)
  the two profiles are of different devices: /device:TPU:4 before, /device:TPU:16 now
where the time goes in v10:
time: 153 us; the launch traced here: 152 us
  waiting for transfers between devices  58.7 us (38%)
  starting transfers between devices  54.7 us (36%)
  blocking collectives  18.5 us (12%)
  Pallas kernels  11.7 us (8%)
  matrix products  6.98 us (5%)
    ppermute x6, waiting for transfers between devices, shift(): return lax.ppermute(array, ('dp', 'tp'), pairs)  30.3 us
    all_to_all x2, starting transfers between devices, exchange(): return lax.all_to_all(array, axis, split_axis=0, concat_axis=0, tiled=True)  22.8 us
    all_to_all x2, waiting for transfers between devices, exchange(): return lax.all_to_all(array, axis, split_axis=0, concat_axis=0, tiled=True)  19.1 us
    all_to_all x1, blocking collectives, exchange(): return lax.all_to_all(array, axis, split_axis=0, concat_axis=0, tiled=True)  18.5 us
    ppermute x6, starting transfers between devices, shift(): return lax.ppermute(array, ('dp', 'tp'), pairs)  17.3 us
    ppermute x2, waiting for transfers between devices, hop_two(): lax.ppermute(array, 'tp', [(i, (i + (2 if i % 2 else size - 2)) % size) f...  9.36 us
    ppermute x2, starting transfers between devices, hop_two(): lax.ppermute(array, 'tp', [(i, (i + (2 if i % 2 else size - 2)) % size) f...  7.81 us
    ppermute x3, starting transfers between devices, swap(): return lax.ppermute(array, 'dp', [(0, 1), (1, 0)])  6.8 us
  transfers between devices with their start and end apart: 13, of which 5 were waited for; matrix products, arithmetic and copies ran while one was open for 2% of the time, Pallas kernels for 6%

profile of v10, /device:TPU:16, one launch (start us, length us, event | category | flops | bytes accessed | tf_op | source)
XLA Modules:
  0.0 151.9 jit_solution(10635558010434681992)
XLA Ops:
  0.0 3.2 %dispatch.1 = bf16[256,2432]{1,0:T(8,128)(2,1)} custom-call(s32[1]{0:T(128)} %bitcast.start_ref.gu_start, s32[8,24]{1,0:T(8,128)} %bitcast.40, bf16[24,7168]{1,0:T(8,128)(2,1)} %tokens_ref.1), custom_call_target="tpu_custom_call" | custom-call | flops 29884416 | bytes 2097152 | tf_op jit(solution)/shard_map/dispatch/pallas_call | solution.py:238
  3.3 13.0 %all-to-all-start = ((bf16[32,8,2432]{2,1,0:T(8,128)(2,1)}), bf16[32,8,2432]{2,1,0:T(8,128)(2,1)S(1)}, u32[]{:S(2)}, u32[]{:S(2)}) async-start(bf16[32,8,2432]{2,1,0:T(8,128)(2,1)} %bitcast.39), calls=%async_computation | async-start | bytes 2490368 | tf_op jit(solution)/shard_map/all_to_all | solution.py:33
  16.3 2.2 %shard_map.64 = bf16[2432,256]{1,0:T(8,128)(2,1)} custom-call(s32[1]{0:T(128)} %bitcast.8.start_ref, bf16[1,7168,128]{2,1,0:T(8,128)(2,1)} %gate_ref.1, bf16[1,7168,128]{2,1,0:T(8,128)(2,1)} %up_ref.1), custom_call_target="tpu_custom_call" | custom-call | flops 311296000 | bytes 2490368 | tf_op jit(solution)/shard_map/pallas_call | solution.py:93
  18.5 1.9 %collective-permute-start = (bf16[2432,256]{1,0:T(8,128)(2,1)}, bf16[2432,256]{1,0:T(8,128)(2,1)S(1)}, u32[]{:S(2)}, u32[]{:S(2)}) collective-permute-start(bf16[2432,256]{1,0:T(8,128)(2,1)} %shard_map.64), channel_id=1, source_target_pairs={{0,1},{1,2},{2,3},{3,4},{4,5},{5,6},{6,7},{7,8},{8,9},{9,10},{10,1... | collective-permute-start | bytes 3735560 | tf_op jit(solution)/shard_map/ppermute | solution.py:25
  20.4 24.8 %collective-permute-done = bf16[2432,256]{1,0:T(8,128)(2,1)S(1)} collective-permute-done((bf16[2432,256]{1,0:T(8,128)(2,1)}, bf16[2432,256]{1,0:T(8,128)(2,1)S(1)}, u32[]{:S(2)}, u32[]{:S(2)}) %collective-permute-start) | collective-permute-done | bytes 1245216 | tf_op jit(solution)/shard_map/ppermute | solution.py:25
  45.3 1.9 %collective-permute-start.2 = (bf16[2432,256]{1,0:T(8,128)(2,1)S(1)}, bf16[2432,256]{1,0:T(8,128)(2,1)}, u32[]{:S(2)}, u32[]{:S(2)}) collective-permute-start(bf16[2432,256]{1,0:T(8,128)(2,1)S(1)} %collective-permute-done), channel_id=1, source_target_pairs={{0,12},{12,0},{1,13},{13,1},{2,14},{14,2},{3,15},{15,3},{4,16},{16... | collective-permute-start | bytes 3735560 | tf_op jit(solution)/shard_map/ppermute | solution.py:29
  47.2 1.8 %shard_map.65 = bf16[128,1792]{1,0:T(8,128)(2,1)} custom-call(s32[1]{0:T(128)} %bitcast.9.start_ref, bf16[1,128,7168]{2,1,0:T(8,128)(2,1)} %down_ref.1), custom_call_target="tpu_custom_call" | custom-call | flops 114688000 | bytes 917504 | tf_op jit(solution)/shard_map/pallas_call | solution.py:93
  49.0 1.9 %collective-permute-start.7 = (bf16[128,1792]{1,0:T(8,128)(2,1)}, bf16[128,1792]{1,0:T(8,128)(2,1)S(1)}, u32[]{:S(2)}, u32[]{:S(2)}) collective-permute-start(bf16[128,1792]{1,0:T(8,128)(2,1)} %shard_map.65), channel_id=1, source_target_pairs={{0,1},{1,2},{2,3},{3,4},{4,5},{5,6},{6,7},{7,8},{8,9},{9,10},{10,1... | collective-permute-start | bytes 1376264 | tf_op jit(solution)/shard_map/ppermute | solution.py:25
  51.0 2.9 %cut_own.1 = (bf16[2432,256]{1,0:T(8,128)(2,1)}, bf16[128,1792]{1,0:T(8,128)(2,1)}, bf16[128,896]{1,0:T(8,128)(2,1)}) custom-call(s32[1]{0:T(128)} %bitcast.start_ref.gu_start, s32[1]{0:T(128)} %bitcast.6.dn_start, s32[1]{0:T(128)} %bitcast.7.two_start, bf16[1,7168,128]{2,1,0:T(8,128)(2,1)} %gate_ref.1, bf16[1,7168,128]{2,1,0:T(8,128)(2,1)} %up_ref.1, ...), custom_call_target="tpu_custom_call" | custom-call | flops 483328000 | bytes 3866624 | tf_op jit(solution)/shard_map/cut_own/pallas_call | solution.py:176
  53.8 5.4 %collective-permute-start.9 = (bf16[128,896]{1,0:T(8,128)(2,1)}, bf16[128,896]{1,0:T(8,128)(2,1)S(1)}, u32[]{:S(2)}, u32[]{:S(2)}) collective-permute-start(bf16[128,896]{1,0:T(8,128)(2,1)} %get-tuple-element.22), channel_id=1, source_target_pairs={{0,10},{1,3},{2,0},{3,5},{4,2},{5,7},{6,4},{7,9},{8,6},{9,11},{10,... | collective-permute-start | bytes 688136 | tf_op jit(solution)/shard_map/ppermute | solution.py:38
  59.2 4.9 %collective-permute-done.9 = bf16[128,896]{1,0:T(8,128)(2,1)S(1)} collective-permute-done((bf16[128,896]{1,0:T(8,128)(2,1)}, bf16[128,896]{1,0:T(8,128)(2,1)S(1)}, u32[]{:S(2)}, u32[]{:S(2)}) %collective-permute-start.9) | collective-permute-done | bytes 229408 | tf_op jit(solution)/shard_map/ppermute | solution.py:38
  64.1 3.0 %collective-permute-start.10 = (bf16[128,896]{1,0:T(8,128)(2,1)S(1)}, bf16[128,896]{1,0:T(8,128)(2,1)S(1)}, u32[]{:S(2)}, u32[]{:S(2)}) collective-permute-start(bf16[128,896]{1,0:T(8,128)(2,1)S(1)} %collective-permute-done.9), channel_id=1, source_target_pairs={{0,12},{12,0},{1,13},{13,1},{2,14},{14,2},{3,15},{15,3},{4,16},{16... | collective-permute-start | bytes 688136 | tf_op jit(solution)/shard_map/ppermute | solution.py:29
  67.0 0.0 collective-permute-done.7
  67.0 1.9 %collective-permute-start.8 = (bf16[128,1792]{1,0:T(8,128)(2,1)S(1)}, bf16[128,1792]{1,0:T(8,128)(2,1)}, u32[]{:S(2)}, u32[]{:S(2)}) collective-permute-start(bf16[128,1792]{1,0:T(8,128)(2,1)S(1)} %collective-permute-done.7), channel_id=1, source_target_pairs={{0,12},{12,0},{1,13},{13,1},{2,14},{14,2},{3,15},{15,3},{4,16},{16... | collective-permute-start | bytes 1376264 | tf_op jit(solution)/shard_map/ppermute | solution.py:29
  69.0 0.0 all-to-all-done
  69.0 0.6 fusion.16
  69.6 0.0 copy-start
  69.6 4.5 %collective-permute-start.1 = (bf16[256,256]{0,1:T(8,128)(2,1)S(1)}, bf16[256,256]{0,1:T(8,128)(2,1)S(1)}, u32[]{:S(2)}, u32[]{:S(2)}) collective-permute-start(bf16[256,256]{0,1:T(8,128)(2,1)S(1)} %fusion.16), channel_id=1, source_target_pairs={{0,11},{1,0},{2,1},{3,2},{4,3},{5,4},{6,5},{7,6},{8,7},{9,8},{10,9... | collective-permute-start | bytes 393224 | tf_op jit(solution)/shard_map/ppermute | solution.py:25
  74.2 0.0 collective-permute-done.2
  74.2 1.9 %fusion.19 = bf16[256,256]{0,1:T(8,128)(2,1)S(1)} fusion(bf16[2432,256]{1,0:T(8,128)(2,1)} %collective-permute-done.2, bf16[32,8,2432]{2,1,0:T(8,128)(2,1)S(1)} %all-to-all-done), kind=kOutput, calls=%fused_computation.18 | convolution fusion | flops 318832640 | bytes 2621440 | tf_op jit(solution)/shard_map/dot_general | solution.py:333
  76.1 1.9 %collective-permute-start.3 = (bf16[256,256]{0,1:T(8,128)(2,1)S(1)}, bf16[256,256]{0,1:T(8,128)(2,1)S(1)}, u32[]{:S(2)}, u32[]{:S(2)}) collective-permute-start(bf16[256,256]{0,1:T(8,128)(2,1)S(1)} %fusion.19), channel_id=1, source_target_pairs={{0,1},{1,2},{2,3},{3,4},{4,5},{5,6},{6,7},{7,8},{8,9},{9,10},{10,1... | collective-permute-start | bytes 393224 | tf_op jit(solution)/shard_map/ppermute | solution.py:25
  78.0 0.0 copy-done
  78.0 0.6 fusion.14
  78.7 0.0 copy-start.1
  78.7 0.0 collective-permute-done.1
  78.7 5.5 %collective-permute-done.3 = bf16[256,256]{0,1:T(8,128)(2,1)S(1)} collective-permute-done((bf16[256,256]{0,1:T(8,128)(2,1)S(1)}, bf16[256,256]{0,1:T(8,128)(2,1)S(1)}, u32[]{:S(2)}, u32[]{:S(2)}) %collective-permute-start.3) | collective-permute-done | bytes 131104 | tf_op jit(solution)/shard_map/ppermute | solution.py:25
  84.2 0.1 convert_add_fusion
  84.3 1.9 %collective-permute-start.4 = (bf16[256,128]{0,1:T(8,128)(2,1)S(1)}, bf16[256,128]{0,1:T(8,128)(2,1)S(1)}, u32[]{:S(2)}, u32[]{:S(2)}) collective-permute-start(bf16[256,128]{0,1:T(8,128)(2,1)S(1)} %fusion.32), channel_id=1, source_target_pairs={{0,1},{1,2},{2,3},{3,4},{4,5},{5,6},{6,7},{7,8},{8,9},{9,10},{10,1... | collective-permute-start | bytes 196616 | tf_op jit(solution)/shard_map/ppermute | solution.py:25
  86.2 5.1 %collective-permute-start.5 = (bf16[256,128]{0,1:T(8,128)(2,1)S(1)}, bf16[256,128]{0,1:T(8,128)(2,1)S(1)}, u32[]{:S(2)}, u32[]{:S(2)}) collective-permute-start(bf16[256,128]{0,1:T(8,128)(2,1)S(1)} %fusion.32), channel_id=1, source_target_pairs={{0,11},{1,0},{2,1},{3,2},{4,3},{5,4},{6,5},{7,6},{8,7},{9,8},{10,9... | collective-permute-start | bytes 196616 | tf_op jit(solution)/shard_map/ppermute | solution.py:25
  91.3 2.4 %collective-permute-start.6 = (bf16[256,128]{0,1:T(8,128)(2,1)S(1)}, bf16[256,128]{0,1:T(8,128)(2,1)S(1)}, u32[]{:S(2)}, u32[]{:S(2)}) collective-permute-start(bf16[256,128]{0,1:T(8,128)(2,1)S(1)} %fusion.32), channel_id=1, source_target_pairs={{0,10},{1,3},{2,0},{3,5},{4,2},{5,7},{6,4},{7,9},{8,6},{9,11},{10,... | collective-permute-start | bytes 196616 | tf_op jit(solution)/shard_map/ppermute | solution.py:38
  93.8 0.0 collective-permute-done.10
  93.8 0.1 broadcast_select_fusion.1
  93.9 0.0 collective-permute-done.8
  93.9 0.0 collective-permute-done.4
  93.9 0.0 collective-permute-done.5
  93.9 4.5 %collective-permute-done.6 = bf16[256,128]{0,1:T(8,128)(2,1)S(1)} collective-permute-done((bf16[256,128]{0,1:T(8,128)(2,1)S(1)}, bf16[256,128]{0,1:T(8,128)(2,1)S(1)}, u32[]{:S(2)}, u32[]{:S(2)}) %collective-permute-start.6) | collective-permute-done | bytes 65568 | tf_op jit(solution)/shard_map/ppermute | solution.py:38
  98.4 0.0 copy-done.1
  98.4 2.6 %fusion = bf16[32,8,1792]{2,1,0:T(8,128)(2,1)} fusion(bf16[128,896]{1,0:T(8,128)(2,1)S(1)} %get-tuple-element.24, bf16[128,896]{1,0:T(8,128)(2,1)S(1)} %get-tuple-element.23, bf16[128,1792]{1,0:T(8,128)(2,1)} %collective-permute-done.8, bf16[128,1792]{1,0:T(8,128)(2,1)S(1)} %copy-done.1, bf16[128,1792]{1,0:T(8,128)(2,1)S(1)} %collective-permute-done.7, ...), kind=kOutput, calls=%fused_computation.1 | convolution fusion | flops 480444416 | bytes 3014656 | tf_op jit(solution)/shard_map/dot_general | solution.py:343
  101.0 9.8 %all-to-all-start.1 = ((bf16[32,8,1792]{2,1,0:T(8,128)(2,1)}), bf16[32,8,1792]{2,1,0:T(8,128)(2,1)S(1)}, u32[]{:S(2)}, u32[]{:S(2)}) async-start(bf16[32,8,1792]{2,1,0:T(8,128)(2,1)} %fusion), calls=%async_computation.1 | async-start | bytes 1835008 | tf_op jit(solution)/shard_map/all_to_all | solution.py:33
  110.8 1.6 %weigh.1 = bf16[2,256,24]{2,1,0:T(8,128)(2,1)} custom-call(s32[8,24]{1,0:T(8,128)} %bitcast.41, f32[8,24]{1,0:T(8,128)} %bitcast.42), custom_call_target="tpu_custom_call" | custom-call | flops 67108864 | bytes 32768 | tf_op jit(solution)/shard_map/weigh/pallas_call | solution.py:283
  112.4 19.1 %all-to-all-done.1 = bf16[32,8,1792]{2,1,0:T(8,128)(2,1)S(1)} async-done(((bf16[32,8,1792]{2,1,0:T(8,128)(2,1)}), bf16[32,8,1792]{2,1,0:T(8,128)(2,1)S(1)}, u32[]{:S(2)}, u32[]{:S(2)}) %all-to-all-start.1) | async-done | bytes 917536 | tf_op jit(solution)/shard_map/all_to_all | solution.py:33
  131.4 1.2 fusion.22
  132.7 18.5 %all_to_all.15 = bf16[12,2,1792]{2,1,0:T(2,128)(2,1)S(1)} all-to-all(bf16[12,2,1792]{2,1,0:T(2,128)(2,1)S(1)} %convert_element_type.42), channel_id=1, replica_groups=mesh['ep'=32,'dp'=2,'tp'=12] {'tp'}, dimensions={0} | all-to-all | bytes 172032 | tf_op jit(solution)/shard_map/all_to_all | solution.py:33
  151.3 0.6 pad_maximum_fusion
  (5 shorter events, 0.2 us)
Async XLA Ops:
  3.3 65.7 %all-to-all-start = ((bf16[32,8,2432]{2,1,0:T(8,128)(2,1)}), bf16[32,8,2432]{2,1,0:T(8,128)(2,1)S(1)}, u32[]{:S(2)}, u32[]{:S(2)}) async-start(bf16[32,8,2432]{2,1,0:T(8,128)(2,1)} %bitcast.39), calls=%async_computation | async-start | bytes 2490368 | tf_op jit(solution)/shard_map/all_to_all | solution.py:33
  18.5 26.8 %collective-permute-start = (bf16[2432,256]{1,0:T(8,128)(2,1)}, bf16[2432,256]{1,0:T(8,128)(2,1)S(1)}, u32[]{:S(2)}, u32[]{:S(2)}) collective-permute-start(bf16[2432,256]{1,0:T(8,128)(2,1)} %shard_map.64), channel_id=1, source_target_pairs={{0,1},{1,2},{2,3},{3,4},{4,5},{5,6},{6,7},{7,8},{8,9},{9,10},{10,1... | collective-permute-start | bytes 3735560 | tf_op jit(solution)/shard_map/ppermute | solution.py:25
  45.3 28.9 %collective-permute-start.2 = (bf16[2432,256]{1,0:T(8,128)(2,1)S(1)}, bf16[2432,256]{1,0:T(8,128)(2,1)}, u32[]{:S(2)}, u32[]{:S(2)}) collective-permute-start(bf16[2432,256]{1,0:T(8,128)(2,1)S(1)} %collective-permute-done), channel_id=1, source_target_pairs={{0,12},{12,0},{1,13},{13,1},{2,14},{14,2},{3,15},{15,3},{4,16},{16... | collective-permute-start | bytes 3735560 | tf_op jit(solution)/shard_map/ppermute | solution.py:29
  49.0 18.1 %collective-permute-start.7 = (bf16[128,1792]{1,0:T(8,128)(2,1)}, bf16[128,1792]{1,0:T(8,128)(2,1)S(1)}, u32[]{:S(2)}, u32[]{:S(2)}) collective-permute-start(bf16[128,1792]{1,0:T(8,128)(2,1)} %shard_map.65), channel_id=1, source_target_pairs={{0,1},{1,2},{2,3},{3,4},{4,5},{5,6},{6,7},{7,8},{8,9},{9,10},{10,1... | collective-permute-start | bytes 1376264 | tf_op jit(solution)/shard_map/ppermute | solution.py:25
  53.8 10.2 %collective-permute-start.9 = (bf16[128,896]{1,0:T(8,128)(2,1)}, bf16[128,896]{1,0:T(8,128)(2,1)S(1)}, u32[]{:S(2)}, u32[]{:S(2)}) collective-permute-start(bf16[128,896]{1,0:T(8,128)(2,1)} %get-tuple-element.22), channel_id=1, source_target_pairs={{0,10},{1,3},{2,0},{3,5},{4,2},{5,7},{6,4},{7,9},{8,6},{9,11},{10,... | collective-permute-start | bytes 688136 | tf_op jit(solution)/shard_map/ppermute | solution.py:38
  64.1 29.7 %collective-permute-start.10 = (bf16[128,896]{1,0:T(8,128)(2,1)S(1)}, bf16[128,896]{1,0:T(8,128)(2,1)S(1)}, u32[]{:S(2)}, u32[]{:S(2)}) collective-permute-start(bf16[128,896]{1,0:T(8,128)(2,1)S(1)} %collective-permute-done.9), channel_id=1, source_target_pairs={{0,12},{12,0},{1,13},{13,1},{2,14},{14,2},{3,15},{15,3},{4,16},{16... | collective-permute-start | bytes 688136 | tf_op jit(solution)/shard_map/ppermute | solution.py:29
  67.0 26.8 %collective-permute-start.8 = (bf16[128,1792]{1,0:T(8,128)(2,1)S(1)}, bf16[128,1792]{1,0:T(8,128)(2,1)}, u32[]{:S(2)}, u32[]{:S(2)}) collective-permute-start(bf16[128,1792]{1,0:T(8,128)(2,1)S(1)} %collective-permute-done.7), channel_id=1, source_target_pairs={{0,12},{12,0},{1,13},{13,1},{2,14},{14,2},{3,15},{15,3},{4,16},{16... | collective-permute-start | bytes 1376264 | tf_op jit(solution)/shard_map/ppermute | solution.py:29
  69.6 8.4 %copy-start = (bf16[2432,256]{1,0:T(8,128)(2,1)S(1)}, bf16[2432,256]{1,0:T(8,128)(2,1)}, u32[]{:S(2)}) copy-start(bf16[2432,256]{1,0:T(8,128)(2,1)} %get-tuple-element.20) | copy-start | bytes 3735556
  69.6 9.1 %collective-permute-start.1 = (bf16[256,256]{0,1:T(8,128)(2,1)S(1)}, bf16[256,256]{0,1:T(8,128)(2,1)S(1)}, u32[]{:S(2)}, u32[]{:S(2)}) collective-permute-start(bf16[256,256]{0,1:T(8,128)(2,1)S(1)} %fusion.16), channel_id=1, source_target_pairs={{0,11},{1,0},{2,1},{3,2},{4,3},{5,4},{6,5},{7,6},{8,7},{9,8},{10,9... | collective-permute-start | bytes 393224 | tf_op jit(solution)/shard_map/ppermute | solution.py:25
  76.1 8.1 %collective-permute-start.3 = (bf16[256,256]{0,1:T(8,128)(2,1)S(1)}, bf16[256,256]{0,1:T(8,128)(2,1)S(1)}, u32[]{:S(2)}, u32[]{:S(2)}) collective-permute-start(bf16[256,256]{0,1:T(8,128)(2,1)S(1)} %fusion.19), channel_id=1, source_target_pairs={{0,1},{1,2},{2,3},{3,4},{4,5},{5,6},{6,7},{7,8},{8,9},{9,10},{10,1... | collective-permute-start | bytes 393224 | tf_op jit(solution)/shard_map/ppermute | solution.py:25
  78.7 19.7 %copy-start.1 = (bf16[128,1792]{1,0:T(8,128)(2,1)S(1)}, bf16[128,1792]{1,0:T(8,128)(2,1)}, u32[]{:S(2)}) copy-start(bf16[128,1792]{1,0:T(8,128)(2,1)} %get-tuple-element.21) | copy-start | bytes 1376260
  84.3 9.6 %collective-permute-start.4 = (bf16[256,128]{0,1:T(8,128)(2,1)S(1)}, bf16[256,128]{0,1:T(8,128)(2,1)S(1)}, u32[]{:S(2)}, u32[]{:S(2)}) collective-permute-start(bf16[256,128]{0,1:T(8,128)(2,1)S(1)} %fusion.32), channel_id=1, source_target_pairs={{0,1},{1,2},{2,3},{3,4},{4,5},{5,6},{6,7},{7,8},{8,9},{9,10},{10,1... | collective-permute-start | bytes 196616 | tf_op jit(solution)/shard_map/ppermute | solution.py:25
  86.2 7.7 %collective-permute-start.5 = (bf16[256,128]{0,1:T(8,128)(2,1)S(1)}, bf16[256,128]{0,1:T(8,128)(2,1)S(1)}, u32[]{:S(2)}, u32[]{:S(2)}) collective-permute-start(bf16[256,128]{0,1:T(8,128)(2,1)S(1)} %fusion.32), channel_id=1, source_target_pairs={{0,11},{1,0},{2,1},{3,2},{4,3},{5,4},{6,5},{7,6},{8,7},{9,8},{10,9... | collective-permute-start | bytes 196616 | tf_op jit(solution)/shard_map/ppermute | solution.py:25
  91.3 7.1 %collective-permute-start.6 = (bf16[256,128]{0,1:T(8,128)(2,1)S(1)}, bf16[256,128]{0,1:T(8,128)(2,1)S(1)}, u32[]{:S(2)}, u32[]{:S(2)}) collective-permute-start(bf16[256,128]{0,1:T(8,128)(2,1)S(1)} %fusion.32), channel_id=1, source_target_pairs={{0,10},{1,3},{2,0},{3,5},{4,2},{5,7},{6,4},{7,9},{8,6},{9,11},{10,... | collective-permute-start | bytes 196616 | tf_op jit(solution)/shard_map/ppermute | solution.py:38
  101.0 30.4 %all-to-all-start.1 = ((bf16[32,8,1792]{2,1,0:T(8,128)(2,1)}), bf16[32,8,1792]{2,1,0:T(8,128)(2,1)S(1)}, u32[]{:S(2)}, u32[]{:S(2)}) async-start(bf16[32,8,1792]{2,1,0:T(8,128)(2,1)} %fusion), calls=%async_computation.1 | async-start | bytes 1835008 | tf_op jit(solution)/shard_map/all_to_all | solution.py:33

commit v11 on v8

--- a/solution.py
+++ b/solution.py
@@ -193,19 +193,19 @@
 
 
 def weigh_kernel(ids_ref, route_ref, weights_ref):
-    count, capacity = weights_ref.shape[1:]
-    lane = lax.broadcasted_iota(jnp.int32, (count, capacity), 1)
-    expert, slot = lane // MOST, lane % MOST
-    member = jnp.zeros((count, capacity), jnp.float32)
-    weight = jnp.zeros((count, capacity), jnp.float32)
+    capacity, count = weights_ref.shape[1:]
+    line = lax.broadcasted_iota(jnp.int32, (capacity, count), 0)
+    expert, slot = line // MOST, line % MOST
+    member = jnp.zeros((capacity, count), jnp.float32)
+    weight = jnp.zeros((capacity, count), jnp.float32)
     for k in range(TOP):
-        same = ids_ref[:, k : k + 1] == expert
+        same = ids_ref[k : k + 1, :] == expert
         member = jnp.where(same, 1.0, member)
-        weight = jnp.where(same, route_ref[:, k : k + 1], weight)
+        weight = jnp.where(same, route_ref[k : k + 1, :], weight)
     row = lax.broadcasted_iota(jnp.int32, (count, count), 0)
     column = lax.broadcasted_iota(jnp.int32, (count, count), 1)
-    above = jnp.where(column < row, 1.0, 0.0).astype(jnp.bfloat16)
-    earlier = jnp.dot(above, member.astype(jnp.bfloat16), preferred_element_type=jnp.float32)
+    before = jnp.where(row < column, 1.0, 0.0).astype(jnp.bfloat16)
+    earlier = jnp.dot(member.astype(jnp.bfloat16), before, preferred_element_type=jnp.float32)
     weight = jnp.where(earlier == slot.astype(jnp.float32), weight, 0.0)
     high = weight.astype(jnp.bfloat16)
     weights_ref[0] = high
@@ -213,7 +213,7 @@
 
 
 def weigh(expert_ids, route_weight):
-    shape = (2, expert_ids.shape[0], EXPERTS * MOST)
+    shape = (2, EXPERTS * MOST, expert_ids.shape[0])
     return pl.pallas_call(
         weigh_kernel,
         out_shape=jax.ShapeDtypeStruct(shape, jnp.bfloat16),
@@ -221,14 +221,12 @@
             flops=2**26, bytes_accessed=2**15, transcendentals=0
         ),
         name="weigh",
-    )(expert_ids, route_weight)
+    )(expert_ids.T, route_weight.T)
 
 
 def combine(weights, returned):
-    parts, rows, capacity = weights.shape
-    both = weights.reshape(parts * rows, capacity)
-    sums = jnp.dot(both, returned, preferred_element_type=jnp.float32)
-    return sums[:rows] + sums[rows:]
+    sums = jnp.einsum("ipt,pd->itd", weights, returned, preferred_element_type=jnp.float32)
+    return sums[0] + sums[1]
 
 
 def per_device(tokens, expert_ids, route_weight, gate_weight, up_weight, down_weight):

time: 152 us -> 152 us (level)
  transfers between devices with their start and end apart: 13 -> 13, of which waited for: 5 -> 5; matrix products, arithmetic and copies ran while one was open for 3% -> 2% of each run, Pallas kernels for 7% -> 7%
where the time goes in v11:
time: 152 us; the launch traced here: 151 us
  starting transfers between devices  55.3 us (36%)
  waiting for transfers between devices  55.1 us (36%)
  blocking collectives  17.6 us (12%)
  Pallas kernels  14.4 us (9%)
  matrix products  6.98 us (5%)
    ppermute x6, waiting for transfers between devices, shift(): return lax.ppermute(array, ('dp', 'tp'), pairs)  29.7 us
    all_to_all x2, starting transfers between devices, exchange(): return lax.all_to_all(array, axis, split_axis=0, concat_axis=0, tiled=True)  22.9 us
    all_to_all x2, waiting for transfers between devices, exchange(): return lax.all_to_all(array, axis, split_axis=0, concat_axis=0, tiled=True)  19.2 us
    ppermute x6, starting transfers between devices, shift(): return lax.ppermute(array, ('dp', 'tp'), pairs)  18.4 us
    all_to_all x1, blocking collectives, exchange(): return lax.all_to_all(array, axis, split_axis=0, concat_axis=0, tiled=True)  17.6 us
    pallas_call x5, Pallas kernels, cut(): pl.pallas_call(kernel, out_shape=jax.ShapeDtypeStruct(shape, jnp.bfloat16...  9.67 us
    ppermute x2, starting transfers between devices, hop_two(): lax.ppermute(array, 'tp', [(i, (i + (2 if i % 2 else size - 2)) % size) f...  7.82 us
    ppermute x3, starting transfers between devices, swap(): return lax.ppermute(array, 'dp', [(0, 1), (1, 0)])  6.23 us
  transfers between devices with their start and end apart: 13, of which 5 were waited for; matrix products, arithmetic and copies ran while one was open for 2% of the time, Pallas kernels for 7%

profile of v11, /device:TPU:4, one launch (start us, length us, event | category | flops | bytes accessed | tf_op | source)
XLA Modules:
  0.0 150.7 jit_solution(6168585615972154892)
XLA Ops:
  0.0 3.2 %dispatch.1 = bf16[256,2432]{1,0:T(8,128)(2,1)} custom-call(s32[1]{0:T(128)} %bitcast.start_ref, s32[8,24]{1,0:T(8,128)} %bitcast.40, bf16[24,7168]{1,0:T(8,128)(2,1)} %tokens_ref.1), custom_call_target="tpu_custom_call" | custom-call | flops 29884416 | bytes 2097152 | tf_op jit(solution)/shard_map/dispatch/pallas_call | solution.py:172
  3.2 13.1 %all-to-all-start = ((bf16[32,8,2432]{2,1,0:T(8,128)(2,1)}), bf16[32,8,2432]{2,1,0:T(8,128)(2,1)S(1)}, u32[]{:S(2)}, u32[]{:S(2)}) async-start(bf16[32,8,2432]{2,1,0:T(8,128)(2,1)} %bitcast.39), calls=%async_computation | async-start | bytes 2490368 | tf_op jit(solution)/shard_map/all_to_all | solution.py:33
  16.3 2.2 %shard_map.65 = bf16[2432,256]{1,0:T(8,128)(2,1)} custom-call(s32[1]{0:T(128)} %bitcast.6.start_ref, bf16[1,7168,128]{2,1,0:T(8,128)(2,1)} %gate_ref.1, bf16[1,7168,128]{2,1,0:T(8,128)(2,1)} %up_ref.1), custom_call_target="tpu_custom_call" | custom-call | flops 311296000 | bytes 2490368 | tf_op jit(solution)/shard_map/pallas_call | solution.py:93
  18.5 1.9 %collective-permute-start = (bf16[2432,256]{1,0:T(8,128)(2,1)}, bf16[2432,256]{1,0:T(8,128)(2,1)S(1)}, u32[]{:S(2)}, u32[]{:S(2)}) collective-permute-start(bf16[2432,256]{1,0:T(8,128)(2,1)} %shard_map.65), channel_id=1, source_target_pairs={{0,1},{1,2},{2,3},{3,4},{4,5},{5,6},{6,7},{7,8},{8,9},{9,10},{10,1... | collective-permute-start | bytes 3735560 | tf_op jit(solution)/shard_map/ppermute | solution.py:25
  20.5 24.9 %collective-permute-done = bf16[2432,256]{1,0:T(8,128)(2,1)S(1)} collective-permute-done((bf16[2432,256]{1,0:T(8,128)(2,1)}, bf16[2432,256]{1,0:T(8,128)(2,1)S(1)}, u32[]{:S(2)}, u32[]{:S(2)}) %collective-permute-start) | collective-permute-done | bytes 1245216 | tf_op jit(solution)/shard_map/ppermute | solution.py:25
  45.3 1.9 %collective-permute-start.2 = (bf16[2432,256]{1,0:T(8,128)(2,1)S(1)}, bf16[2432,256]{1,0:T(8,128)(2,1)}, u32[]{:S(2)}, u32[]{:S(2)}) collective-permute-start(bf16[2432,256]{1,0:T(8,128)(2,1)S(1)} %collective-permute-done), channel_id=1, source_target_pairs={{0,12},{12,0},{1,13},{13,1},{2,14},{14,2},{3,15},{15,3},{4,16},{16... | collective-permute-start | bytes 3735560 | tf_op jit(solution)/shard_map/ppermute | solution.py:29
  47.3 1.8 %shard_map.66 = bf16[128,1792]{1,0:T(8,128)(2,1)} custom-call(s32[1]{0:T(128)} %bitcast.7.start_ref, bf16[1,128,7168]{2,1,0:T(8,128)(2,1)} %down_ref.2), custom_call_target="tpu_custom_call" | custom-call | flops 114688000 | bytes 917504 | tf_op jit(solution)/shard_map/pallas_call | solution.py:93
  49.1 1.9 %collective-permute-start.7 = (bf16[128,1792]{1,0:T(8,128)(2,1)}, bf16[128,1792]{1,0:T(8,128)(2,1)S(1)}, u32[]{:S(2)}, u32[]{:S(2)}) collective-permute-start(bf16[128,1792]{1,0:T(8,128)(2,1)} %shard_map.66), channel_id=1, source_target_pairs={{0,1},{1,2},{2,3},{3,4},{4,5},{5,6},{6,7},{7,8},{8,9},{9,10},{10,1... | collective-permute-start | bytes 1376264 | tf_op jit(solution)/shard_map/ppermute | solution.py:25
  51.0 1.7 %shard_map.68 = bf16[128,896]{1,0:T(8,128)(2,1)} custom-call(s32[1]{0:T(128)} %bitcast.9.start_ref, bf16[1,128,7168]{2,1,0:T(8,128)(2,1)} %down_ref.2), custom_call_target="tpu_custom_call" | custom-call | flops 57344000 | bytes 458752 | tf_op jit(solution)/shard_map/pallas_call | solution.py:93
  52.7 5.4 %collective-permute-start.9 = (bf16[128,896]{1,0:T(8,128)(2,1)}, bf16[128,896]{1,0:T(8,128)(2,1)S(1)}, u32[]{:S(2)}, u32[]{:S(2)}) collective-permute-start(bf16[128,896]{1,0:T(8,128)(2,1)} %shard_map.68), channel_id=1, source_target_pairs={{0,10},{1,3},{2,0},{3,5},{4,2},{5,7},{6,4},{7,9},{8,6},{9,11},{10,... | collective-permute-start | bytes 688136 | tf_op jit(solution)/shard_map/ppermute | solution.py:38
  58.1 1.8 %shard_map.67 = bf16[128,1792]{1,0:T(8,128)(2,1)} custom-call(s32[1]{0:T(128)} %bitcast.8.start_ref, bf16[1,128,7168]{2,1,0:T(8,128)(2,1)} %down_ref.2), custom_call_target="tpu_custom_call" | custom-call | flops 114688000 | bytes 917504 | tf_op jit(solution)/shard_map/pallas_call | solution.py:93
  59.9 2.2 %shard_map.64 = bf16[2432,256]{1,0:T(8,128)(2,1)} custom-call(s32[1]{0:T(128)} %bitcast.start_ref, bf16[1,7168,128]{2,1,0:T(8,128)(2,1)} %gate_ref.1, bf16[1,7168,128]{2,1,0:T(8,128)(2,1)} %up_ref.1), custom_call_target="tpu_custom_call" | custom-call | flops 311296000 | bytes 2490368 | tf_op jit(solution)/shard_map/pallas_call | solution.py:93
  62.1 1.6 %collective-permute-done.9 = bf16[128,896]{1,0:T(8,128)(2,1)S(1)} collective-permute-done((bf16[128,896]{1,0:T(8,128)(2,1)}, bf16[128,896]{1,0:T(8,128)(2,1)S(1)}, u32[]{:S(2)}, u32[]{:S(2)}) %collective-permute-start.9) | collective-permute-done | bytes 229408 | tf_op jit(solution)/shard_map/ppermute | solution.py:38
  63.7 2.2 %collective-permute-start.10 = (bf16[128,896]{1,0:T(8,128)(2,1)S(1)}, bf16[128,896]{1,0:T(8,128)(2,1)S(1)}, u32[]{:S(2)}, u32[]{:S(2)}) collective-permute-start(bf16[128,896]{1,0:T(8,128)(2,1)S(1)} %collective-permute-done.9), channel_id=1, source_target_pairs={{0,12},{12,0},{1,13},{13,1},{2,14},{14,2},{3,15},{15,3},{4,16},{16... | collective-permute-start | bytes 688136 | tf_op jit(solution)/shard_map/ppermute | solution.py:29
  65.9 0.0 collective-permute-done.7
  65.9 2.2 %collective-permute-start.8 = (bf16[128,1792]{1,0:T(8,128)(2,1)S(1)}, bf16[128,1792]{1,0:T(8,128)(2,1)}, u32[]{:S(2)}, u32[]{:S(2)}) collective-permute-start(bf16[128,1792]{1,0:T(8,128)(2,1)S(1)} %collective-permute-done.7), channel_id=1, source_target_pairs={{0,12},{12,0},{1,13},{13,1},{2,14},{14,2},{3,15},{15,3},{4,16},{16... | collective-permute-start | bytes 1376264 | tf_op jit(solution)/shard_map/ppermute | solution.py:29
  68.1 0.0 all-to-all-done
  68.1 0.6 fusion.16
  68.7 0.0 copy-start
  68.7 4.9 %collective-permute-start.1 = (bf16[256,256]{0,1:T(8,128)(2,1)S(1)}, bf16[256,256]{0,1:T(8,128)(2,1)S(1)}, u32[]{:S(2)}, u32[]{:S(2)}) collective-permute-start(bf16[256,256]{0,1:T(8,128)(2,1)S(1)} %fusion.16), channel_id=1, source_target_pairs={{0,11},{1,0},{2,1},{3,2},{4,3},{5,4},{6,5},{7,6},{8,7},{9,8},{10,9... | collective-permute-start | bytes 393224 | tf_op jit(solution)/shard_map/ppermute | solution.py:25
  73.6 0.0 collective-permute-done.2
  73.6 1.9 %fusion.19 = bf16[256,256]{0,1:T(8,128)(2,1)S(1)} fusion(bf16[2432,256]{1,0:T(8,128)(2,1)} %collective-permute-done.2, bf16[32,8,2432]{2,1,0:T(8,128)(2,1)S(1)} %all-to-all-done), kind=kOutput, calls=%fused_computation.18 | convolution fusion | flops 318832640 | bytes 2621440 | tf_op jit(solution)/shard_map/dot_general | solution.py:266
  75.6 2.6 %collective-permute-start.3 = (bf16[256,256]{0,1:T(8,128)(2,1)S(1)}, bf16[256,256]{0,1:T(8,128)(2,1)S(1)}, u32[]{:S(2)}, u32[]{:S(2)}) collective-permute-start(bf16[256,256]{0,1:T(8,128)(2,1)S(1)} %fusion.19), channel_id=1, source_target_pairs={{0,1},{1,2},{2,3},{3,4},{4,5},{5,6},{6,7},{7,8},{8,9},{9,10},{10,1... | collective-permute-start | bytes 393224 | tf_op jit(solution)/shard_map/ppermute | solution.py:25
  78.1 0.0 copy-done
  78.2 0.6 fusion.14
  78.8 0.0 copy-start.1
  78.8 0.0 collective-permute-done.1
  78.8 4.8 %collective-permute-done.3 = bf16[256,256]{0,1:T(8,128)(2,1)S(1)} collective-permute-done((bf16[256,256]{0,1:T(8,128)(2,1)S(1)}, bf16[256,256]{0,1:T(8,128)(2,1)S(1)}, u32[]{:S(2)}, u32[]{:S(2)}) %collective-permute-start.3) | collective-permute-done | bytes 131104 | tf_op jit(solution)/shard_map/ppermute | solution.py:25
  83.6 0.1 convert_add_fusion
  83.7 1.9 %collective-permute-start.4 = (bf16[256,128]{0,1:T(8,128)(2,1)S(1)}, bf16[256,128]{0,1:T(8,128)(2,1)S(1)}, u32[]{:S(2)}, u32[]{:S(2)}) collective-permute-start(bf16[256,128]{0,1:T(8,128)(2,1)S(1)} %fusion.32), channel_id=1, source_target_pairs={{0,1},{1,2},{2,3},{3,4},{4,5},{5,6},{6,7},{7,8},{8,9},{9,10},{10,1... | collective-permute-start | bytes 196616 | tf_op jit(solution)/shard_map/ppermute | solution.py:25
  85.7 5.1 %collective-permute-start.5 = (bf16[256,128]{0,1:T(8,128)(2,1)S(1)}, bf16[256,128]{0,1:T(8,128)(2,1)S(1)}, u32[]{:S(2)}, u32[]{:S(2)}) collective-permute-start(bf16[256,128]{0,1:T(8,128)(2,1)S(1)} %fusion.32), channel_id=1, source_target_pairs={{0,11},{1,0},{2,1},{3,2},{4,3},{5,4},{6,5},{7,6},{8,7},{9,8},{10,9... | collective-permute-start | bytes 196616 | tf_op jit(solution)/shard_map/ppermute | solution.py:25
  90.8 2.4 %collective-permute-start.6 = (bf16[256,128]{0,1:T(8,128)(2,1)S(1)}, bf16[256,128]{0,1:T(8,128)(2,1)S(1)}, u32[]{:S(2)}, u32[]{:S(2)}) collective-permute-start(bf16[256,128]{0,1:T(8,128)(2,1)S(1)} %fusion.32), channel_id=1, source_target_pairs={{0,10},{1,3},{2,0},{3,5},{4,2},{5,7},{6,4},{7,9},{8,6},{9,11},{10,... | collective-permute-start | bytes 196616 | tf_op jit(solution)/shard_map/ppermute | solution.py:38
  93.3 0.0 collective-permute-done.10
  93.3 0.1 broadcast_select_fusion.1
  93.3 0.0 collective-permute-done.8
  93.3 0.0 collective-permute-done.4
  93.4 0.0 collective-permute-done.5
  93.4 4.5 %collective-permute-done.6 = bf16[256,128]{0,1:T(8,128)(2,1)S(1)} collective-permute-done((bf16[256,128]{0,1:T(8,128)(2,1)S(1)}, bf16[256,128]{0,1:T(8,128)(2,1)S(1)}, u32[]{:S(2)}, u32[]{:S(2)}) %collective-permute-start.6) | collective-permute-done | bytes 65568 | tf_op jit(solution)/shard_map/ppermute | solution.py:38
  97.9 0.0 copy-done.1
  97.9 2.6 %fusion = bf16[32,8,1792]{2,1,0:T(8,128)(2,1)} fusion(bf16[128,896]{1,0:T(8,128)(2,1)S(1)} %get-tuple-element.18, bf16[128,896]{1,0:T(8,128)(2,1)S(1)} %get-tuple-element.17, bf16[128,1792]{1,0:T(8,128)(2,1)} %collective-permute-done.8, bf16[128,1792]{1,0:T(8,128)(2,1)S(1)} %copy-done.1, bf16[128,1792]{1,0:T(8,128)(2,1)S(1)} %collective-permute-done.7, ...), kind=kOutput, calls=%fused_computation.1 | convolution fusion | flops 480444416 | bytes 3014656 | tf_op jit(solution)/shard_map/dot_general | solution.py:276
  100.5 9.8 %all-to-all-start.1 = ((bf16[32,8,1792]{2,1,0:T(8,128)(2,1)}), bf16[32,8,1792]{2,1,0:T(8,128)(2,1)S(1)}, u32[]{:S(2)}, u32[]{:S(2)}) async-start(bf16[32,8,1792]{2,1,0:T(8,128)(2,1)} %fusion), calls=%async_computation.1 | async-start | bytes 1835008 | tf_op jit(solution)/shard_map/all_to_all | solution.py:33
  110.3 1.6 %weigh.1 = bf16[2,256,24]{2,1,0:T(8,128)(2,1)} custom-call(s32[8,24]{1,0:T(8,128)} %bitcast.41, f32[8,24]{1,0:T(8,128)} %bitcast.42), custom_call_target="tpu_custom_call" | custom-call | flops 67108864 | bytes 32768 | tf_op jit(solution)/shard_map/weigh/pallas_call | solution.py:217
  111.9 19.2 %all-to-all-done.1 = bf16[32,8,1792]{2,1,0:T(8,128)(2,1)S(1)} async-done(((bf16[32,8,1792]{2,1,0:T(8,128)(2,1)}), bf16[32,8,1792]{2,1,0:T(8,128)(2,1)S(1)}, u32[]{:S(2)}, u32[]{:S(2)}) %all-to-all-start.1) | async-done | bytes 917536 | tf_op jit(solution)/shard_map/all_to_all | solution.py:33
  131.1 1.2 fusion.22
  132.3 17.6 %all_to_all.15 = bf16[12,2,1792]{2,1,0:T(2,128)(2,1)S(1)} all-to-all(bf16[12,2,1792]{2,1,0:T(2,128)(2,1)S(1)} %convert_element_type.42), channel_id=1, replica_groups=mesh['ep'=32,'dp'=2,'tp'=12] {'tp'}, dimensions={0} | all-to-all | bytes 172032 | tf_op jit(solution)/shard_map/all_to_all | solution.py:33
  150.1 0.6 pad_maximum_fusion
  (5 shorter events, 0.2 us)
Async XLA Ops:
  3.2 64.9 %all-to-all-start = ((bf16[32,8,2432]{2,1,0:T(8,128)(2,1)}), bf16[32,8,2432]{2,1,0:T(8,128)(2,1)S(1)}, u32[]{:S(2)}, u32[]{:S(2)}) async-start(bf16[32,8,2432]{2,1,0:T(8,128)(2,1)} %bitcast.39), calls=%async_computation | async-start | bytes 2490368 | tf_op jit(solution)/shard_map/all_to_all | solution.py:33
  18.5 26.8 %collective-permute-start = (bf16[2432,256]{1,0:T(8,128)(2,1)}, bf16[2432,256]{1,0:T(8,128)(2,1)S(1)}, u32[]{:S(2)}, u32[]{:S(2)}) collective-permute-start(bf16[2432,256]{1,0:T(8,128)(2,1)} %shard_map.65), channel_id=1, source_target_pairs={{0,1},{1,2},{2,3},{3,4},{4,5},{5,6},{6,7},{7,8},{8,9},{9,10},{10,1... | collective-permute-start | bytes 3735560 | tf_op jit(solution)/shard_map/ppermute | solution.py:25
  45.3 28.3 %collective-permute-start.2 = (bf16[2432,256]{1,0:T(8,128)(2,1)S(1)}, bf16[2432,256]{1,0:T(8,128)(2,1)}, u32[]{:S(2)}, u32[]{:S(2)}) collective-permute-start(bf16[2432,256]{1,0:T(8,128)(2,1)S(1)} %collective-permute-done), channel_id=1, source_target_pairs={{0,12},{12,0},{1,13},{13,1},{2,14},{14,2},{3,15},{15,3},{4,16},{16... | collective-permute-start | bytes 3735560 | tf_op jit(solution)/shard_map/ppermute | solution.py:29
  49.1 16.8 %collective-permute-start.7 = (bf16[128,1792]{1,0:T(8,128)(2,1)}, bf16[128,1792]{1,0:T(8,128)(2,1)S(1)}, u32[]{:S(2)}, u32[]{:S(2)}) collective-permute-start(bf16[128,1792]{1,0:T(8,128)(2,1)} %shard_map.66), channel_id=1, source_target_pairs={{0,1},{1,2},{2,3},{3,4},{4,5},{5,6},{6,7},{7,8},{8,9},{9,10},{10,1... | collective-permute-start | bytes 1376264 | tf_op jit(solution)/shard_map/ppermute | solution.py:25
  52.7 11.0 %collective-permute-start.9 = (bf16[128,896]{1,0:T(8,128)(2,1)}, bf16[128,896]{1,0:T(8,128)(2,1)S(1)}, u32[]{:S(2)}, u32[]{:S(2)}) collective-permute-start(bf16[128,896]{1,0:T(8,128)(2,1)} %shard_map.68), channel_id=1, source_target_pairs={{0,10},{1,3},{2,0},{3,5},{4,2},{5,7},{6,4},{7,9},{8,6},{9,11},{10,... | collective-permute-start | bytes 688136 | tf_op jit(solution)/shard_map/ppermute | solution.py:38
  63.7 29.5 %collective-permute-start.10 = (bf16[128,896]{1,0:T(8,128)(2,1)S(1)}, bf16[128,896]{1,0:T(8,128)(2,1)S(1)}, u32[]{:S(2)}, u32[]{:S(2)}) collective-permute-start(bf16[128,896]{1,0:T(8,128)(2,1)S(1)} %collective-permute-done.9), channel_id=1, source_target_pairs={{0,12},{12,0},{1,13},{13,1},{2,14},{14,2},{3,15},{15,3},{4,16},{16... | collective-permute-start | bytes 688136 | tf_op jit(solution)/shard_map/ppermute | solution.py:29
  65.9 27.4 %collective-permute-start.8 = (bf16[128,1792]{1,0:T(8,128)(2,1)S(1)}, bf16[128,1792]{1,0:T(8,128)(2,1)}, u32[]{:S(2)}, u32[]{:S(2)}) collective-permute-start(bf16[128,1792]{1,0:T(8,128)(2,1)S(1)} %collective-permute-done.7), channel_id=1, source_target_pairs={{0,12},{12,0},{1,13},{13,1},{2,14},{14,2},{3,15},{15,3},{4,16},{16... | collective-permute-start | bytes 1376264 | tf_op jit(solution)/shard_map/ppermute | solution.py:29
  68.7 9.4 %copy-start = (bf16[2432,256]{1,0:T(8,128)(2,1)S(1)}, bf16[2432,256]{1,0:T(8,128)(2,1)}, u32[]{:S(2)}) copy-start(bf16[2432,256]{1,0:T(8,128)(2,1)} %shard_map.64) | copy-start | bytes 3735556
  68.7 10.1 %collective-permute-start.1 = (bf16[256,256]{0,1:T(8,128)(2,1)S(1)}, bf16[256,256]{0,1:T(8,128)(2,1)S(1)}, u32[]{:S(2)}, u32[]{:S(2)}) collective-permute-start(bf16[256,256]{0,1:T(8,128)(2,1)S(1)} %fusion.16), channel_id=1, source_target_pairs={{0,11},{1,0},{2,1},{3,2},{4,3},{5,4},{6,5},{7,6},{8,7},{9,8},{10,9... | collective-permute-start | bytes 393224 | tf_op jit(solution)/shard_map/ppermute | solution.py:25
  75.6 8.1 %collective-permute-start.3 = (bf16[256,256]{0,1:T(8,128)(2,1)S(1)}, bf16[256,256]{0,1:T(8,128)(2,1)S(1)}, u32[]{:S(2)}, u32[]{:S(2)}) collective-permute-start(bf16[256,256]{0,1:T(8,128)(2,1)S(1)} %fusion.19), channel_id=1, source_target_pairs={{0,1},{1,2},{2,3},{3,4},{4,5},{5,6},{6,7},{7,8},{8,9},{9,10},{10,1... | collective-permute-start | bytes 393224 | tf_op jit(solution)/shard_map/ppermute | solution.py:25
  78.8 19.1 %copy-start.1 = (bf16[128,1792]{1,0:T(8,128)(2,1)S(1)}, bf16[128,1792]{1,0:T(8,128)(2,1)}, u32[]{:S(2)}) copy-start(bf16[128,1792]{1,0:T(8,128)(2,1)} %shard_map.67) | copy-start | bytes 1376260
  83.7 9.6 %collective-permute-start.4 = (bf16[256,128]{0,1:T(8,128)(2,1)S(1)}, bf16[256,128]{0,1:T(8,128)(2,1)S(1)}, u32[]{:S(2)}, u32[]{:S(2)}) collective-permute-start(bf16[256,128]{0,1:T(8,128)(2,1)S(1)} %fusion.32), channel_id=1, source_target_pairs={{0,1},{1,2},{2,3},{3,4},{4,5},{5,6},{6,7},{7,8},{8,9},{9,10},{10,1... | collective-permute-start | bytes 196616 | tf_op jit(solution)/shard_map/ppermute | solution.py:25
  85.7 7.7 %collective-permute-start.5 = (bf16[256,128]{0,1:T(8,128)(2,1)S(1)}, bf16[256,128]{0,1:T(8,128)(2,1)S(1)}, u32[]{:S(2)}, u32[]{:S(2)}) collective-permute-start(bf16[256,128]{0,1:T(8,128)(2,1)S(1)} %fusion.32), channel_id=1, source_target_pairs={{0,11},{1,0},{2,1},{3,2},{4,3},{5,4},{6,5},{7,6},{8,7},{9,8},{10,9... | collective-permute-start | bytes 196616 | tf_op jit(solution)/shard_map/ppermute | solution.py:25
  90.8 7.1 %collective-permute-start.6 = (bf16[256,128]{0,1:T(8,128)(2,1)S(1)}, bf16[256,128]{0,1:T(8,128)(2,1)S(1)}, u32[]{:S(2)}, u32[]{:S(2)}) collective-permute-start(bf16[256,128]{0,1:T(8,128)(2,1)S(1)} %fusion.32), channel_id=1, source_target_pairs={{0,10},{1,3},{2,0},{3,5},{4,2},{5,7},{6,4},{7,9},{8,6},{9,11},{10,... | collective-permute-start | bytes 196616 | tf_op jit(solution)/shard_map/ppermute | solution.py:38
  100.5 30.6 %all-to-all-start.1 = ((bf16[32,8,1792]{2,1,0:T(8,128)(2,1)}), bf16[32,8,1792]{2,1,0:T(8,128)(2,1)S(1)}, u32[]{:S(2)}, u32[]{:S(2)}) async-start(bf16[32,8,1792]{2,1,0:T(8,128)(2,1)} %fusion), calls=%async_computation.1 | async-start | bytes 1835008 | tf_op jit(solution)/shard_map/all_to_all | solution.py:33
